TPU v7x, 128 devices: a whole 4x4x4 slice. The times are simulated.
128 devices in a mesh: patch: 32 (over x, z, core), grp: 4 (over y).
Axes of the slice: x: 4, y: 4, z: 4, core: 2. Of those that a mesh axis runs over, the one named last changes fastest.
Arguments:
- previous: float32 [4, 32, 12, 21, 256], P('grp', 'patch'), may hold values from -4 to 4
- predicted: float32 [4, 32, 12, 21, 256], P('grp', 'patch'), may hold values from -4 to 4
- new_owner: int32 [4, 32, 12], replicated, may hold values from 0 to 31, as said below
- levels: int32 [4, 32, 12], replicated, may hold values from 0 to 2
- diffusion: float32 [21], replicated, may hold values from 0.05 to 0.5
- decay: float32 [21], replicated, may hold values from 0.1 to 1
- reaction: float32 [21, 21], replicated, may hold values from -1.25 to 1.25
Outputs:
- solution: float32 [4, 32, 16, 21, 256], P('grp', 'patch')
Inputs may be any that keep to these rules, and one draw needn't show every extreme that they name: new_owner[b, o, s] is o, except that a patch of the last column of an owner o < 31 may get o + 1 and a patch of the first column of an owner o > 0 may get o - 1; at most 2 patches of one owner get o + 1 and at most 2 get o - 1; owner (0, 0) hands exactly 2 to o + 1 and owner (0, 31) exactly 2 to o - 1.
All inputs are finite; a program needn't handle non-finite values.
Results may differ from a plain program's by a relative error of at most 0.0003.
Values sent between devices are 32-bit elements; how exact they have to be, the bound alone decides.
No kernel may reach another device: no remote copies, remote signals or barrier semaphores. Data moves between devices by JAX's collectives and lax.ppermute only.
A program may use at most 128 MiB of HBM per device.

v0:
```python
import jax
import jax.numpy as jnp
from jax import lax
from jax.sharding import Mesh
from jax.sharding import PartitionSpec as P

SPECIES = 21
CELLS = 16
ROWS_DEV = 4
COLS_DEV = 3
MOVE_CAP = 2
KRYLOV = 3
NEWTON = 2
PATCH_DEV = 12
PATCH = ("patch_0", "patch_1", "patch_2")
PATCH_GRP = ("patch_0", "patch_1", "patch_2", "grp")


step_rate = 4.0
epsilon = 1e-12
highest = lax.Precision.HIGHEST
opposite = (1, 0, 3, 2)


def extended(x, sides, width):
    for axis, dim in sides:
        devices, length = (lax.axis_size(axis), x.shape[dim])
        up = [(i, (i + 1) % devices) for i in range(devices - 1)]
        down = [(j, i) for i, j in up]
        last = lax.slice_in_dim(x, length - width, length, axis=dim)
        initial = lax.slice_in_dim(x, 0, width, axis=dim)
        before = lax.ppermute(last, axis, up)
        after = lax.ppermute(initial, axis, down)
        x = jnp.concatenate([before, x, after], axis=dim)
    return x


def over_axes(x, axes):
    for axis in axes:
        x = lax.psum(x, axis)
    return x


def passed_along(block, axis, distance):
    devices = range(lax.axis_size(axis))
    route = [(i - distance, i) for i in devices if i - distance in devices]
    return lax.ppermute(block, axis, route)


def neighbor_ids(patch_ids, band_total, owner_total):
    valid = patch_ids >= 0
    safe = jnp.maximum(patch_ids, 0)
    per_owner = ROWS_DEV * COLS_DEV
    column_of = safe % COLS_DEV
    row_of = safe // COLS_DEV % ROWS_DEV
    owner_of = safe // per_owner % owner_total
    band_of = safe // (per_owner * owner_total)

    def compose(band_val, owner_val, row_val, column_val, inside):
        ident = ((band_val * owner_total + owner_val) * ROWS_DEV + row_val) * COLS_DEV + column_val
        return jnp.where(inside & valid, ident, -1)

    west = compose(
        band_of,
        jnp.where(column_of > 0, owner_of, owner_of - 1),
        row_of,
        jnp.where(column_of > 0, column_of - 1, COLS_DEV - 1),
        (column_of > 0) | (owner_of > 0),
    )
    east = compose(
        band_of,
        jnp.where(column_of < COLS_DEV - 1, owner_of, owner_of + 1),
        row_of,
        jnp.where(column_of < COLS_DEV - 1, column_of + 1, 0),
        (column_of < COLS_DEV - 1) | (owner_of < owner_total - 1),
    )
    south = compose(
        jnp.where(row_of > 0, band_of, band_of - 1),
        owner_of,
        jnp.where(row_of > 0, row_of - 1, ROWS_DEV - 1),
        column_of,
        (row_of > 0) | (band_of > 0),
    )
    north = compose(
        jnp.where(row_of < ROWS_DEV - 1, band_of, band_of + 1),
        owner_of,
        jnp.where(row_of < ROWS_DEV - 1, row_of + 1, 0),
        column_of,
        (row_of < ROWS_DEV - 1) | (band_of < band_total - 1),
    )
    return jnp.stack([west, east, south, north], axis=-1)


def conductance(level_vals):
    return jnp.where(level_vals == 0, 1.0, jnp.where(level_vals == 1, 4.0, 16.0)).astype(
        jnp.float32
    )


def small_solve(gram, rhs):
    dimension = gram.shape[0]
    matrix = gram
    vector = rhs
    for column_at in range(dimension):
        for target in range(column_at + 1, dimension):
            factor = matrix[target, column_at] / matrix[column_at, column_at]
            matrix = matrix.at[target].add(-factor * matrix[column_at])
            vector = vector.at[target].add(-factor * vector[column_at])
    answer = [None] * dimension
    for column_at in reversed(range(dimension)):
        running = vector[column_at]
        for later in range(column_at + 1, dimension):
            running = running - matrix[column_at, later] * answer[later]
        answer[column_at] = running / matrix[column_at, column_at]
    return jnp.stack(answer)


def pack_movers(offset, data):
    grid_off = offset.reshape(ROWS_DEV, COLS_DEV)
    row_slots = jnp.arange(ROWS_DEV, dtype=jnp.int32) * COLS_DEV
    packs = []
    for column_at, sign in ((COLS_DEV - 1, 1), (0, -1)):
        moving = (grid_off[:, column_at] == sign).astype(jnp.int32)
        ranks = jnp.cumsum(moving) - 1
        choose = (moving[:, None] == 1) & (
            ranks[:, None] == jnp.arange(MOVE_CAP, dtype=jnp.int32)[None, :]
        )
        present = jnp.any(choose, axis=0)
        source = jnp.sum(jnp.where(choose, (row_slots + column_at)[:, None], 0), axis=0)
        picked = jnp.take(data, source, axis=0)
        packs.append(jnp.where(present.reshape((MOVE_CAP,) + (1,) * (data.ndim - 1)), picked, 0.0))
    return packs


def neighbor_strips(values, window_tags, near_ids):
    slot_count = values.shape[0]
    squared = values.reshape(slot_count, SPECIES, CELLS, CELLS)
    bank = jnp.stack(
        [squared[:, :, :, 0], squared[:, :, :, -1], squared[:, :, 0, :], squared[:, :, -1, :]],
        axis=0,
    )
    flat = bank.reshape(1, 1, -1)
    half_len = flat.shape[2] // 2
    beside = extended(flat, ((PATCH, 1),), 1)
    across = extended(beside[:, :, half_len:], (("grp", 0),), 1)
    blank = jnp.zeros((1, 3, half_len), jnp.float32)
    sides = jnp.concatenate([blank, beside[:, :, :half_len], blank], axis=0)
    received = jnp.concatenate([sides, across], axis=2)
    pieces = received.reshape(9, 4, slot_count, SPECIES * CELLS)
    tags = window_tags.reshape(9 * slot_count)
    ghosts = []
    for direction in range(4):
        wanted = near_ids[:, direction]
        selector = ((wanted[:, None] == tags[None, :]) & (wanted[:, None] >= 0)).astype(jnp.float32)
        candidates = pieces[:, opposite[direction]].reshape(9 * slot_count, SPECIES * CELLS)
        picked = jnp.dot(
            selector, candidates, precision=highest, preferred_element_type=jnp.float32
        )
        ghosts.append(picked.reshape(slot_count, SPECIES, CELLS))
    return ghosts


def laplace_slots(values, ghosts, face_self, face_near):
    slot_count = values.shape[0]
    flat_pos = jnp.arange(CELLS * CELLS, dtype=jnp.int32)
    column_of = flat_pos % CELLS
    row_of = flat_pos // CELLS
    zero_one = jnp.zeros((slot_count, SPECIES, 1), jnp.float32)
    zero_row = jnp.zeros((slot_count, SPECIES, CELLS), jnp.float32)
    west_vals = jnp.where(
        column_of == 0,
        jnp.repeat(ghosts[0], CELLS, axis=-1),
        jnp.concatenate([zero_one, values[:, :, :-1]], axis=2),
    )
    east_vals = jnp.where(
        column_of == CELLS - 1,
        jnp.repeat(ghosts[1], CELLS, axis=-1),
        jnp.concatenate([values[:, :, 1:], zero_one], axis=2),
    )
    south_vals = jnp.where(
        row_of == 0,
        jnp.tile(ghosts[2], (1, 1, CELLS)),
        jnp.concatenate([zero_row, values[:, :, :-CELLS]], axis=2),
    )
    north_vals = jnp.where(
        row_of == CELLS - 1,
        jnp.tile(ghosts[3], (1, 1, CELLS)),
        jnp.concatenate([values[:, :, CELLS:], zero_row], axis=2),
    )
    own_face = face_self[:, None, None]

    def face(edge_mask, direction):
        return jnp.where(
            edge_mask,
            0.5 * (own_face + face_near[:, direction][:, None, None]),
            0.5 * (own_face + own_face),
        )

    return (
        face(column_of == 0, 0) * (west_vals - values)
        + face(column_of == CELLS - 1, 1) * (east_vals - values)
        + face(row_of == 0, 2) * (south_vals - values)
        + face(row_of == CELLS - 1, 3) * (north_vals - values)
    )


def newton_solve(
    prev_slots, pred_slots, layout_ids, band_pos, owner_pos, levels, diffusion, decay, reaction
):
    band_total, owner_total, slot_count = layout_ids.shape
    slot_ids = lax.dynamic_slice(layout_ids, (band_pos, owner_pos, 0), (1, 1, slot_count))[0, 0]
    padded_ids = jnp.pad(layout_ids, ((1, 1), (1, 1), (0, 0)), constant_values=-1)
    window_tags = lax.dynamic_slice(padded_ids, (band_pos, owner_pos, 0), (3, 3, slot_count))
    near_ids = neighbor_ids(slot_ids, band_total, owner_total)
    level_flat = levels.reshape(-1)

    def kappa_of(ident):
        return jnp.where(ident >= 0, conductance(jnp.take(level_flat, jnp.maximum(ident, 0))), 0.0)

    face_self = kappa_of(slot_ids)
    face_near = jnp.where(near_ids >= 0, kappa_of(near_ids), face_self[:, None])
    differential = (jnp.arange(SPECIES) < SPECIES - 1).astype(jnp.float32)[None, :, None]
    diff_col = diffusion[None, :, None]
    decay_col = decay[None, :, None]

    def laplace_of(values):
        return laplace_slots(
            values, neighbor_strips(values, window_tags, near_ids), face_self, face_near
        )

    def mixing(values):
        return jnp.einsum("st,kta->ksa", reaction, values, precision=highest)

    state = pred_slots
    for newton_step in range(NEWTON):
        resid = (
            differential * step_rate * (state - prev_slots)
            - diff_col * laplace_of(state)
            - mixing(state)
            + decay_col * (state * state * state)
        )
        squares = over_axes(jnp.sum(resid * resid), PATCH_GRP)
        scale = jnp.sqrt(squares + epsilon)
        basis = [-resid / scale]
        curvature = 3.0 * decay_col * (state * state)
        hess = jnp.zeros((KRYLOV + 1, KRYLOV), jnp.float32)
        for column_at in range(KRYLOV):
            current = basis[column_at]
            image = (
                differential * step_rate * current
                - diff_col * laplace_of(current)
                - mixing(current)
                + curvature * current
            )
            stacked = jnp.stack(basis)
            local_products = jnp.einsum("mksa,ksa->m", stacked, image, precision=highest)
            coeffs, length_sq = (
                over_axes(local_products, PATCH_GRP),
                over_axes(jnp.sum(image * image), PATCH_GRP),
            )
            image = image - jnp.einsum("m,mksa->ksa", coeffs, stacked, precision=highest)
            height = jnp.sqrt(length_sq - jnp.sum(coeffs * coeffs) + epsilon)
            hess = hess.at[: column_at + 1, column_at].set(coeffs)
            hess = hess.at[column_at + 1, column_at].set(height)
            basis.append(image / height)
        gram = jnp.dot(hess.T, hess, precision=highest)
        weights = small_solve(gram, scale * hess[0])
        state = state + jnp.einsum(
            "m,mksa->ksa", weights, jnp.stack(basis[:KRYLOV]), precision=highest
        )
    return state


def per_device(previous, predicted, new_owner, levels, diffusion, decay, reaction):
    band_pos = lax.axis_index("grp")
    owner_pos = lax.axis_index(PATCH)
    previous = previous[0, 0]
    predicted = predicted[0, 0]
    own_offset = (
        lax.dynamic_slice(new_owner, (band_pos, owner_pos, 0), (1, 1, PATCH_DEV))[0, 0] - owner_pos
    )
    stays = own_offset == 0
    layout_ids = jnp.arange(new_owner.size, dtype=jnp.int32).reshape(new_owner.shape)
    solved = newton_solve(
        previous, predicted, layout_ids, band_pos, owner_pos, levels, diffusion, decay, reaction
    )
    to_right, to_left = pack_movers(own_offset, solved)
    arrived = []
    for shift_by, payload in ((1, to_right), (-1, to_left)):
        arrived.append(passed_along(payload, PATCH, shift_by))
    kept = jnp.where(stays[:, None, None], solved, 0.0)
    result = jnp.concatenate([kept, arrived[0], arrived[1]], axis=0)
    return result[None, None]


def solution(mesh):
    torus = Mesh(
        mesh.devices.reshape(4, 4, 2, mesh.shape["grp"]), ("patch_0", "patch_1", "patch_2", "grp")
    )
    in_specs = (
        P("grp", PATCH, None, None, None),
        P("grp", PATCH, None, None, None),
        P(),
        P(),
        P(),
        P(),
        P(),
    )
    out_specs = P("grp", PATCH, None, None, None)
    return jax.shard_map(
        per_device, mesh=torus, in_specs=in_specs, out_specs=out_specs, check_vma=False
    )
```

profile of v0, /device:TPU:1, one launch (start us, length us, event | category | flops | bytes accessed | tf_op | source)
XLA Modules:
  0.0 771.5 jit_solution(6101554286599429304)
XLA Ops:
  57.9 9.1 %psum.392 = f32[]{:T(128)} all-reduce(f32[]{:T(128)} %get-tuple-element.531), channel_id=1, replica_groups=mesh['patch_0'=4,'patch_1'=4,'patch_2'=2,'grp'=4] {'patch_0'}, use_global_device_ids=true, to_apply=%region_1.2 | all-reduce | flops 1 | bytes 8 | tf_op jit(solution)/shard_map/psum | solution.py:40
  66.9 9.0 %psum.393 = f32[]{:T(128)} all-reduce(f32[]{:T(128)} %psum.392), channel_id=1, replica_groups=mesh['patch_0'=4,'patch_1'=4,'patch_2'=2,'grp'=4] {'patch_1'}, use_global_device_ids=true, to_apply=%region_2.3 | all-reduce | flops 1 | bytes 8 | tf_op jit(solution)/shard_map/psum | solution.py:40
  76.5 9.8 %psum.394 = f32[]{:T(128)} all-reduce(f32[]{:T(128)} %psum.393), channel_id=1, replica_groups=mesh['patch_0'=4,'patch_1'=4,'patch_2'=2,'grp'=4] {'patch_2'}, use_global_device_ids=true, to_apply=%region_3.4 | all-reduce | flops 1 | bytes 8 | tf_op jit(solution)/shard_map/psum | solution.py:40
  87.0 7.9 %psum.395 = f32[]{:T(128)} all-reduce(f32[]{:T(128)} %psum.394), channel_id=1, replica_groups=mesh['patch_0'=4,'patch_1'=4,'patch_2'=2,'grp'=4] {'grp'}, use_global_device_ids=true, to_apply=%region_4.5 | all-reduce | flops 1 | bytes 8 | tf_op jit(solution)/shard_map/psum | solution.py:40
  150.6 6.7 all-reduce.52
  157.2 11.7 %all-reduce.46 = (f32[]{:T(128)}, f32[1]{0:T(128)}) all-reduce(f32[]{:T(128)} %get-tuple-element.339, f32[1]{0:T(128)} %get-tuple-element.340), channel_id=1, replica_groups=mesh['patch_0'=4,'patch_1'=4,'patch_2'=2,'grp'=4] {'patch_1'}, use_global_device_ids=true, to_apply=%region_11.12 | all-reduce | flops 2 | bytes 16 | tf_op jit(solution)/shard_map/psum | solution.py:40
  173.7 6.9 all-reduce.40
  194.1 5.6 collective-permute-start.8
  242.8 6.8 all-reduce.51
  249.6 10.2 %all-reduce.45 = (f32[2]{0:T(128)S(1)}, f32[]{:T(128)}) all-reduce(f32[2]{0:T(128)S(1)} %get-tuple-element.337, f32[]{:T(128)} %get-tuple-element.338), channel_id=1, replica_groups=mesh['patch_0'=4,'patch_1'=4,'patch_2'=2,'grp'=4] {'patch_1'}, use_global_device_ids=true, to_apply=%region_16.17 | all-reduce | flops 3 | bytes 24 | tf_op jit(solution)/shard_map/psum | solution.py:40
  259.8 6.6 all-reduce.57
  266.4 6.7 all-reduce.39
  335.9 6.6 all-reduce.50
  342.5 9.4 %all-reduce.44 = (f32[3]{0:T(128)S(1)}, f32[]{:T(128)}) all-reduce(f32[3]{0:T(128)S(1)} %get-tuple-element.335, f32[]{:T(128)} %get-tuple-element.336), channel_id=1, replica_groups=mesh['patch_0'=4,'patch_1'=4,'patch_2'=2,'grp'=4] {'patch_1'}, use_global_device_ids=true, to_apply=%region_27.28 | all-reduce | flops 4 | bytes 32 | tf_op jit(solution)/shard_map/psum | solution.py:40
  352.0 7.7 all-reduce.56
  359.6 6.9 all-reduce.38
  436.7 6.6 psum.420
  443.9 10.6 %psum.421 = f32[]{:T(128)} all-reduce(f32[]{:T(128)} %psum.420), channel_id=1, replica_groups=mesh['patch_0'=4,'patch_1'=4,'patch_2'=2,'grp'=4] {'patch_1'}, use_global_device_ids=true, to_apply=%region_38.39 | all-reduce | flops 1 | bytes 8 | tf_op jit(solution)/shard_map/psum | solution.py:40
  455.1 5.6 psum.422
  462.3 7.2 psum.423
  525.6 6.7 all-reduce.49
  532.3 9.7 %all-reduce.43 = (f32[]{:T(128)}, f32[1]{0:T(128)}) all-reduce(f32[]{:T(128)} %get-tuple-element.333, f32[1]{0:T(128)} %get-tuple-element.334), channel_id=1, replica_groups=mesh['patch_0'=4,'patch_1'=4,'patch_2'=2,'grp'=4] {'patch_1'}, use_global_device_ids=true, to_apply=%region_47.48 | all-reduce | flops 2 | bytes 16 | tf_op jit(solution)/shard_map/psum | solution.py:40
  542.0 5.6 all-reduce.55
  547.6 6.9 all-reduce.37
  612.7 6.6 all-reduce.48
  619.3 10.6 %all-reduce.42 = (f32[2]{0:T(128)S(1)}, f32[]{:T(128)}) all-reduce(f32[2]{0:T(128)S(1)} %get-tuple-element.331, f32[]{:T(128)} %get-tuple-element.332), channel_id=1, replica_groups=mesh['patch_0'=4,'patch_1'=4,'patch_2'=2,'grp'=4] {'patch_1'}, use_global_device_ids=true, to_apply=%region_51.52 | all-reduce | flops 3 | bytes 24 | tf_op jit(solution)/shard_map/psum | solution.py:40
  629.9 6.6 all-reduce.54
  636.5 6.7 all-reduce.36
  705.3 6.6 all-reduce.47
  711.9 9.2 %all-reduce.41 = (f32[3]{0:T(128)S(1)}, f32[]{:T(128)}) all-reduce(f32[3]{0:T(128)S(1)} %get-tuple-element.329, f32[]{:T(128)} %get-tuple-element.330), channel_id=1, replica_groups=mesh['patch_0'=4,'patch_1'=4,'patch_2'=2,'grp'=4] {'patch_1'}, use_global_device_ids=true, to_apply=%region_61.62 | all-reduce | flops 4 | bytes 32 | tf_op jit(solution)/shard_map/psum | solution.py:40
  721.1 7.8 %all-reduce.53 = (f32[3]{0:T(128)S(1)}, f32[]{:T(128)}) all-reduce(f32[3]{0:T(128)S(1)} %get-tuple-element.317, f32[]{:T(128)} %get-tuple-element.318), channel_id=1, replica_groups=mesh['patch_0'=4,'patch_1'=4,'patch_2'=2,'grp'=4] {'patch_2'}, use_global_device_ids=true, to_apply=%region_62.63 | all-reduce | flops 4 | bytes 32 | tf_op jit(solution)/shard_map/psum | solution.py:40
  728.9 6.9 all-reduce.35
  (781 shorter events, 488.2 us)
Async XLA Ops:
  10.9 21.2 %collective-permute-start = (f32[1,1,16128]{2,1,0:T(1,128)S(1)}, f32[1,1,16128]{2,1,0:T(1,128)S(1)}, u32[]{:S(2)}, u32[]{:S(2)}) collective-permute-start(f32[1,1,16128]{2,1,0:T(1,128)S(1)} %reshape.2537), channel_id=1, source_target_pairs={{0,4},{4,8},{8,12},{12,16},{16,20},{20,24},{24,28},{28,32},{32,36}... | collective-permute-start | bytes 193544 | tf_op jit(solution)/shard_map/ppermute | solution.py:32
  15.8 16.3 %collective-permute-start.1 = (f32[1,1,16128]{2,1,0:T(1,128)S(1)}, f32[1,1,16128]{2,1,0:T(1,128)S(1)}, u32[]{:S(2)}, u32[]{:S(2)}) collective-permute-start(f32[1,1,16128]{2,1,0:T(1,128)S(1)} %reshape.2537), channel_id=1, source_target_pairs={{4,0},{8,4},{12,8},{16,12},{20,16},{24,20},{28,24},{32,28},{36,32}... | collective-permute-start | bytes 193544 | tf_op jit(solution)/shard_map/ppermute | solution.py:33
  35.5 5.7 collective-permute-start.3
  106.4 7.7 %collective-permute-start.4 = (f32[1,1,16128]{2,1,0:T(1,128)S(1)}, f32[1,1,16128]{2,1,0:T(1,128)S(1)}, u32[]{:S(2)}, u32[]{:S(2)}) collective-permute-start(f32[1,1,16128]{2,1,0:T(1,128)S(1)} %reshape.2544), channel_id=1, source_target_pairs={{0,4},{4,8},{8,12},{12,16},{16,20},{20,24},{24,28},{28,32},{32,36}... | collective-permute-start | bytes 193544 | tf_op jit(solution)/shard_map/ppermute | solution.py:32
  110.4 5.6 collective-permute-start.5
  118.5 5.7 collective-permute-start.7
  194.1 10.2 %collective-permute-start.8 = (f32[1,1,16128]{2,1,0:T(1,128)S(1)}, f32[1,1,16128]{2,1,0:T(1,128)S(1)}, u32[]{:S(2)}, u32[]{:S(2)}) collective-permute-start(f32[1,1,16128]{2,1,0:T(1,128)S(1)} %reshape.2554), channel_id=1, source_target_pairs={{0,4},{4,8},{8,12},{12,16},{16,20},{20,24},{24,28},{28,32},{32,36}... | collective-permute-start | bytes 193544 | tf_op jit(solution)/shard_map/ppermute | solution.py:32
  199.7 5.6 collective-permute-start.9
  205.5 5.7 collective-permute-start.10
  209.1 5.7 collective-permute-start.11
  288.8 12.8 %collective-permute-start.12 = (f32[1,1,16128]{2,1,0:T(1,128)S(1)}, f32[1,1,16128]{2,1,0:T(1,128)S(1)}, u32[]{:S(2)}, u32[]{:S(2)}) collective-permute-start(f32[1,1,16128]{2,1,0:T(1,128)S(1)} %reshape.2565), channel_id=1, source_target_pairs={{0,4},{4,8},{8,12},{12,16},{16,20},{20,24},{24,28},{28,32},{32,36}... | collective-permute-start | bytes 193544 | tf_op jit(solution)/shard_map/ppermute | solution.py:32
  294.4 7.2 collective-permute-start.13
  301.8 6.4 collective-permute-start.14
  305.5 5.7 collective-permute-start.15
  397.9 8.4 %collective-permute-start.16 = (f32[1,1,16128]{2,1,0:T(1,128)S(1)}, f32[1,1,16128]{2,1,0:T(1,128)S(1)}, u32[]{:S(2)}, u32[]{:S(2)}) collective-permute-start(f32[1,1,16128]{2,1,0:T(1,128)S(1)} %reshape.2581), channel_id=1, source_target_pairs={{0,4},{4,8},{8,12},{12,16},{16,20},{20,24},{24,28},{28,32},{32,36}... | collective-permute-start | bytes 193544 | tf_op jit(solution)/shard_map/ppermute | solution.py:32
  403.5 5.6 collective-permute-start.17
  409.3 6.1 collective-permute-start.18
  412.9 5.7 collective-permute-start.19
  481.1 9.3 %collective-permute-start.20 = (f32[1,1,16128]{2,1,0:T(1,128)S(1)}, f32[1,1,16128]{2,1,0:T(1,128)S(1)}, u32[]{:S(2)}, u32[]{:S(2)}) collective-permute-start(f32[1,1,16128]{2,1,0:T(1,128)S(1)} %reshape.2588), channel_id=1, source_target_pairs={{0,4},{4,8},{8,12},{12,16},{16,20},{20,24},{24,28},{28,32},{32,36}... | collective-permute-start | bytes 193544 | tf_op jit(solution)/shard_map/ppermute | solution.py:32
  486.7 5.6 collective-permute-start.21
  492.5 5.7 collective-permute-start.22
  496.1 5.7 collective-permute-start.23
  566.5 10.1 %collective-permute-start.24 = (f32[1,1,16128]{2,1,0:T(1,128)S(1)}, f32[1,1,16128]{2,1,0:T(1,128)S(1)}, u32[]{:S(2)}, u32[]{:S(2)}) collective-permute-start(f32[1,1,16128]{2,1,0:T(1,128)S(1)} %reshape.2598), channel_id=1, source_target_pairs={{0,4},{4,8},{8,12},{12,16},{16,20},{20,24},{24,28},{28,32},{32,36}... | collective-permute-start | bytes 193544 | tf_op jit(solution)/shard_map/ppermute | solution.py:32
  572.0 5.6 collective-permute-start.25
  577.8 5.8 collective-permute-start.26
  581.4 5.7 collective-permute-start.27
  658.3 12.8 %collective-permute-start.28 = (f32[1,1,16128]{2,1,0:T(1,128)S(1)}, f32[1,1,16128]{2,1,0:T(1,128)S(1)}, u32[]{:S(2)}, u32[]{:S(2)}) collective-permute-start(f32[1,1,16128]{2,1,0:T(1,128)S(1)} %reshape.2607), channel_id=1, source_target_pairs={{0,4},{4,8},{8,12},{12,16},{16,20},{20,24},{24,28},{28,32},{32,36}... | collective-permute-start | bytes 193544 | tf_op jit(solution)/shard_map/ppermute | solution.py:32
  663.8 7.2 collective-permute-start.29
  671.3 6.4 collective-permute-start.30
  674.9 5.7 collective-permute-start.31
  758.7 8.2 %collective-permute-start.32 = (f32[2,21,256]{2,1,0:T(8,128)S(1)}, f32[2,21,256]{2,1,0:T(8,128)S(1)}, u32[]{:S(2)}, u32[]{:S(2)}) collective-permute-start(f32[2,21,256]{2,1,0:T(8,128)S(1)} %select_select_fusion.1), channel_id=1, source_target_pairs={{0,4},{4,8},{8,12},{12,16},{16,20},{20,24},{24,28},{28,32},{32,36}... | collective-permute-start | bytes 129032 | tf_op jit(solution)/shard_map/ppermute | solution.py:47
  765.0 5.4 collective-permute-start.33
  (136 other events, 1044.7 us)
where the time goes:
time: 781 us; the launch traced here: 771 us
  blocking collectives  246 us (31%)
  local copies, waits for them, and re-layouts  231 us (30%)
  starting transfers between devices  104 us (13%)
  matrix products  69.1 us (9%)
  other arithmetic  44.7 us (6%)
  waiting for transfers between devices  39.5 us (5%)
  between operations  36 us (5%)
    psum x32, blocking collectives, over_axes(): x = lax.psum(x, axis)  246 us
    ppermute x16, starting transfers between devices, extended(): before = lax.ppermute(last, axis, up)  69.3 us
    unnamed x286, local copies, waits for them, and re-layouts  39.7 us
    ppermute x16, waiting for transfers between devices, extended(): after = lax.ppermute(initial, axis, down)  35.7 us
    ppermute x16, starting transfers between devices, extended(): after = lax.ppermute(initial, axis, down)  27.6 us
    dot_general x8, matrix products, mixing(): return jnp.einsum('st,kta->ksa', reaction, values, precision=highest)  22.3 us
    slice x8, local copies, waits for them, and re-layouts, neighbor_strips(): squared[:, :, :, 0]  21.5 us
    dot_general x64, local copies, waits for them, and re-layouts, neighbor_strips(): jnp.dot(selector, candidates, precision=highest, preferred_element_type=j...  20.5 us
  transfers between devices with their start and end apart: 34, of which 15 were waited for; matrix products, arithmetic and copies ran while one was open for 5% of the time, Pallas kernels for 0%

commit v1 on v0

v1 whole, which is shorter than its diff:
```python
import jax
import jax.numpy as jnp
from jax import lax
from jax.experimental import pallas as pl
from jax.experimental.pallas import tpu as pltpu
from jax.sharding import Mesh
from jax.sharding import PartitionSpec as P

SPECIES = 21
COLS_DEV = 3
ROWS_DEV = 4
MOVE_CAP = 2
PATCH_DEV = 12
BANDS = 4
OWNERS = 32
PATCH = ("patch_0", "patch_1", "patch_2")
EVERY = ("patch_0", "patch_1", "patch_2", "grp")
DEVICES = 128

ROWS = 80
OWN_LO, OWN_HI = 8, 72
LANES = 128
TILES = 10
MSG = TILES + TILES // 2

SIGMA = 32.0
THETA = 14.0
EPSILON = 1e-12
BREAKDOWN = 3e-7

f32 = jnp.float32
bf16 = jnp.bfloat16
STATE = (ROWS, 3, 8, LANES)


def lanes_of(shape=(8, LANES)):
    return lax.broadcasted_iota(jnp.int32, shape, len(shape) - 1)


def roll(x, amount):
    return pltpu.roll(x, amount % LANES, axis=x.ndim - 1)


def swap_blocks(tiles, group):
    tiles = list(tiles)
    for bit in (1, 2, 4):
        high = (group & bit) != 0
        for i in range(8):
            if i & bit:
                continue
            a, b = tiles[i], tiles[i + bit]
            tiles[i] = jnp.where(high, roll(b, 16 * bit), a)
            tiles[i + bit] = jnp.where(high, b, roll(a, -16 * bit))
    return tiles


def face_kernel(levels_ref, where_ref, out_ref):
    band, owner = where_ref[0], where_ref[1]
    lane_group = lanes_of() // 16
    kappas = []
    for idx in range(6):
        patch_row = band * ROWS_DEV + idx - 1
        row_in = (patch_row >= 0) & (patch_row < BANDS * ROWS_DEV)
        row_safe = jnp.clip(patch_row, 0, BANDS * ROWS_DEV - 1)
        row_base = (row_safe // ROWS_DEV) * (OWNERS * PATCH_DEV) + (row_safe % ROWS_DEV) * COLS_DEV
        kap = jnp.zeros((8, LANES), f32)
        for g in range(8):
            near_owner = owner + (g - 2 - (g - 2) % COLS_DEV) // COLS_DEV
            inside = row_in & (near_owner >= 0) & (near_owner < OWNERS)
            safe = jnp.clip(near_owner, 0, OWNERS - 1)
            level = levels_ref[row_base + safe * PATCH_DEV + (g - 2) % COLS_DEV]
            value = jnp.where(level == 0, 1.0, jnp.where(level == 1, 4.0, 16.0))
            value = jnp.where(inside, value, 0.0).astype(f32)
            kap = jnp.where(lane_group == g, value, kap)
        kappas.append(kap)

    def face(own, near):
        return jnp.where(own == 0.0, 0.0, jnp.where(near == 0.0, own, 0.5 * (own + near)))

    for idx in range(6):
        kap = kappas[idx]
        out_ref[idx, 0] = face(kap, roll(kap, 1))
        out_ref[idx, 1] = face(kap, roll(kap, -1))
        out_ref[idx, 2] = face(kap, kappas[max(idx - 1, 0)])
        out_ref[idx, 3] = face(kap, kappas[min(idx + 1, 5)])
        out_ref[idx, 4] = kap


def tile_of(patch_ref, south_ref, north_ref, which, k, c):
    if k == 0:
        return south_ref[which, c]
    if k == TILES - 1:
        return north_ref[which, c]
    half = (k - 1) % 2
    return patch_ref[((k - 1) // 2) * COLS_DEV + c, :, half * LANES : (half + 1) * LANES]


def pack_kernel(pred_ref, prev_ref, south_ref, north_ref, right_ref, left_ref):
    odd = (lax.broadcasted_iota(jnp.int32, (SPECIES, LANES), 1) // 8) % 2 == 1
    for which, patch_ref in enumerate((pred_ref, prev_ref)):
        for ref in (right_ref, left_ref):
            ref[which, :, SPECIES:24, :] = jnp.zeros((MSG, 24 - SPECIES, LANES), f32)
        for k in range(TILES):
            right_ref[which, k, 0:SPECIES, :] = tile_of(patch_ref, south_ref, north_ref, which, k, 2)
            left_ref[which, k, 0:SPECIES, :] = tile_of(patch_ref, south_ref, north_ref, which, k, 0)
        for pair in range(TILES // 2):
            low = tile_of(patch_ref, south_ref, north_ref, which, 2 * pair, 1)
            high = tile_of(patch_ref, south_ref, north_ref, which, 2 * pair + 1, 1)
            right_ref[which, TILES + pair, 0:SPECIES, :] = jnp.where(odd, high, roll(low, -8))
            left_ref[which, TILES + pair, 0:SPECIES, :] = jnp.where(odd, roll(high, 8), low)


def row_faces(face_ref, row):
    idx = (row + 8) // 16
    kap = face_ref[idx, 4]
    south = face_ref[idx, 2] if row % 16 == 8 else kap
    north = face_ref[idx, 3] if row % 16 == 7 else kap
    return face_ref[idx, 0], face_ref[idx, 1], south, north


def mixed_rows(source, first, blocks):
    x = jnp.concatenate(
        [source[first : first + 2].reshape(48, LANES), source[first + 2 : first + 4].reshape(48, LANES)],
        axis=1,
    )
    high = x.astype(bf16)
    low = (x - high.astype(f32)).astype(bf16)
    m = jnp.dot(blocks, jnp.concatenate([high, low, high], axis=0), preferred_element_type=f32)
    m = m.reshape(2, 3, 8, 2 * LANES)
    return [m[0, :, :, :LANES], m[1, :, :, :LANES], m[0, :, :, LANES:], m[1, :, :, LANES:]]


def spread(source, row, faces):
    west, east, south, north = faces
    v = source[row]
    return (west * roll(v, 1) + east * roll(v, -1)) + (
        south * source[row - 1] + north * source[row + 1]
    )


def apply_rows(source, lo, hi, start, blocks, face_ref, diff, emit):
    for first in range(start, hi, 4):
        mixed = mixed_rows(source, first, blocks)
        for off in range(4):
            row = first + off
            if row < lo or row >= hi:
                continue
            faces = row_faces(face_ref, row)
            emit(row, faces, diff * spread(source, row, faces) + mixed[off])


class Dots:
    def __init__(self):
        self.sums = {}

    def add(self, key, value):
        self.sums[key] = value if key not in self.sums else self.sums[key] + value

    def write(self, out_ref):
        lane = lanes_of((1, LANES))
        own = (lanes_of() >= 32) & (lanes_of() < 80)
        total = jnp.zeros((1, LANES), f32)
        for at, key in enumerate(PAIRS):
            value = jnp.where(own, jnp.sum(self.sums[key], axis=0), 0.0)
            value = jnp.sum(jnp.sum(value, axis=0, keepdims=True), axis=1, keepdims=True)
            total = jnp.where(lane == at, value, total)
        out_ref[...] = total


PAIRS = [(i, j) for j in range(4) for i in range(j + 1)]


def krylov(refs, diag_ref, face_ref, diff, blocks, dots, reach, last_ref):
    for k in range(3):
        source, target = refs[k], last_ref if k == 2 else refs[k + 1]
        width = reach - k - 1
        lo, hi = OWN_LO - width, OWN_HI + width
        start = lo - (lo % 2)

        def emit(row, faces, rest, source=source, target=target, k=k):
            new = diag_ref[row] * source[row] - rest
            if target is not None:
                target[row] = new
            if OWN_LO <= row < OWN_HI:
                for i in range(k + 1):
                    dots.add((i, k + 1), refs[i][row] * new)
                dots.add((k + 1, k + 1), new * new)

        apply_rows(source, lo, hi, start, blocks, face_ref, diff, emit)


def first_kernel(
    pred_ref, prev_ref, south_ref, north_ref, from_left_ref, from_right_ref, face_ref, param_ref,
    block_ref, state_ref, p0_ref, p1_ref, p2_ref, p3_ref, gram_ref, own_ref, old_ref, diag_ref,
):
    group = lanes_of() // 16
    own_ref[:, SPECIES:24, :] = jnp.zeros((TILES * COLS_DEV, 24 - SPECIES, LANES), f32)
    for which, (patch_ref, target) in enumerate(((pred_ref, state_ref), (prev_ref, old_ref))):
        for k in range(TILES):
            for c in range(COLS_DEV):
                own_ref[k * COLS_DEV + c, 0:SPECIES, :] = tile_of(
                    patch_ref, south_ref, north_ref, which, k, c
                )
        for k in range(TILES):
            far_left = from_left_ref[which, TILES + k // 2].reshape(3, 8, LANES)
            far_right = from_right_ref[which, TILES + k // 2].reshape(3, 8, LANES)
            tiles = [
                far_left if k % 2 else roll(far_left, 8),
                from_left_ref[which, k].reshape(3, 8, LANES),
                own_ref[k * COLS_DEV].reshape(3, 8, LANES),
                own_ref[k * COLS_DEV + 1].reshape(3, 8, LANES),
                own_ref[k * COLS_DEV + 2].reshape(3, 8, LANES),
                from_right_ref[which, k].reshape(3, 8, LANES),
                roll(far_right, -8) if k % 2 else far_right,
                jnp.zeros((3, 8, LANES), f32),
            ]
            for a, row in enumerate(swap_blocks(tiles, group)):
                target[k * 8 + a] = row
    rate, diff, decay = param_ref[0], param_ref[1], param_ref[2]
    blocks = block_ref[...]
    dots = Dots()

    def emit(row, faces, rest):
        u = state_ref[row]
        west, east, south, north = faces
        base = rate + diff * ((west + east) + (south + north))
        cubic = decay * (u * u)
        new = (base + cubic) * u - rate * old_ref[row] - rest
        diag_ref[row] = base + 3.0 * cubic - THETA / SIGMA
        p0_ref[row] = new
        if OWN_LO <= row < OWN_HI:
            dots.add((0, 0), new * new)

    apply_rows(state_ref, 2, 78, 2, blocks, face_ref, diff, emit)
    krylov((p0_ref, p1_ref, p2_ref), diag_ref, face_ref, diff, blocks, dots, 6, p3_ref)
    dots.write(gram_ref)


def small_solve(matrix, vector):
    matrix = [list(row) for row in matrix]
    vector = list(vector)
    size = len(vector)
    for col in range(size):
        for target in range(col + 1, size):
            factor = matrix[target][col] / matrix[col][col]
            for at in range(col, size):
                matrix[target][at] = matrix[target][at] - factor * matrix[col][at]
            vector[target] = vector[target] - factor * vector[col]
    answer = [None] * size
    for col in reversed(range(size)):
        running = vector[col]
        for later in range(col + 1, size):
            running = running - matrix[col][later] * answer[later]
        answer[col] = running / matrix[col][col]
    return answer


def combine(parts_ref):
    totals = jnp.sum(parts_ref[...], axis=0, keepdims=True)
    gram = [[None] * 4 for _ in range(4)]
    for at, (i, j) in enumerate(PAIRS):
        gram[i][j] = gram[j][i] = jnp.broadcast_to(totals[:, at : at + 1], (8, LANES))
    zero = jnp.zeros((8, LANES), f32)
    beta = jnp.sqrt(gram[0][0] * (SIGMA * SIGMA) + EPSILON)
    basis = [[-SIGMA / beta]]
    hess = [[zero] * 3 for _ in range(4)]

    def dot(x, y):
        total = x[0] * y[0]
        for at in range(1, len(x)):
            total = total + x[at] * y[at]
        return total

    for j in range(3):
        last = basis[j]
        w = [THETA * last[at] for at in range(j + 1)] + [SIGMA * last[j]]
        for at in range(j):
            w[at + 1] = w[at + 1] + SIGMA * last[at]
        gw = [dot(w, gram[at]) for at in range(j + 2)]
        size = dot(w, gw)
        for i in range(j + 1):
            hess[i][j] = dot(basis[i], gw)
        for i in range(j + 1):
            for at in range(i + 1):
                w[at] = w[at] - hess[i][j] * basis[i][at]
        rest = dot(w, [dot(w, gram[at]) for at in range(j + 2)])
        alive = rest > BREAKDOWN * size
        height = jnp.sqrt(jnp.where(alive, rest, 0.0) + EPSILON)
        hess[j + 1][j] = height
        basis.append([jnp.where(alive, value / height, 0.0) for value in w])
    normal = [[dot([h[i] for h in hess], [h[j] for h in hess]) for j in range(3)] for i in range(3)]
    y = small_solve(normal, [beta * hess[0][i] for i in range(3)])
    out = []
    for at in range(3):
        total = None
        for j in range(at, 3):
            term = y[j] * basis[j][at]
            total = term if total is None else total + term
        out.append(total)
    return out


def second_kernel(
    parts_ref, state_ref, p0_ref, p1_ref, p2_ref, p3_ref, face_ref, param_ref, block_ref,
    next_ref, q0_ref, q1_ref, q2_ref, gram_ref, diag_ref,
):
    c0, c1, c2 = combine(parts_ref)
    shift = THETA / SIGMA
    rate, diff, decay = param_ref[0], param_ref[1], param_ref[2]
    blocks = block_ref[...]
    dots = Dots()
    a0, a1, a2 = 1.0 + shift * c0, c0 + shift * c1, c1 + shift * c2
    for row in range(5, 75):
        p0, p1, p2, u = p0_ref[row], p1_ref[row], p2_ref[row], state_ref[row]
        d = c0 * p0 + c1 * p1 + c2 * p2
        linear = (a0 * p0 + a1 * p1) + (a2 * p2 + c2 * p3_ref[row])
        new = linear + (decay * (d * d)) * (3.0 * u + d)
        west, east, south, north = row_faces(face_ref, row)
        u = u + d
        diag_ref[row] = (
            rate + diff * ((west + east) + (south + north)) + 3.0 * decay * (u * u) - shift
        )
        next_ref[row] = u
        q0_ref[row] = new
        if OWN_LO <= row < OWN_HI:
            dots.add((0, 0), new * new)
    krylov((q0_ref, q1_ref, q2_ref), diag_ref, face_ref, diff, blocks, dots, 3, None)
    dots.write(gram_ref)


def last_kernel(parts_ref, next_ref, q0_ref, q1_ref, q2_ref, owner_ref, where_ref, out_ref):
    band, owner = where_ref[0], where_ref[1]
    c0, c1, c2 = combine(parts_ref)
    group = lanes_of() // 16
    for slot in range(PATCH_DEV, PATCH_DEV + 2 * MOVE_CAP):
        out_ref[slot] = jnp.zeros((SPECIES, 2 * LANES), f32)
    base = (band * OWNERS + owner) * PATCH_DEV
    stays = [owner_ref[base + s] == owner for s in range(PATCH_DEV)]
    left_base = jnp.maximum(base - PATCH_DEV, 0)
    right_base = jnp.minimum(base + PATCH_DEV, BANDS * OWNERS * PATCH_DEV - PATCH_DEV)
    left_in = [
        (owner > 0) & (owner_ref[left_base + r * COLS_DEV + COLS_DEV - 1] == owner)
        for r in range(ROWS_DEV)
    ]
    right_in = [
        (owner < OWNERS - 1) & (owner_ref[right_base + r * COLS_DEV] == owner)
        for r in range(ROWS_DEV)
    ]
    for r in range(ROWS_DEV):
        halves = []
        for half in range(2):
            rows = []
            for a in range(8):
                row = OWN_LO + r * 16 + half * 8 + a
                rows.append(
                    next_ref[row] + (c0 * q0_ref[row] + c1 * q1_ref[row] + c2 * q2_ref[row])
                )
            halves.append([t.reshape(24, LANES)[:SPECIES] for t in swap_blocks(rows, group)])
        for c in range(COLS_DEV):
            keep = stays[r * COLS_DEV + c]
            for half in range(2):
                out_ref[r * COLS_DEV + c, :, half * LANES : (half + 1) * LANES] = jnp.where(
                    keep, halves[half][2 + c], 0.0
                )
        for moving, g, first in ((left_in, 1, PATCH_DEV), (right_in, 5, PATCH_DEV + MOVE_CAP)):
            rank = jnp.int32(0)
            for before in range(r):
                rank = rank + moving[before].astype(jnp.int32)
            for place in range(min(r + 1, MOVE_CAP)):

                @pl.when(moving[r] & (rank == place))
                def _(place=place, g=g, first=first):
                    for half in range(2):
                        out_ref[first + place, :, half * LANES : (half + 1) * LANES] = halves[half][g]


def call(kernel, out_shape, in_specs, scratch=(), limit=40):
    return pl.pallas_call(
        kernel,
        out_shape=out_shape,
        in_specs=in_specs,
        out_specs=jax.tree.map(lambda _: pl.BlockSpec(memory_space=pltpu.VMEM), out_shape),
        scratch_shapes=list(scratch),
        compiler_params=pltpu.CompilerParams(vmem_limit_bytes=limit << 20),
    )


def vm():
    return pl.BlockSpec(memory_space=pltpu.VMEM)


def sm():
    return pl.BlockSpec(memory_space=pltpu.SMEM)


def shifted(x, axis, step):
    count = lax.axis_size(axis)
    return lax.ppermute(
        x, axis, [(i, i + step) for i in range(count) if 0 <= i + step < count]
    )


def summed(gram):
    spread_out = jnp.broadcast_to(gram[None], (DEVICES, 1, LANES))
    return lax.all_to_all(spread_out, EVERY, 0, 0).reshape(DEVICES, LANES)


def per_device(previous, predicted, new_owner, levels, diffusion, decay, reaction):
    where = jnp.stack([lax.axis_index("grp"), lax.axis_index(PATCH)]).astype(jnp.int32)
    prev, pred = previous[0, 0], predicted[0, 0]
    up = jnp.stack([pred[9:12, :, LANES:], prev[9:12, :, LANES:]])
    down = jnp.stack([pred[0:3, :, :LANES], prev[0:3, :, :LANES]])
    south, north = shifted(up, "grp", 1), shifted(down, "grp", -1)

    rate = jnp.where(jnp.arange(24) < SPECIES - 1, 4.0, 0.0)
    pad = (0, 24 - SPECIES)
    params = jnp.stack([rate, jnp.pad(diffusion, pad), jnp.pad(decay, pad)]) / SIGMA
    params = jnp.broadcast_to(params.astype(f32)[:, :, None], (3, 24, LANES)).reshape(3, 3, 8, LANES)
    matrix = jnp.pad(reaction / SIGMA, (pad, pad))
    high = matrix.astype(bf16)
    low = (matrix - high.astype(f32)).astype(bf16)
    none = jnp.zeros_like(high)

    def two(x):
        return jnp.concatenate(
            [jnp.concatenate([x, none], axis=1), jnp.concatenate([none, x], axis=1)], axis=0
        )

    blocks = jnp.concatenate([two(high), two(high), two(low)], axis=1)

    shape = jax.ShapeDtypeStruct
    faces = call(face_kernel, shape((6, 5, 8, LANES), f32), [sm(), sm()])(levels.reshape(-1), where)
    message = shape((2, MSG, 24, LANES), f32)
    to_right, to_left = call(pack_kernel, (message, message), [vm()] * 4)(pred, prev, south, north)
    from_left, from_right = shifted(to_right, PATCH, 1), shifted(to_left, PATCH, -1)
    state = shape(STATE, f32)
    gram = shape((1, LANES), f32)
    u0, p0, p1, p2, p3, gram1 = call(
        first_kernel,
        (state,) * 5 + (gram,),
        [vm()] * 9,
        [
            pltpu.VMEM((TILES * COLS_DEV, 24, LANES), f32),
            pltpu.VMEM(STATE, f32),
            pltpu.VMEM(STATE, f32),
        ],
    )(pred, prev, south, north, from_left, from_right, faces, params, blocks)
    u1, q0, q1, q2, gram2 = call(
        second_kernel, (state,) * 4 + (gram,), [vm()] * 9, [pltpu.VMEM(STATE, f32)]
    )(summed(gram1), u0, p0, p1, p2, p3, faces, params, blocks)
    out = call(
        last_kernel,
        shape((PATCH_DEV + 2 * MOVE_CAP, SPECIES, 2 * LANES), f32),
        [vm()] * 5 + [sm(), sm()],
    )(summed(gram2), u1, q0, q1, q2, new_owner.reshape(-1), where)
    return out[None, None]


def solution(mesh):
    torus = Mesh(
        mesh.devices.reshape(4, 4, 2, mesh.shape["grp"]), ("patch_0", "patch_1", "patch_2", "grp")
    )
    spec = P("grp", PATCH, None, None, None)
    in_specs = (spec, spec, P(), P(), P(), P(), P())
    return jax.shard_map(
        per_device, mesh=torus, in_specs=in_specs, out_specs=spec, check_vma=False
    )
```

time: 781 us -> 74.2 us (0.10); the launches traced: 771 us -> 73.8 us
  blocking collectives: 246 us -> 20.8 us
  local copies, waits for them, and re-layouts: 231 us -> 6.68 us
  starting transfers between devices: 104 us -> 17.2 us
  matrix products: 69.1 us -> 0 us
  other arithmetic: 44.7 us -> 0.21 us
  between operations: 36 us -> 0.2 us
  waiting for transfers between devices: 39.5 us -> 15.2 us
  Pallas kernels: 0 us -> 13.4 us
    psum x32 -> x0, blocking collectives: 246 us -> none  [over_axes(): x = lax.psum(x, axis)]
    ppermute x34 -> x4, starting transfers between devices: 104 us -> 13.3 us  [shifted(): lax.ppermute(x, axis, [(i, i + step) for i in range(count) if 0 <= i + st...]
    dot_general x50 -> x0, matrix products: 69.1 us -> none  [the longest x8 22.3 us: mixing(): return jnp.einsum('st,kta->ksa', reaction, values, precision=highest)]
    another operation x87 -> x3, local copies, waits for them, and re-layouts: 58.6 us -> 0.18 us  [the longest x2 0.17 us: per_device(): jnp.stack([rate, jnp.pad(diffusion, pad), jnp.pad(decay, pad)]) / SIGMA]
    slice x48 -> x0, local copies, waits for them, and re-layouts: 48.2 us -> none  [the longest x8 21.5 us: neighbor_strips(): squared[:, :, :, 0]]
    reshape x40 -> x2, local copies, waits for them, and re-layouts: 35.5 us -> 0.2 us  [the longest x1 0.1 us: per_device(): new_owner.reshape(-1)]
    unnamed x286 -> x20, local copies, waits for them, and re-layouts: 39.7 us -> 4.61 us
    ppermute x34 -> x4, waiting for transfers between devices: 39.5 us -> 5.54 us  [shifted(): lax.ppermute(x, axis, [(i, i + step) for i in range(count) if 0 <= i + st...]
  transfers between devices with their start and end apart: 34 -> 5, of which waited for: 15 -> 3; matrix products, arithmetic and copies ran while one was open for 5% -> 1% of each run, Pallas kernels for 0% -> 1%
where the time goes in v1:
time: 74.2 us; the launch traced here: 73.8 us
  blocking collectives  20.8 us (28%)
  starting transfers between devices  17.2 us (23%)
  waiting for transfers between devices  15.2 us (20%)
  Pallas kernels  13.4 us (18%)
  local copies, waits for them, and re-layouts  6.68 us (9%)
    all_to_all x1, blocking collectives, summed(): return lax.all_to_all(spread_out, EVERY, 0, 0).reshape(DEVICES, LANES)  20.8 us
    ppermute x4, starting transfers between devices, shifted(): lax.ppermute(x, axis, [(i, i + step) for i in range(count) if 0 <= i + st...  13.3 us
    all_to_all x1, waiting for transfers between devices, summed(): return lax.all_to_all(spread_out, EVERY, 0, 0).reshape(DEVICES, LANES)  9.69 us
    pallas_call x1, Pallas kernels, per_device(): call(first_kernel, (state,) * 5 + (gram,), [vm()] * 9, [pltpu.VMEM((TILES...  7.3 us
    ppermute x4, waiting for transfers between devices, shifted(): lax.ppermute(x, axis, [(i, i + step) for i in range(count) if 0 <= i + st...  5.54 us
    unnamed x20, local copies, waits for them, and re-layouts  4.61 us
    all_to_all x1, starting transfers between devices, summed(): return lax.all_to_all(spread_out, EVERY, 0, 0).reshape(DEVICES, LANES)  3.96 us
    pallas_call x1, Pallas kernels, per_device(): call(second_kernel, (state,) * 4 + (gram,), [vm()] * 9, [pltpu.VMEM(STATE...  3.1 us
  transfers between devices with their start and end apart: 5, of which 3 were waited for; matrix products, arithmetic and copies ran while one was open for 1% of the time, Pallas kernels for 1%

profile of v1, /device:TPU:1, one launch (start us, length us, event | category | flops | bytes accessed | tf_op | source)
XLA Modules:
  0.0 73.8 jit_solution(2182015944928986102)
XLA Ops:
  0.0 1.0 %copy.19 = f32[1,1,12,21,256]{4,3,1,2,0:T(8,128)S(1)} copy(f32[1,1,12,21,256]{4,1,3,2,0:T(1,128)} %param.7) | data formatting | bytes 516096
  1.0 0.1 copy-done.2
  1.1 1.3 %collective-permute-start.1 = (f32[2,3,21,128]{3,2,1,0:T(8,128)S(1)}, f32[2,3,21,128]{3,2,1,0:T(8,128)S(1)}, u32[]{:S(2)}, u32[]{:S(2)}) collective-permute-start(f32[2,3,21,128]{3,2,1,0:T(8,128)S(1)} %pad_maximum_fusion.1), channel_id=1, source_target_pairs={{1,0},{2,1},{3,2},{5,4},{6,5},{7,6},{9,8},{10,9},{11,10},{13,12},{... | collective-permute-start | bytes 193544 | tf_op jit(solution)/shard_map/ppermute | solution.py:398
  2.5 4.7 %collective-permute-start = (f32[2,3,21,128]{3,2,1,0:T(8,128)S(1)}, f32[2,3,21,128]{3,2,1,0:T(8,128)S(1)}, u32[]{:S(2)}, u32[]{:S(2)}) collective-permute-start(f32[2,3,21,128]{3,2,1,0:T(8,128)S(1)} %pad_maximum_fusion), channel_id=1, source_target_pairs={{0,1},{1,2},{2,3},{4,5},{5,6},{6,7},{8,9},{9,10},{10,11},{12,13},{... | collective-permute-start | bytes 193544 | tf_op jit(solution)/shard_map/ppermute | solution.py:398
  7.2 1.3 %collective-permute-done.south_ref = f32[2,3,21,128]{3,2,1,0:T(8,128)S(1)} collective-permute-done((f32[2,3,21,128]{3,2,1,0:T(8,128)S(1)}, f32[2,3,21,128]{3,2,1,0:T(8,128)S(1)}, u32[]{:S(2)}, u32[]{:S(2)}) %collective-permute-start) | collective-permute-done | bytes 64544 | tf_op jit(solution)/shard_map/ppermute | solution.py:398
  8.5 0.1 shard_map.73
  8.7 5.4 %collective-permute-start.2 = (f32[2,15,24,128]{3,2,1,0:T(8,128)S(1)}, f32[2,15,24,128]{3,2,1,0:T(8,128)S(1)}, u32[]{:S(2)}, u32[]{:S(2)}) collective-permute-start(f32[2,15,24,128]{3,2,1,0:T(8,128)S(1)} %get-tuple-element.18), channel_id=1, source_target_pairs={{0,4},{4,8},{8,12},{12,16},{16,20},{20,24},{24,28},{28,32},{32,36}... | collective-permute-start | bytes 1105928 | tf_op jit(solution)/shard_map/ppermute | solution.py:398
  14.1 1.9 %collective-permute-start.3 = (f32[2,15,24,128]{3,2,1,0:T(8,128)S(1)}, f32[2,15,24,128]{3,2,1,0:T(8,128)S(1)}, u32[]{:S(2)}, u32[]{:S(2)}) collective-permute-start(f32[2,15,24,128]{3,2,1,0:T(8,128)S(1)} %get-tuple-element.19), channel_id=1, source_target_pairs={{4,0},{8,4},{12,8},{16,12},{20,16},{24,20},{28,24},{32,28},{36,32}... | collective-permute-start | bytes 1105928 | tf_op jit(solution)/shard_map/ppermute | solution.py:398
  16.0 0.1 pad_add_fusion.where_ref
  16.1 0.1 copy.12
  16.2 0.1 reshape.58.levels_ref
  16.3 0.6 copy-done.6
  16.8 0.1 stack.46
  16.9 0.6 copy-done.7
  17.5 0.1 stack.47
  17.6 0.9 %shard_map.74.face_ref = f32[6,5,8,128]{3,2,1,0:T(8,128)S(1)} custom-call(s32[1536]{0:T(1024)S(1)} %reshape.58.levels_ref, s32[2]{0:T(128)S(1)} %pad_add_fusion.where_ref), custom_call_target="tpu_custom_call" | custom-call | tf_op jit(solution)/shard_map/pallas_call | solution.py:432
  18.5 0.1 fusion.9
  18.6 0.1 fusion.7.block_ref
  18.7 4.2 %collective-permute-done.3.from_right_ref = f32[2,15,24,128]{3,2,1,0:T(8,128)S(1)} collective-permute-done((f32[2,15,24,128]{3,2,1,0:T(8,128)S(1)}, f32[2,15,24,128]{3,2,1,0:T(8,128)S(1)}, u32[]{:S(2)}, u32[]{:S(2)}) %collective-permute-start.3) | collective-permute-done | bytes 368672 | tf_op jit(solution)/shard_map/ppermute | solution.py:398
  22.9 0.1 broadcast_in_dim.36.param_ref
  23.0 7.3 %shard_map.75 = (f32[80,3,8,128]{3,2,1,0:T(8,128)S(1)}, f32[80,3,8,128]{3,2,1,0:T(8,128)S(1)}, f32[80,3,8,128]{3,2,1,0:T(8,128)S(1)}, f32[80,3,8,128]{3,2,1,0:T(...) custom-call(f32[12,21,256]{2,1,0:T(8,128)S(1)} %bitcast.26, f32[12,21,256]{2,1,0:T(8,128)S(1)} %bitcast.23, ...), custom_call_target="tpu_custom_call" | custom-call | tf_op jit(solution)/shard_map/pallas_call | solution.py:438
  30.3 20.8 %all_to_all.10 = f32[128,1,128]{2,1,0:T(1,128)S(1)} all-to-all(f32[128,1,128]{2,1,0:T(1,128)S(1)} %broadcast_in_dim.38), channel_id=1, replica_groups=mesh['patch_0'=4,'patch_1'=4,'patch_2'=2,'grp'=4] {'patch_0','patch_1','..., dimensions={0} | all-to-all | bytes 131072 | tf_op jit(solution)/shard_map/all_to_all | solution.py:405
  51.1 3.1 %shard_map.76 = (f32[80,3,8,128]{3,2,1,0:T(8,128)S(1)}, f32[80,3,8,128]{3,2,1,0:T(8,128)S(1)}, f32[80,3,8,128]{3,2,1,0:T(8,128)S(1)}, f32[80,3,8,128]{3,2,1,0:T(8,128)S(1)}, f32[1,128]{1,0:T(1,128)S(1)}) custom-call(f32[128,128]{1,0:T(8,128)S(1)} %bitcast.29, f32[80,3,8,128]{3,2,1,0:T(8,128)S(1)} %get-tuple-element.21.state_ref, ...), custom_call_target="tpu_custom_call" | custom-call | tf_op jit(solution)/shard_map/pallas_call | solution.py:448
  54.2 1.0 %copy-done = f32[80,3,8,128]{3,2,1,0:T(8,128)} copy-done((f32[80,3,8,128]{3,2,1,0:T(8,128)}, f32[80,3,8,128]{3,2,1,0:T(8,128)S(1)}, u32[]{:S(2)}) %copy-start) | copy-done | bytes 983064
  55.2 0.7 broadcast_in_dim.40
  55.8 4.0 %all-to-all-start.1 = ((f32[128,1,128]{2,1,0:T(1,128)}), f32[128,1,128]{2,1,0:T(1,128)S(1)}, u32[]{:S(2)}, u32[]{:S(2)}) async-start(f32[128,1,128]{2,1,0:T(1,128)} %broadcast_in_dim.40), calls=%async_computation.1 | async-start | bytes 131072 | tf_op jit(solution)/shard_map/all_to_all | solution.py:405
  59.8 0.1 copy.13
  59.9 0.1 reshape.61.owner_ref
  60.0 9.7 %all-to-all-done.1 = f32[128,1,128]{2,1,0:T(1,128)S(1)} async-done(((f32[128,1,128]{2,1,0:T(1,128)}), f32[128,1,128]{2,1,0:T(1,128)S(1)}, u32[]{:S(2)}, u32[]{:S(2)}) %all-to-all-start.1) | async-done | bytes 65568 | tf_op jit(solution)/shard_map/all_to_all | solution.py:405
  69.7 1.2 %copy-done.1 = f32[80,3,8,128]{3,2,1,0:T(8,128)S(1)} copy-done((f32[80,3,8,128]{3,2,1,0:T(8,128)S(1)}, f32[80,3,8,128]{3,2,1,0:T(8,128)}, u32[]{:S(2)}) %copy-start.1) | copy-done | bytes 983064
  70.9 2.0 %shard_map.77 = f32[16,21,256]{2,1,0:T(8,128)S(1)} custom-call(f32[128,128]{1,0:T(8,128)S(1)} %bitcast.28, f32[80,3,8,128]{3,2,1,0:T(8,128)S(1)} %get-tuple-element.27.next_ref, f32[80,3,8,128]{3,2,1,0:T(8,128)S(1)} %get-tuple-element.28.q0_ref, f32[80,3,8,128]{3,2,1,0:T(8,128)S(1)} %get-tuple-element.29.q1_ref, f32[80,3,8,128]{3,2,1,0:T(8,128)S(1)} %copy-done.1, ...), custom_call_target="tpu_custom_call" | custom-call | tf_op jit(solution)/shard_map/pallas_call | solution.py:451
  72.9 0.8 %copy.14 = f32[1,1,16,21,256]{4,2,3,1,0:T(8,128)} copy(f32[1,1,16,21,256]{4,3,2,1,0:T(8,128)S(1)} %bitcast.27) | data formatting | bytes 688128 | tf_op jit(solution)/shard_map/broadcast_in_dim | solution.py:456
  (25 shorter events, 0.2 us)
Async XLA Ops:
  0.0 1.1 %copy-start.2 = (f32[1,1,12,21,256]{4,1,3,2,0:T(1,128)S(1)}, f32[1,1,12,21,256]{4,1,3,2,0:T(1,128)}, u32[]{:S(2)}) copy-start(f32[1,1,12,21,256]{4,1,3,2,0:T(1,128)} %param.8) | copy-start | bytes 774148
  1.1 6.1 %collective-permute-start.1 = (f32[2,3,21,128]{3,2,1,0:T(8,128)S(1)}, f32[2,3,21,128]{3,2,1,0:T(8,128)S(1)}, u32[]{:S(2)}, u32[]{:S(2)}) collective-permute-start(f32[2,3,21,128]{3,2,1,0:T(8,128)S(1)} %pad_maximum_fusion.1), channel_id=1, source_target_pairs={{1,0},{2,1},{3,2},{5,4},{6,5},{7,6},{9,8},{10,9},{11,10},{13,12},{... | collective-permute-start | bytes 193544 | tf_op jit(solution)/shard_map/ppermute | solution.py:398
  2.4 4.7 %copy-start.5 = (f32[21,21]{1,0:T(8,128)S(1)}, f32[21,21]{1,0:T(8,128)}, u32[]{:S(2)}) copy-start(f32[21,21]{1,0:T(8,128)} %param.13) | copy-start | bytes 5296
  2.5 6.0 %collective-permute-start = (f32[2,3,21,128]{3,2,1,0:T(8,128)S(1)}, f32[2,3,21,128]{3,2,1,0:T(8,128)S(1)}, u32[]{:S(2)}, u32[]{:S(2)}) collective-permute-start(f32[2,3,21,128]{3,2,1,0:T(8,128)S(1)} %pad_maximum_fusion), channel_id=1, source_target_pairs={{0,1},{1,2},{2,3},{4,5},{5,6},{6,7},{8,9},{9,10},{10,11},{12,13},{... | collective-permute-start | bytes 193544 | tf_op jit(solution)/shard_map/ppermute | solution.py:398
  8.5 7.6 %copy-start.3 = (s32[4,32,12]{1,0,2:T(4,128)S(1)}, s32[4,32,12]{1,0,2:T(4,128)}, u32[]{:S(2)}) copy-start(s32[4,32,12]{1,0,2:T(4,128)} %param.10) | copy-start | bytes 18436
  8.7 10.0 %collective-permute-start.2 = (f32[2,15,24,128]{3,2,1,0:T(8,128)S(1)}, f32[2,15,24,128]{3,2,1,0:T(8,128)S(1)}, u32[]{:S(2)}, u32[]{:S(2)}) collective-permute-start(f32[2,15,24,128]{3,2,1,0:T(8,128)S(1)} %get-tuple-element.18), channel_id=1, source_target_pairs={{0,4},{4,8},{8,12},{12,16},{16,20},{20,24},{24,28},{28,32},{32,36}... | collective-permute-start | bytes 1105928 | tf_op jit(solution)/shard_map/ppermute | solution.py:398
  14.1 8.8 %collective-permute-start.3 = (f32[2,15,24,128]{3,2,1,0:T(8,128)S(1)}, f32[2,15,24,128]{3,2,1,0:T(8,128)S(1)}, u32[]{:S(2)}, u32[]{:S(2)}) collective-permute-start(f32[2,15,24,128]{3,2,1,0:T(8,128)S(1)} %get-tuple-element.19), channel_id=1, source_target_pairs={{4,0},{8,4},{12,8},{16,12},{20,16},{24,20},{28,24},{32,28},{36,32}... | collective-permute-start | bytes 1105928 | tf_op jit(solution)/shard_map/ppermute | solution.py:398
  16.2 0.7 copy-start.6
  16.8 0.7 copy-start.7
  54.2 1.0 %copy-start = (f32[80,3,8,128]{3,2,1,0:T(8,128)}, f32[80,3,8,128]{3,2,1,0:T(8,128)S(1)}, u32[]{:S(2)}) copy-start(f32[80,3,8,128]{3,2,1,0:T(8,128)S(1)} %get-tuple-element.30.q2_ref) | copy-start | bytes 2949124
  55.8 4.0 %copy-start.4 = (s32[4,32,12]{1,0,2:T(4,128)S(1)}, s32[4,32,12]{1,0,2:T(4,128)}, u32[]{:S(2)}) copy-start(s32[4,32,12]{1,0,2:T(4,128)} %param.9) | copy-start | bytes 18436
  55.8 13.9 %all-to-all-start.1 = ((f32[128,1,128]{2,1,0:T(1,128)}), f32[128,1,128]{2,1,0:T(1,128)S(1)}, u32[]{:S(2)}, u32[]{:S(2)}) async-start(f32[128,1,128]{2,1,0:T(1,128)} %broadcast_in_dim.40), calls=%async_computation.1 | async-start | bytes 131072 | tf_op jit(solution)/shard_map/all_to_all | solution.py:405
  69.7 1.2 %copy-start.1 = (f32[80,3,8,128]{3,2,1,0:T(8,128)S(1)}, f32[80,3,8,128]{3,2,1,0:T(8,128)}, u32[]{:S(2)}) copy-start(f32[80,3,8,128]{3,2,1,0:T(8,128)} %copy-done) | copy-start | bytes 2949124

commit v2 on v1

v2 whole, which is shorter than its diff:
```python
import jax
import jax.numpy as jnp
from jax import lax
from jax.experimental import pallas as pl
from jax.experimental.pallas import tpu as pltpu
from jax.sharding import Mesh
from jax.sharding import PartitionSpec as P

SPECIES = 21
COLS_DEV = 3
ROWS_DEV = 4
MOVE_CAP = 2
PATCH_DEV = 12
BANDS = 4
OWNERS = 32
PATCH = ("patch_0", "patch_1", "patch_2")
EVERY = ("patch_0", "patch_1", "patch_2", "grp")
DEVICES = 128

ROWS = 80
OWN_LO, OWN_HI = 8, 72
LANES = 128
TILES = 10
MSG = TILES + TILES // 2

SIGMA = 32.0
THETA = 14.0
EPSILON = 1e-12
BREAKDOWN = 3e-7

f32 = jnp.float32
bf16 = jnp.bfloat16
STATE = (ROWS, 3, 8, LANES)


def lanes_of(shape=(8, LANES)):
    return lax.broadcasted_iota(jnp.int32, shape, len(shape) - 1)


def roll(x, amount):
    return pltpu.roll(x, amount % LANES, axis=x.ndim - 1)


def swap_blocks(rolled, wanted):
    group = lanes_of() // 16
    tiles = list(rolled)
    for bit in (1, 2, 4):
        high = (group & bit) != 0
        tiles = [jnp.where(high, tiles[(i + bit) % 8], tiles[i]) for i in range(8)]
    return {a: roll(tiles[-a % 8], -16 * a) for a in wanted}


def face_kernel(levels_ref, where_ref, face_ref, stencil_ref):
    band, owner = where_ref[0], where_ref[1]
    lane_group = lanes_of() // 16
    kappas = []
    for idx in range(6):
        patch_row = band * ROWS_DEV + idx - 1
        row_in = (patch_row >= 0) & (patch_row < BANDS * ROWS_DEV)
        row_safe = jnp.clip(patch_row, 0, BANDS * ROWS_DEV - 1)
        row_base = (row_safe // ROWS_DEV) * (OWNERS * PATCH_DEV) + (row_safe % ROWS_DEV) * COLS_DEV
        kap = jnp.zeros((8, LANES), f32)
        for g in range(8):
            near_owner = owner + (g - 2 - (g - 2) % COLS_DEV) // COLS_DEV
            inside = row_in & (near_owner >= 0) & (near_owner < OWNERS)
            safe = jnp.clip(near_owner, 0, OWNERS - 1)
            level = levels_ref[row_base + safe * PATCH_DEV + (g - 2) % COLS_DEV]
            value = jnp.where(level == 0, 1.0, jnp.where(level == 1, 4.0, 16.0))
            value = jnp.where(inside, value, 0.0).astype(f32)
            kap = jnp.where(lane_group == g, value, kap)
        kappas.append(kap)

    def face(own, near):
        return jnp.where(own == 0.0, 0.0, jnp.where(near == 0.0, own, 0.5 * (own + near)))

    source = lax.broadcasted_iota(jnp.int32, (LANES, LANES), 0)
    target = lax.broadcasted_iota(jnp.int32, (LANES, LANES), 1)
    for idx in range(6):
        kap = kappas[idx]
        west, east = face(kap, roll(kap, 1)), face(kap, roll(kap, -1))
        face_ref[idx, 0] = west + east
        face_ref[idx, 1] = face(kap, kappas[max(idx - 1, 0)])
        face_ref[idx, 2] = face(kap, kappas[min(idx + 1, 5)])
        face_ref[idx, 3] = kap
        weights = jnp.where(
            source == target - 1,
            jnp.broadcast_to(west[0:1], (LANES, LANES)),
            jnp.where(source == target + 1, jnp.broadcast_to(east[0:1], (LANES, LANES)), 0.0),
        ).astype(bf16)
        stencil_ref[idx, 0:LANES, :] = weights
        stencil_ref[idx, LANES : 2 * LANES, :] = weights


def half_tile(patch_ref, slot, half):
    return patch_ref[pl.ds(slot * 2 * SPECIES + half, SPECIES, stride=2), :]


def row_strip_kernel(pred_ref, prev_ref, where_ref, first_ref, second_ref):
    even = where_ref[0] % 2 == 0
    pad = jnp.zeros((24 - SPECIES, LANES), f32)
    for which, patch_ref in enumerate((pred_ref, prev_ref)):
        for c in range(COLS_DEV):
            up = half_tile(patch_ref, 3 * COLS_DEV + c, 1)
            down = half_tile(patch_ref, c, 0)
            first_ref[which, c, 0:SPECIES, :] = jnp.where(even, up, down)
            second_ref[which, c, 0:SPECIES, :] = jnp.where(even, down, up)
            first_ref[which, c, SPECIES:24, :] = pad
            second_ref[which, c, SPECIES:24, :] = pad


def tile_of(patch_ref, rows_ref, where_ref, which, k, c):
    if k in (0, TILES - 1):
        band = where_ref[0]
        even = band % 2 == 0
        first, second = (ref[which, c, 0:SPECIES, :] for ref in rows_ref)
        south, inside = k == 0, (band > 0) if k == 0 else (band < BANDS - 1)
        tile = jnp.where(even, second, first) if south else jnp.where(even, first, second)
        return jnp.where(inside, tile, 0.0)
    return half_tile(patch_ref, ((k - 1) // 2) * COLS_DEV + c, (k - 1) % 2)


def pack_kernel(pred_ref, prev_ref, row1_ref, row2_ref, where_ref, first_ref, second_ref):
    odd = (lax.broadcasted_iota(jnp.int32, (SPECIES, LANES), 1) // 8) % 2 == 1
    even_owner = where_ref[1] % 2 == 0
    rows_ref = (row1_ref, row2_ref)
    for which, patch_ref in enumerate((pred_ref, prev_ref)):
        for ref in (first_ref, second_ref):
            ref[which, :, SPECIES:24, :] = jnp.zeros((MSG, 24 - SPECIES, LANES), f32)

        def put(at, right, left, which=which):
            first_ref[which, at, 0:SPECIES, :] = jnp.where(even_owner, right, left)
            second_ref[which, at, 0:SPECIES, :] = jnp.where(even_owner, left, right)

        def tile(k, c, which=which, patch_ref=patch_ref):
            return tile_of(patch_ref, rows_ref, where_ref, which, k, c)

        for k in range(TILES):
            put(k, tile(k, 2), tile(k, 0))
        for pair in range(TILES // 2):
            low, high = tile(2 * pair, 1), tile(2 * pair + 1, 1)
            put(
                TILES + pair,
                jnp.where(odd, high, roll(low, -8)),
                jnp.where(odd, roll(high, 8), low),
            )


def row_faces(face_ref, row):
    idx = (row + 8) // 16
    kap = face_ref[idx, 3]
    south = face_ref[idx, 1] if row % 16 == 8 else kap
    north = face_ref[idx, 2] if row % 16 == 7 else kap
    return face_ref[idx, 0], south, north


def vertical(source, row, faces):
    _, south, north = faces
    if row % 16 in (7, 8):
        return south * source[row - 1] + north * source[row + 1]
    return south * (source[row - 1] + source[row + 1])


def apply_rows(source, lo, hi, blocks, stencil_ref, face_ref, diff, emit):
    for idx in range(6):
        first, last = max(lo, idx * 16 - 8), min(hi, idx * 16 + 8)
        if first >= last:
            continue
        start, stop = first - first % 2, last + last % 2
        parts = []
        for row in range(start, stop, 2):
            x = source[row : row + 2].reshape(48, LANES)
            high = x.astype(bf16)
            parts.append((high, (x - high.astype(f32)).astype(bf16)))
        beside = jnp.dot(
            jnp.concatenate([jnp.concatenate(part, axis=1) for part in parts], axis=0),
            stencil_ref[idx],
            preferred_element_type=f32,
        ).reshape(stop - start, 3, 8, LANES)
        mixed = []
        for at in range(0, len(parts), 2):
            group = parts[at : at + 2]
            high = jnp.concatenate([part[0] for part in group], axis=1)
            low = jnp.concatenate([part[1] for part in group], axis=1)
            m = jnp.dot(
                blocks, jnp.concatenate([high, low, high], axis=0), preferred_element_type=f32
            ).reshape(2, 3, 8, len(group) * LANES)
            for pair in range(len(group)):
                for off in range(2):
                    mixed.append(m[off, :, :, pair * LANES : (pair + 1) * LANES])
        for row in range(first, last):
            faces = row_faces(face_ref, row)
            near = beside[row - start] + vertical(source, row, faces)
            emit(row, faces, diff * near + mixed[row - start])


class Dots:
    def __init__(self):
        self.sums = {}

    def add(self, key, value):
        self.sums[key] = value if key not in self.sums else self.sums[key] + value

    def write(self, out_ref):
        lane = lanes_of((1, LANES))
        own = (lanes_of() >= 32) & (lanes_of() < 80)
        total = jnp.zeros((1, LANES), f32)
        for at, key in enumerate(PAIRS):
            value = jnp.where(own, jnp.sum(self.sums[key], axis=0), 0.0)
            value = jnp.sum(jnp.sum(value, axis=0, keepdims=True), axis=1, keepdims=True)
            total = jnp.where(lane == at, value, total)
        out_ref[...] = total


PAIRS = [(i, j) for j in range(4) for i in range(j + 1)]


def krylov(refs, diag_ref, tables, diff, dots, reach, last_ref):
    for k in range(3):
        source, target = refs[k], last_ref if k == 2 else refs[k + 1]
        width = reach - k - 1
        lo, hi = OWN_LO - width, OWN_HI + width

        def emit(row, faces, rest, source=source, target=target, k=k):
            new = diag_ref[row] * source[row] - rest
            if target is not None:
                target[row] = new
            if OWN_LO <= row < OWN_HI:
                for i in range(k + 1):
                    dots.add((i, k + 1), refs[i][row] * new)
                dots.add((k + 1, k + 1), new * new)

        apply_rows(source, lo, hi, *tables, diff, emit)


def first_kernel(
    pred_ref, prev_ref, row1_ref, row2_ref, col1_ref, col2_ref, where_ref, face_ref, stencil_ref,
    param_ref, block_ref, state_ref, p0_ref, p1_ref, p2_ref, p3_ref, gram_ref, own_ref, old_ref,
    diag_ref,
):
    owner = where_ref[1]
    even_owner, has_left, has_right = owner % 2 == 0, owner > 0, owner < OWNERS - 1
    rows_ref = (row1_ref, row2_ref)
    own_ref[:, SPECIES:24, :] = jnp.zeros((2 * TILES * COLS_DEV, 24 - SPECIES, LANES), f32)
    for which, patch_ref in enumerate((pred_ref, prev_ref)):
        for k in range(TILES):
            for c in range(COLS_DEV):
                own_ref[(which * TILES + k) * COLS_DEV + c, 0:SPECIES, :] = tile_of(
                    patch_ref, rows_ref, where_ref, which, k, c
                )
    for which, target in enumerate((state_ref, old_ref)):

        def beside(at, which=which):
            first, second = (ref[which, at].reshape(3, 8, LANES) for ref in (col1_ref, col2_ref))
            left, right = jnp.where(even_owner, second, first), jnp.where(even_owner, first, second)
            return jnp.where(has_left, left, 0.0), jnp.where(has_right, right, 0.0)

        for k in range(TILES):
            if k % 2 == 0:
                far_left, far_right = beside(TILES + k // 2)
            left, right = beside(k)
            own = [
                own_ref[(which * TILES + k) * COLS_DEV + c].reshape(3, 8, LANES)
                for c in range(COLS_DEV)
            ]
            tiles = [
                far_left if k % 2 else roll(far_left, 8),
                roll(left, 16),
                roll(own[0], 32),
                roll(own[1], 48),
                roll(own[2], 64),
                roll(right, 80),
                roll(far_right, 88 if k % 2 else 96),
                jnp.zeros((3, 8, LANES), f32),
            ]
            for a, row in swap_blocks(tiles, range(8)).items():
                target[k * 8 + a] = row
    rate, diff, decay = param_ref[0], param_ref[1], param_ref[2]
    tables = (block_ref[...], stencil_ref, face_ref)
    dots = Dots()

    def emit(row, faces, rest):
        u = state_ref[row]
        base = rate + diff * (faces[0] + (faces[1] + faces[2]))
        cubic = decay * (u * u)
        new = (base + cubic) * u - rate * old_ref[row] - rest
        diag_ref[row] = (base - THETA / SIGMA) + 3.0 * cubic
        p0_ref[row] = new
        if OWN_LO <= row < OWN_HI:
            dots.add((0, 0), new * new)

    apply_rows(state_ref, 2, 78, *tables, diff, emit)
    krylov((p0_ref, p1_ref, p2_ref), diag_ref, tables, diff, dots, 6, p3_ref)
    dots.write(gram_ref)


def small_solve(matrix, vector):
    matrix = [list(row) for row in matrix]
    vector = list(vector)
    size = len(vector)
    for col in range(size):
        for target in range(col + 1, size):
            factor = matrix[target][col] / matrix[col][col]
            for at in range(col, size):
                matrix[target][at] = matrix[target][at] - factor * matrix[col][at]
            vector[target] = vector[target] - factor * vector[col]
    answer = [None] * size
    for col in reversed(range(size)):
        running = vector[col]
        for later in range(col + 1, size):
            running = running - matrix[col][later] * answer[later]
        answer[col] = running / matrix[col][col]
    return answer


def combine(parts_ref):
    totals = jnp.sum(parts_ref[...], axis=0, keepdims=True)
    gram = [[None] * 4 for _ in range(4)]
    for at, (i, j) in enumerate(PAIRS):
        gram[i][j] = gram[j][i] = jnp.broadcast_to(totals[:, at : at + 1], (8, LANES))
    zero = jnp.zeros((8, LANES), f32)
    beta = jnp.sqrt(gram[0][0] * (SIGMA * SIGMA) + EPSILON)
    basis = [[-SIGMA / beta]]
    hess = [[zero] * 3 for _ in range(4)]

    def dot(x, y):
        total = x[0] * y[0]
        for at in range(1, len(x)):
            total = total + x[at] * y[at]
        return total

    for j in range(3):
        last = basis[j]
        w = [THETA * last[at] for at in range(j + 1)] + [SIGMA * last[j]]
        for at in range(j):
            w[at + 1] = w[at + 1] + SIGMA * last[at]
        gw = [dot(w, gram[at]) for at in range(j + 2)]
        size = dot(w, gw)
        for i in range(j + 1):
            hess[i][j] = dot(basis[i], gw)
        for i in range(j + 1):
            for at in range(i + 1):
                w[at] = w[at] - hess[i][j] * basis[i][at]
        rest = dot(w, [dot(w, gram[at]) for at in range(j + 2)])
        alive = rest > BREAKDOWN * size
        height = jnp.sqrt(jnp.where(alive, rest, 0.0) + EPSILON)
        hess[j + 1][j] = height
        basis.append([jnp.where(alive, value / height, 0.0) for value in w])
    normal = [[dot([h[i] for h in hess], [h[j] for h in hess]) for j in range(3)] for i in range(3)]
    y = small_solve(normal, [beta * hess[0][i] for i in range(3)])
    out = []
    for at in range(3):
        total = None
        for j in range(at, 3):
            term = y[j] * basis[j][at]
            total = term if total is None else total + term
        out.append(total)
    return out


def second_kernel(
    parts_ref, state_ref, p0_ref, p1_ref, p2_ref, p3_ref, face_ref, stencil_ref, param_ref,
    block_ref, next_ref, q0_ref, q1_ref, q2_ref, gram_ref, diag_ref,
):
    c0, c1, c2 = combine(parts_ref)
    shift = THETA / SIGMA
    rate, diff, decay = param_ref[0], param_ref[1], param_ref[2]
    tables = (block_ref[...], stencil_ref, face_ref)
    dots = Dots()
    a0, a1, a2 = 1.0 + shift * c0, c0 + shift * c1, c1 + shift * c2
    triple = 3.0 * decay
    for row in range(5, 75):
        p0, p1, p2, u = p0_ref[row], p1_ref[row], p2_ref[row], state_ref[row]
        d = c0 * p0 + c1 * p1 + c2 * p2
        linear = (a0 * p0 + a1 * p1) + (a2 * p2 + c2 * p3_ref[row])
        new = linear + (decay * (d * d)) * (3.0 * u + d)
        beside, south, north = row_faces(face_ref, row)
        u = u + d
        base = rate + diff * (beside + (south + north)) - shift
        diag_ref[row] = base + triple * (u * u)
        next_ref[row] = u
        q0_ref[row] = new
        if OWN_LO <= row < OWN_HI:
            dots.add((0, 0), new * new)
    krylov((q0_ref, q1_ref, q2_ref), diag_ref, tables, diff, dots, 3, None)
    dots.write(gram_ref)


SLOTS = PATCH_DEV + 2 * MOVE_CAP


def last_kernel(
    parts_ref, next_ref, q0_ref, q1_ref, q2_ref, owner_ref, where_ref, out_ref, low_ref, high_ref
):
    band, owner = where_ref[0], where_ref[1]
    c0, c1, c2 = combine(parts_ref)
    slots_ref = (low_ref, high_ref)
    for ref in slots_ref:
        ref[PATCH_DEV * 24 : SLOTS * 24, :] = jnp.zeros((2 * MOVE_CAP * 24, LANES), f32)
    base = (band * OWNERS + owner) * PATCH_DEV
    stays = [owner_ref[base + s] == owner for s in range(PATCH_DEV)]
    left_base = jnp.maximum(base - PATCH_DEV, 0)
    right_base = jnp.minimum(base + PATCH_DEV, BANDS * OWNERS * PATCH_DEV - PATCH_DEV)
    left_in = [
        (owner > 0) & (owner_ref[left_base + r * COLS_DEV + COLS_DEV - 1] == owner)
        for r in range(ROWS_DEV)
    ]
    right_in = [
        (owner < OWNERS - 1) & (owner_ref[right_base + r * COLS_DEV] == owner)
        for r in range(ROWS_DEV)
    ]
    for r in range(ROWS_DEV):
        halves = []
        for half in range(2):
            rows = []
            for a in range(8):
                row = OWN_LO + r * 16 + half * 8 + a
                value = next_ref[row] + (c0 * q0_ref[row] + c1 * q1_ref[row] + c2 * q2_ref[row])
                rows.append(roll(value, 16 * a) if a else value)
            halves.append(
                {g: t.reshape(24, LANES) for g, t in swap_blocks(rows, range(1, 6)).items()}
            )
        for c in range(COLS_DEV):
            slot = r * COLS_DEV + c
            for half in range(2):
                slots_ref[half][slot * 24 : slot * 24 + 24, :] = jnp.where(
                    stays[slot], halves[half][2 + c], 0.0
                )
        for moving, g, first in ((left_in, 1, PATCH_DEV), (right_in, 5, PATCH_DEV + MOVE_CAP)):
            rank = jnp.int32(0)
            for before in range(r):
                rank = rank + moving[before].astype(jnp.int32)
            for place in range(min(r + 1, MOVE_CAP)):

                @pl.when(moving[r] & (rank == place))
                def _(slot=first + place, g=g):
                    for half in range(2):
                        slots_ref[half][slot * 24 : slot * 24 + 24, :] = halves[half][g]

    for s in range(SPECIES):
        for part in range(SLOTS // 8):
            for half in range(2):
                out_ref[s, part * 8 : part * 8 + 8, half * LANES : (half + 1) * LANES] = slots_ref[
                    half
                ][pl.ds(part * 8 * 24 + s, 8, stride=24), :]


def call(kernel, out_shape, in_specs, scratch=(), limit=16):
    return pl.pallas_call(
        kernel,
        out_shape=out_shape,
        in_specs=in_specs,
        out_specs=jax.tree.map(lambda _: pl.BlockSpec(memory_space=pltpu.VMEM), out_shape),
        scratch_shapes=list(scratch),
        compiler_params=pltpu.CompilerParams(vmem_limit_bytes=limit << 20),
    )


def vm():
    return pl.BlockSpec(memory_space=pltpu.VMEM)


def sm():
    return pl.BlockSpec(memory_space=pltpu.SMEM)


def exchanged(x, axis, odd):
    count = lax.axis_size(axis)
    mates = [((i - odd) ^ 1) + odd for i in range(odd, count + odd)]
    return lax.ppermute(x, axis, [((i + odd) % count, m % count) for i, m in enumerate(mates)])


def summed(gram):
    spread_out = jnp.broadcast_to(gram[None], (DEVICES, 1, LANES))
    return lax.all_to_all(spread_out, EVERY, 0, 0).reshape(DEVICES, LANES)


def per_device(previous, predicted, new_owner, levels, diffusion, decay, reaction):
    where = jnp.stack([lax.axis_index("grp"), lax.axis_index(PATCH)]).astype(jnp.int32)
    prev, pred = (x.reshape(PATCH_DEV * SPECIES * 2, LANES) for x in (previous, predicted))
    shape = jax.ShapeDtypeStruct
    strip = shape((2, COLS_DEV, 24, LANES), f32)
    strips = call(row_strip_kernel, (strip, strip), [vm(), vm(), sm()])(pred, prev, where)
    row1, row2 = (exchanged(x, "grp", odd) for odd, x in enumerate(strips))

    rate = jnp.where(jnp.arange(24) < SPECIES - 1, 4.0, 0.0)
    pad = (0, 24 - SPECIES)
    params = jnp.stack([rate, jnp.pad(diffusion, pad), jnp.pad(decay, pad)]) / SIGMA
    params = jnp.broadcast_to(params.astype(f32)[:, :, None], (3, 24, LANES)).reshape(3, 3, 8, LANES)
    matrix = jnp.pad(reaction / SIGMA, (pad, pad))
    rounded = lax.reduce_precision(matrix, 8, 7)
    high = rounded.astype(bf16)
    low = (matrix - rounded).astype(bf16)
    none = jnp.zeros_like(high)

    def two(x):
        return jnp.concatenate(
            [jnp.concatenate([x, none], axis=1), jnp.concatenate([none, x], axis=1)], axis=0
        )

    blocks = jnp.concatenate([two(high), two(high), two(low)], axis=1)

    faces, stencil = call(
        face_kernel, (shape((6, 4, 8, LANES), f32), shape((6, 2 * LANES, LANES), bf16)), [sm(), sm()]
    )(levels.reshape(-1), where)
    message = shape((2, MSG, 24, LANES), f32)
    messages = call(pack_kernel, (message, message), [vm()] * 4 + [sm()])(
        pred, prev, row1, row2, where
    )
    col1, col2 = (exchanged(x, PATCH, odd) for odd, x in enumerate(messages))
    state = shape(STATE, f32)
    gram = shape((1, LANES), f32)
    u0, p0, p1, p2, p3, gram1 = call(
        first_kernel,
        (state,) * 5 + (gram,),
        [vm()] * 6 + [sm()] + [vm()] * 4,
        [
            pltpu.VMEM((2 * TILES * COLS_DEV, 24, LANES), f32),
            pltpu.VMEM(STATE, f32),
            pltpu.VMEM(STATE, f32),
        ],
    )(pred, prev, row1, row2, col1, col2, where, faces, stencil, params, blocks)
    u1, q0, q1, q2, gram2 = call(
        second_kernel, (state,) * 4 + (gram,), [vm()] * 10, [pltpu.VMEM(STATE, f32)]
    )(summed(gram1), u0, p0, p1, p2, p3, faces, stencil, params, blocks)
    out = call(
        last_kernel,
        shape((SPECIES, SLOTS, 2 * LANES), f32),
        [vm()] * 5 + [sm(), sm()],
        [pltpu.VMEM((SLOTS * 24, LANES), f32)] * 2,
    )(summed(gram2), u1, q0, q1, q2, new_owner.reshape(-1), where)
    return jnp.transpose(out, (1, 0, 2))[None, None]


def solution(mesh):
    torus = Mesh(
        mesh.devices.reshape(4, 4, 2, mesh.shape["grp"]), ("patch_0", "patch_1", "patch_2", "grp")
    )
    spec = P("grp", PATCH, None, None, None)
    in_specs = (spec, spec, P(), P(), P(), P(), P())
    return jax.shard_map(
        per_device, mesh=torus, in_specs=in_specs, out_specs=spec, check_vma=False
    )
```

time: 74.2 us -> 67.3 us (0.907)
  starting transfers between devices: 17.2 us -> 11.9 us
  Pallas kernels: 13.4 us -> 11.5 us
  blocking collectives: 20.8 us -> 21.6 us
    ppermute x4, starting transfers between devices: 13.3 us -> 7.89 us  [exchanged(): lax.ppermute(x, axis, [((i + odd) % count, m % count) for i, m in enumera...]
    pallas_call x5 -> x6, Pallas kernels: 13.4 us -> 11.5 us  [the longest x1 4.17 us: per_device(): call(first_kernel, (state,) * 5 + (gram,), [vm()] * 6 + [sm()] + [vm()] *...]
    broadcast_in_dim x1 -> x0, local copies, waits for them, and re-layouts: 0.84 us -> none  [per_device(): return out[None, None]]
    all_to_all x1, blocking collectives: 20.8 us -> 21.6 us  [summed(): return lax.all_to_all(spread_out, EVERY, 0, 0).reshape(DEVICES, LANES)]
    unnamed x20 -> x24, local copies, waits for them, and re-layouts: 4.61 us -> 4.86 us
where the time goes in v2:
time: 67.3 us; the launch traced here: 67 us
  blocking collectives  21.6 us (32%)
  waiting for transfers between devices  15.7 us (23%)
  starting transfers between devices  11.9 us (18%)
  Pallas kernels  11.5 us (17%)
  local copies, waits for them, and re-layouts  6.09 us (9%)
    all_to_all x1, blocking collectives, summed(): return lax.all_to_all(spread_out, EVERY, 0, 0).reshape(DEVICES, LANES)  21.6 us
    all_to_all x1, waiting for transfers between devices, summed(): return lax.all_to_all(spread_out, EVERY, 0, 0).reshape(DEVICES, LANES)  9.7 us
    ppermute x4, starting transfers between devices, exchanged(): lax.ppermute(x, axis, [((i + odd) % count, m % count) for i, m in enumera...  7.89 us
    ppermute x4, waiting for transfers between devices, exchanged(): lax.ppermute(x, axis, [((i + odd) % count, m % count) for i, m in enumera...  6.01 us
    unnamed x24, local copies, waits for them, and re-layouts  4.86 us
    pallas_call x1, Pallas kernels, per_device(): call(first_kernel, (state,) * 5 + (gram,), [vm()] * 6 + [sm()] + [vm()] *...  4.17 us
    all_to_all x1, starting transfers between devices, summed(): return lax.all_to_all(spread_out, EVERY, 0, 0).reshape(DEVICES, LANES)  3.96 us
    pallas_call x1, Pallas kernels, per_device(): call(second_kernel, (state,) * 4 + (gram,), [vm()] * 10, [pltpu.VMEM(STAT...  2.63 us
  transfers between devices with their start and end apart: 5, of which 3 were waited for; matrix products, arithmetic and copies ran while one was open for 1% of the time, Pallas kernels for 1%

profile of v2, /device:TPU:1, one launch (start us, length us, event | category | flops | bytes accessed | tf_op | source)
XLA Modules:
  0.0 67.0 jit_solution(6313382230756084206)
XLA Ops:
  0.0 0.1 pad_add_fusion.where_ref
  0.1 0.9 %copy-done = f32[1,1,12,21,256]{4,1,3,2,0:T(1,128)S(1)} copy-done((f32[1,1,12,21,256]{4,1,3,2,0:T(1,128)S(1)}, f32[1,1,12,21,256]{4,1,3,2,0:T(1,128)}, u32[]{:S(2)}) %copy-start) | copy-done | bytes 258072
  1.0 0.9 %copy-done.2 = f32[1,1,12,21,256]{4,1,3,2,0:T(1,128)S(1)} copy-done((f32[1,1,12,21,256]{4,1,3,2,0:T(1,128)S(1)}, f32[1,1,12,21,256]{4,1,3,2,0:T(1,128)}, u32[]{:S(2)}) %copy-start.2) | copy-done | bytes 258072
  2.0 0.6 shard_map.73
  2.5 2.2 %collective-permute-start = (f32[2,3,24,128]{3,2,1,0:T(8,128)S(1)}, f32[2,3,24,128]{3,2,1,0:T(8,128)S(1)}, u32[]{:S(2)}, u32[]{:S(2)}) collective-permute-start(f32[2,3,24,128]{3,2,1,0:T(8,128)S(1)} %get-tuple-element.22), channel_id=1, source_target_pairs={{0,1},{1,0},{2,3},{3,2},{4,5},{5,4},{6,7},{7,6},{8,9},{9,8},{10,11... | collective-permute-start | bytes 221192 | tf_op jit(solution)/shard_map/ppermute | solution.py:469
  4.7 1.9 %collective-permute-start.1 = (f32[2,3,24,128]{3,2,1,0:T(8,128)S(1)}, f32[2,3,24,128]{3,2,1,0:T(8,128)S(1)}, u32[]{:S(2)}, u32[]{:S(2)}) collective-permute-start(f32[2,3,24,128]{3,2,1,0:T(8,128)S(1)} %get-tuple-element.23), channel_id=1, source_target_pairs={{1,2},{2,1},{3,0},{0,3},{5,6},{6,5},{7,4},{4,7},{9,10},{10,9},{11,... | collective-permute-start | bytes 221192 | tf_op jit(solution)/shard_map/ppermute | solution.py:469
  6.7 0.0 copy-start.10
  6.7 0.1 stack.22
  6.8 0.6 copy-done.10
  7.3 0.1 stack.23
  7.4 1.7 %collective-permute-done.1.row2_ref = f32[2,3,24,128]{3,2,1,0:T(8,128)S(1)} collective-permute-done((f32[2,3,24,128]{3,2,1,0:T(8,128)S(1)}, f32[2,3,24,128]{3,2,1,0:T(8,128)S(1)}, u32[]{:S(2)}, u32[]{:S(2)}) %collective-permute-start.1) | collective-permute-done | bytes 73760 | tf_op jit(solution)/shard_map/ppermute | solution.py:469
  9.2 0.7 %shard_map.74 = (f32[2,15,24,128]{3,2,1,0:T(8,128)S(1)}, f32[2,15,24,128]{3,2,1,0:T(8,128)S(1)}) custom-call(f32[504,128]{1,0:T(8,128)S(1)} %bitcast.12, f32[504,128]{1,0:T(8,128)S(1)} %bitcast.15, f32[2,3,24,128]{3,2,1,0:T(8,128)S(1)} %collective-permute-done.row1_ref, f32[2,3,24,128]{3,2,1,0:T(8,128)S(1)} %collective-permute-done.1.row2_ref, ...), custom_call_target="tpu_custom_call" | custom-call | tf_op jit(solution)/shard_map/pallas_call | solution.py:506
  9.9 2.2 %collective-permute-start.2 = (f32[2,15,24,128]{3,2,1,0:T(8,128)S(1)}, f32[2,15,24,128]{3,2,1,0:T(8,128)S(1)}, u32[]{:S(2)}, u32[]{:S(2)}) collective-permute-start(f32[2,15,24,128]{3,2,1,0:T(8,128)S(1)} %get-tuple-element.24), channel_id=1, source_target_pairs={{0,4},{4,0},{8,12},{12,8},{16,20},{20,16},{24,28},{28,24},{32,36},... | collective-permute-start | bytes 1105928 | tf_op jit(solution)/shard_map/ppermute | solution.py:469
  12.0 1.6 %collective-permute-start.3 = (f32[2,15,24,128]{3,2,1,0:T(8,128)S(1)}, f32[2,15,24,128]{3,2,1,0:T(8,128)S(1)}, u32[]{:S(2)}, u32[]{:S(2)}) collective-permute-start(f32[2,15,24,128]{3,2,1,0:T(8,128)S(1)} %get-tuple-element.25), channel_id=1, source_target_pairs={{4,8},{8,4},{12,16},{16,12},{20,24},{24,20},{28,32},{32,28},{36,40... | collective-permute-start | bytes 1105928 | tf_op jit(solution)/shard_map/ppermute | solution.py:469
  13.7 0.1 copy.10
  13.8 0.1 reshape.66.levels_ref
  13.9 0.9 %shard_map.75 = (f32[6,4,8,128]{3,2,1,0:T(8,128)S(1)}, bf16[6,256,128]{2,1,0:T(8,128)(2,1)S(1)}) custom-call(s32[1536]{0:T(1024)S(1)} %reshape.66.levels_ref, s32[2]{0:T(128)S(1)} %pad_add_fusion.where_ref), custom_call_target="tpu_custom_call" | custom-call | tf_op jit(solution)/shard_map/pallas_call | solution.py:502
  14.8 0.1 fusion.10
  14.9 0.1 fusion.7.block_ref
  15.0 4.3 %collective-permute-done.3.col2_ref = f32[2,15,24,128]{3,2,1,0:T(8,128)S(1)} collective-permute-done((f32[2,15,24,128]{3,2,1,0:T(8,128)S(1)}, f32[2,15,24,128]{3,2,1,0:T(8,128)S(1)}, u32[]{:S(2)}, u32[]{:S(2)}) %collective-permute-start.3) | collective-permute-done | bytes 368672 | tf_op jit(solution)/shard_map/ppermute | solution.py:469
  19.3 0.1 broadcast_in_dim.36.param_ref
  19.3 4.2 %shard_map.76 = (f32[80,3,8,128]{3,2,1,0:T(8,128)S(1)}, f32[80,3,8,128]{3,2,1,0:T(8,128)S(1)}, f32[80,3,8,128]{3,2,1,0:T(8,128)S(1)}, f32[80,3,8,128]{3,2,1,0:T(...) custom-call(f32[504,128]{1,0:T(8,128)S(1)} %bitcast.13, f32[504,128]{1,0:T(8,128)S(1)} %bitcast.16, ...), custom_call_target="tpu_custom_call" | custom-call | tf_op jit(solution)/shard_map/pallas_call | solution.py:512
  23.6 21.6 %all_to_all.10 = f32[128,1,128]{2,1,0:T(1,128)S(1)} all-to-all(f32[128,1,128]{2,1,0:T(1,128)S(1)} %broadcast_in_dim.38), channel_id=1, replica_groups=mesh['patch_0'=4,'patch_1'=4,'patch_2'=2,'grp'=4] {'patch_0','patch_1','..., dimensions={0} | all-to-all | bytes 131072 | tf_op jit(solution)/shard_map/all_to_all | solution.py:474
  45.1 2.6 %shard_map.77 = (f32[80,3,8,128]{3,2,1,0:T(8,128)S(1)}, f32[80,3,8,128]{3,2,1,0:T(8,128)S(1)}, f32[80,3,8,128]{3,2,1,0:T(8,128)S(1)}, f32[80,3,8,128]{3,2,1,0:T(8,128)S(1)}, f32[1,128]{1,0:T(1,128)S(1)}) custom-call(f32[128,128]{1,0:T(8,128)S(1)} %bitcast.18, f32[80,3,8,128]{3,2,1,0:T(8,128)S(1)} %get-tuple-element.29.state_ref, ...), custom_call_target="tpu_custom_call" | custom-call | tf_op jit(solution)/shard_map/pallas_call | solution.py:522
  47.8 1.0 %copy-done.4 = f32[80,3,8,128]{3,2,1,0:T(8,128)} copy-done((f32[80,3,8,128]{3,2,1,0:T(8,128)}, f32[80,3,8,128]{3,2,1,0:T(8,128)S(1)}, u32[]{:S(2)}) %copy-start.4) | copy-done | bytes 983064
  48.7 0.7 broadcast_in_dim.40
  49.4 4.0 %all-to-all-start.1 = ((f32[128,1,128]{2,1,0:T(1,128)}), f32[128,1,128]{2,1,0:T(1,128)S(1)}, u32[]{:S(2)}, u32[]{:S(2)}) async-start(f32[128,1,128]{2,1,0:T(1,128)} %broadcast_in_dim.40), calls=%async_computation.1 | async-start | bytes 131072 | tf_op jit(solution)/shard_map/all_to_all | solution.py:474
  53.4 0.1 copy.11
  53.5 0.1 reshape.69.owner_ref
  53.6 9.7 %all-to-all-done.1 = f32[128,1,128]{2,1,0:T(1,128)S(1)} async-done(((f32[128,1,128]{2,1,0:T(1,128)}), f32[128,1,128]{2,1,0:T(1,128)S(1)}, u32[]{:S(2)}, u32[]{:S(2)}) %all-to-all-start.1) | async-done | bytes 65568 | tf_op jit(solution)/shard_map/all_to_all | solution.py:474
  63.3 1.2 %copy-done.5 = f32[80,3,8,128]{3,2,1,0:T(8,128)S(1)} copy-done((f32[80,3,8,128]{3,2,1,0:T(8,128)S(1)}, f32[80,3,8,128]{3,2,1,0:T(8,128)}, u32[]{:S(2)}) %copy-start.5) | copy-done | bytes 983064
  64.5 2.5 %shard_map.78 = f32[21,16,256]{2,1,0:T(8,128)} custom-call(f32[128,128]{1,0:T(8,128)S(1)} %bitcast.17, f32[80,3,8,128]{3,2,1,0:T(8,128)S(1)} %get-tuple-element.35.next_ref, f32[80,3,8,128]{3,2,1,0:T(8,128)S(1)} %get-tuple-element.36.q0_ref, f32[80,3,8,128]{3,2,1,0:T(8,128)S(1)} %get-tuple-element.37.q1_ref, f32[80,3,8,128]{3,2,1,0:T(8,128)S(1)} %copy-done.5, ...), custom_call_target="tpu_custom_call" | custom-call | tf_op jit(solution)/shard_map/pallas_call | solution.py:525
  (25 shorter events, 0.1 us)
Async XLA Ops:
  0.0 6.6 %copy-start.8 = (f32[21,21]{1,0:T(8,128)S(1)}, f32[21,21]{1,0:T(8,128)}, u32[]{:S(2)}) copy-start(f32[21,21]{1,0:T(8,128)} %param.13) | copy-start | bytes 5296
  0.1 0.9 %copy-start = (f32[1,1,12,21,256]{4,1,3,2,0:T(1,128)S(1)}, f32[1,1,12,21,256]{4,1,3,2,0:T(1,128)}, u32[]{:S(2)}) copy-start(f32[1,1,12,21,256]{4,1,3,2,0:T(1,128)} %param.8) | copy-start | bytes 774148
  1.0 0.9 %copy-start.2 = (f32[1,1,12,21,256]{4,1,3,2,0:T(1,128)S(1)}, f32[1,1,12,21,256]{4,1,3,2,0:T(1,128)}, u32[]{:S(2)}) copy-start(f32[1,1,12,21,256]{4,1,3,2,0:T(1,128)} %param.7) | copy-start | bytes 774148
  2.0 7.2 %copy-start.1 = (f32[1,1,12,21,256]{4,1,3,2,0:T(1,128)S(1)}, f32[1,1,12,21,256]{4,1,3,2,0:T(1,128)}, u32[]{:S(2)}) copy-start(f32[1,1,12,21,256]{4,1,3,2,0:T(1,128)} %param.8) | copy-start | bytes 774148
  2.0 7.2 %copy-start.3 = (f32[1,1,12,21,256]{4,1,3,2,0:T(1,128)S(1)}, f32[1,1,12,21,256]{4,1,3,2,0:T(1,128)}, u32[]{:S(2)}) copy-start(f32[1,1,12,21,256]{4,1,3,2,0:T(1,128)} %param.7) | copy-start | bytes 774148
  2.5 4.9 %collective-permute-start = (f32[2,3,24,128]{3,2,1,0:T(8,128)S(1)}, f32[2,3,24,128]{3,2,1,0:T(8,128)S(1)}, u32[]{:S(2)}, u32[]{:S(2)}) collective-permute-start(f32[2,3,24,128]{3,2,1,0:T(8,128)S(1)} %get-tuple-element.22), channel_id=1, source_target_pairs={{0,1},{1,0},{2,3},{3,2},{4,5},{5,4},{6,7},{7,6},{8,9},{9,8},{10,11... | collective-permute-start | bytes 221192 | tf_op jit(solution)/shard_map/ppermute | solution.py:469
  4.7 1.9 %copy-start.9 = (f32[21]{0:T(128)S(1)}, f32[21]{0:T(128)}, u32[]{:S(2)}) copy-start(f32[21]{0:T(128)} %param.11) | copy-start | bytes 256
  4.7 4.4 %collective-permute-start.1 = (f32[2,3,24,128]{3,2,1,0:T(8,128)S(1)}, f32[2,3,24,128]{3,2,1,0:T(8,128)S(1)}, u32[]{:S(2)}, u32[]{:S(2)}) collective-permute-start(f32[2,3,24,128]{3,2,1,0:T(8,128)S(1)} %get-tuple-element.23), channel_id=1, source_target_pairs={{1,2},{2,1},{3,0},{0,3},{5,6},{6,5},{7,4},{4,7},{9,10},{10,9},{11,... | collective-permute-start | bytes 221192 | tf_op jit(solution)/shard_map/ppermute | solution.py:469
  6.7 0.7 copy-start.10
  9.2 4.5 %copy-start.6 = (s32[4,32,12]{1,0,2:T(4,128)S(1)}, s32[4,32,12]{1,0,2:T(4,128)}, u32[]{:S(2)}) copy-start(s32[4,32,12]{1,0,2:T(4,128)} %param.10) | copy-start | bytes 18436
  9.9 5.1 %collective-permute-start.2 = (f32[2,15,24,128]{3,2,1,0:T(8,128)S(1)}, f32[2,15,24,128]{3,2,1,0:T(8,128)S(1)}, u32[]{:S(2)}, u32[]{:S(2)}) collective-permute-start(f32[2,15,24,128]{3,2,1,0:T(8,128)S(1)} %get-tuple-element.24), channel_id=1, source_target_pairs={{0,4},{4,0},{8,12},{12,8},{16,20},{20,16},{24,28},{28,24},{32,36},... | collective-permute-start | bytes 1105928 | tf_op jit(solution)/shard_map/ppermute | solution.py:469
  12.0 7.2 %collective-permute-start.3 = (f32[2,15,24,128]{3,2,1,0:T(8,128)S(1)}, f32[2,15,24,128]{3,2,1,0:T(8,128)S(1)}, u32[]{:S(2)}, u32[]{:S(2)}) collective-permute-start(f32[2,15,24,128]{3,2,1,0:T(8,128)S(1)} %get-tuple-element.25), channel_id=1, source_target_pairs={{4,8},{8,4},{12,16},{16,12},{20,24},{24,20},{28,32},{32,28},{36,40... | collective-permute-start | bytes 1105928 | tf_op jit(solution)/shard_map/ppermute | solution.py:469
  47.8 1.0 %copy-start.4 = (f32[80,3,8,128]{3,2,1,0:T(8,128)}, f32[80,3,8,128]{3,2,1,0:T(8,128)S(1)}, u32[]{:S(2)}) copy-start(f32[80,3,8,128]{3,2,1,0:T(8,128)S(1)} %get-tuple-element.38.q2_ref) | copy-start | bytes 2949124
  49.4 4.0 %copy-start.7 = (s32[4,32,12]{1,0,2:T(4,128)S(1)}, s32[4,32,12]{1,0,2:T(4,128)}, u32[]{:S(2)}) copy-start(s32[4,32,12]{1,0,2:T(4,128)} %param.9) | copy-start | bytes 18436
  49.4 13.9 %all-to-all-start.1 = ((f32[128,1,128]{2,1,0:T(1,128)}), f32[128,1,128]{2,1,0:T(1,128)S(1)}, u32[]{:S(2)}, u32[]{:S(2)}) async-start(f32[128,1,128]{2,1,0:T(1,128)} %broadcast_in_dim.40), calls=%async_computation.1 | async-start | bytes 131072 | tf_op jit(solution)/shard_map/all_to_all | solution.py:474
  63.3 1.2 %copy-start.5 = (f32[80,3,8,128]{3,2,1,0:T(8,128)S(1)}, f32[80,3,8,128]{3,2,1,0:T(8,128)}, u32[]{:S(2)}) copy-start(f32[80,3,8,128]{3,2,1,0:T(8,128)} %copy-done.4) | copy-start | bytes 2949124

commit v3 on v2

--- a/solution.py
+++ b/solution.py
@@ -33,6 +33,10 @@
 STATE = (ROWS, 3, 8, LANES)
 
 
+def position():
+    return lax.axis_index("grp"), lax.axis_index(PATCH)
+
+
 def lanes_of(shape=(8, LANES)):
     return lax.broadcasted_iota(jnp.int32, shape, len(shape) - 1)
 
@@ -41,17 +45,51 @@
     return pltpu.roll(x, amount % LANES, axis=x.ndim - 1)
 
 
-def swap_blocks(rolled, wanted):
+def mix_blocks(rolled):
     group = lanes_of() // 16
     tiles = list(rolled)
     for bit in (1, 2, 4):
         high = (group & bit) != 0
         tiles = [jnp.where(high, tiles[(i + bit) % 8], tiles[i]) for i in range(8)]
-    return {a: roll(tiles[-a % 8], -16 * a) for a in wanted}
-
-
-def face_kernel(levels_ref, where_ref, face_ref, stencil_ref):
-    band, owner = where_ref[0], where_ref[1]
+    return tiles
+
+
+def swap_blocks(rolled, wanted):
+    tiles = mix_blocks(rolled)
+    return {a: roll(tiles[-a % 8], -16 * a) if a else tiles[0] for a in wanted}
+
+
+STAYS = PATCH_DEV
+ARRIVALS = [(r, m) for r in range(ROWS_DEV) for m in range(min(r + 1, MOVE_CAP))]
+FLAGS = STAYS + 2 * len(ARRIVALS)
+
+
+def write_flags(owners_ref, flag_ref, band, owner):
+    base = (band * OWNERS + owner) * PATCH_DEV
+
+    def put(at, condition):
+        flag_ref[at] = jnp.full((8, LANES), jnp.where(condition, 1, 0), jnp.int32)
+
+    for slot in range(PATCH_DEV):
+        put(slot, owners_ref[base + slot] == owner)
+    left_base = jnp.maximum(base - PATCH_DEV, 0)
+    right_base = jnp.minimum(base + PATCH_DEV, (BANDS * OWNERS - 1) * PATCH_DEV)
+    sides = ((owner > 0, left_base + COLS_DEV - 1), (owner < OWNERS - 1, right_base))
+    for side, (exists, first) in enumerate(sides):
+        moving = [
+            jnp.where(exists & (owners_ref[first + r * COLS_DEV] == owner), 1, 0)
+            for r in range(ROWS_DEV)
+        ]
+        for at, (r, m) in enumerate(ARRIVALS):
+            rank = jnp.int32(0)
+            for before in range(r):
+                rank = rank + moving[before]
+            put(STAYS + side * len(ARRIVALS) + at, (moving[r] == 1) & (rank == m))
+
+
+def face_kernel(levels_ref, owners_ref, face_ref, stencil_ref, flag_ref):
+    band, owner = position()
+    write_flags(owners_ref, flag_ref, band, owner)
     lane_group = lanes_of() // 16
     kappas = []
     for idx in range(6):
@@ -95,44 +133,90 @@
     return patch_ref[pl.ds(slot * 2 * SPECIES + half, SPECIES, stride=2), :]
 
 
-def row_strip_kernel(pred_ref, prev_ref, where_ref, first_ref, second_ref):
-    even = where_ref[0] % 2 == 0
-    pad = jnp.zeros((24 - SPECIES, LANES), f32)
-    for which, patch_ref in enumerate((pred_ref, prev_ref)):
+ROW_TILES = 2 * COLS_DEV
+COL_TILES = 2 * MSG
+
+
+def dense(tiles):
+    return -(-(tiles * SPECIES + 24 - SPECIES) // 8) * 8
+
+
+def put_tile(ref, at, tile):
+    ref[at * SPECIES : (at + 1) * SPECIES, :] = tile
+
+
+def finish(ref, tiles):
+    ref[tiles * SPECIES :, :] = jnp.zeros((dense(tiles) - tiles * SPECIES, LANES), f32)
+
+
+def get_tile(ref, at):
+    tile = ref[at * SPECIES : at * SPECIES + 24, :]
+    species = lax.broadcasted_iota(jnp.int32, (24, LANES), 0)
+    return jnp.where(species < SPECIES, tile, 0.0)
+
+
+INPUT_ROWS = PATCH_DEV * 2 * SPECIES
+EDGE = 128
+
+
+def row_strip_kernel(pred_hbm, prev_hbm, pred_ref, prev_ref, first_ref, second_ref, sems):
+    band, _ = position()
+    even = band % 2 == 0
+    top = INPUT_ROWS - EDGE
+    spans = ((0, EDGE), (top, EDGE), (EDGE, top - EDGE))
+    pairs = ((pred_hbm, pred_ref), (prev_hbm, prev_ref))
+    copies = [
+        [
+            pltpu.make_async_copy(
+                source.at[pl.ds(start, size), :],
+                target.at[pl.ds(start, size), :],
+                sems.at[3 * which + at],
+            )
+            for at, (start, size) in enumerate(spans)
+        ]
+        for which, (source, target) in enumerate(pairs)
+    ]
+    for at in range(3):
+        for which in range(2):
+            copies[which][at].start()
+    for which, (_, patch_ref) in enumerate(pairs):
+        copies[which][0].wait()
+        copies[which][1].wait()
         for c in range(COLS_DEV):
-            up = half_tile(patch_ref, 3 * COLS_DEV + c, 1)
+            up = half_tile(patch_ref, PATCH_DEV - COLS_DEV + c, 1)
             down = half_tile(patch_ref, c, 0)
-            first_ref[which, c, 0:SPECIES, :] = jnp.where(even, up, down)
-            second_ref[which, c, 0:SPECIES, :] = jnp.where(even, down, up)
-            first_ref[which, c, SPECIES:24, :] = pad
-            second_ref[which, c, SPECIES:24, :] = pad
-
-
-def tile_of(patch_ref, rows_ref, where_ref, which, k, c):
+            put_tile(first_ref, which * COLS_DEV + c, jnp.where(even, up, down))
+            put_tile(second_ref, which * COLS_DEV + c, jnp.where(even, down, up))
+    finish(first_ref, ROW_TILES)
+    finish(second_ref, ROW_TILES)
+    copies[0][2].wait()
+    copies[1][2].wait()
+
+
+def tile_of(patch_ref, rows_ref, which, k, c):
     if k in (0, TILES - 1):
-        band = where_ref[0]
+        band, _ = position()
         even = band % 2 == 0
-        first, second = (ref[which, c, 0:SPECIES, :] for ref in rows_ref)
+        at = (which * COLS_DEV + c) * SPECIES
+        first, second = (ref[at : at + SPECIES, :] for ref in rows_ref)
         south, inside = k == 0, (band > 0) if k == 0 else (band < BANDS - 1)
         tile = jnp.where(even, second, first) if south else jnp.where(even, first, second)
         return jnp.where(inside, tile, 0.0)
     return half_tile(patch_ref, ((k - 1) // 2) * COLS_DEV + c, (k - 1) % 2)
 
 
-def pack_kernel(pred_ref, prev_ref, row1_ref, row2_ref, where_ref, first_ref, second_ref):
+def pack_kernel(pred_ref, prev_ref, row1_ref, row2_ref, first_ref, second_ref):
     odd = (lax.broadcasted_iota(jnp.int32, (SPECIES, LANES), 1) // 8) % 2 == 1
-    even_owner = where_ref[1] % 2 == 0
-    rows_ref = (row1_ref, row2_ref)
+    _, owner = position()
+    even_owner = owner % 2 == 0
     for which, patch_ref in enumerate((pred_ref, prev_ref)):
-        for ref in (first_ref, second_ref):
-            ref[which, :, SPECIES:24, :] = jnp.zeros((MSG, 24 - SPECIES, LANES), f32)
 
         def put(at, right, left, which=which):
-            first_ref[which, at, 0:SPECIES, :] = jnp.where(even_owner, right, left)
-            second_ref[which, at, 0:SPECIES, :] = jnp.where(even_owner, left, right)
+            put_tile(first_ref, which * MSG + at, jnp.where(even_owner, right, left))
+            put_tile(second_ref, which * MSG + at, jnp.where(even_owner, left, right))
 
         def tile(k, c, which=which, patch_ref=patch_ref):
-            return tile_of(patch_ref, rows_ref, where_ref, which, k, c)
+            return tile_of(patch_ref, (row1_ref, row2_ref), which, k, c)
 
         for k in range(TILES):
             put(k, tile(k, 2), tile(k, 0))
@@ -143,6 +227,27 @@
                 jnp.where(odd, high, roll(low, -8)),
                 jnp.where(odd, roll(high, 8), low),
             )
+    finish(first_ref, COL_TILES)
+    finish(second_ref, COL_TILES)
+
+
+def own_kernel(pred_ref, prev_ref, row1_ref, row2_ref, own_ref, tile_ref):
+    tile_ref[:, SPECIES:24, :] = jnp.zeros((2 * TILES * COLS_DEV, 24 - SPECIES, LANES), f32)
+    for which, patch_ref in enumerate((pred_ref, prev_ref)):
+        for k in range(TILES):
+            for c in range(COLS_DEV):
+                tile_ref[(which * TILES + k) * COLS_DEV + c, 0:SPECIES, :] = tile_of(
+                    patch_ref, (row1_ref, row2_ref), which, k, c
+                )
+    blank = jnp.zeros((3, 8, LANES), f32)
+    for which in range(2):
+        for k in range(TILES):
+            tiles = [blank] * 8
+            for c in range(COLS_DEV):
+                tile = tile_ref[(which * TILES + k) * COLS_DEV + c].reshape(3, 8, LANES)
+                tiles[2 + c] = roll(tile, 16 * (2 + c))
+            for a, tile in enumerate(mix_blocks(tiles)):
+                own_ref[which, k * 8 + a] = tile
 
 
 def row_faces(face_ref, row):
@@ -193,25 +298,44 @@
             emit(row, faces, diff * near + mixed[row - start])
 
 
+PAIRS = [(i, j) for j in range(4) for i in range(j + 1)]
+
+
 class Dots:
-    def __init__(self):
+    def __init__(self, packed_ref):
         self.sums = {}
-
-    def add(self, key, value):
-        self.sums[key] = value if key not in self.sums else self.sums[key] + value
+        self.packed_ref = packed_ref
+        self.half = None
+        lane = lanes_of()
+        self.own = (lane >= 32) & (lane < 80)
+        self.both = self.own | (lane >= 96) | (lane < 16)
+
+    def add(self, basis, row, value):
+        if not OWN_LO <= row < OWN_HI:
+            return
+        if row % 2 == 0:
+            self.half = value
+            return
+        at = (row - OWN_LO) // 2
+        value = jnp.where(self.own, self.half, roll(value, 64))
+        if basis < 3:
+            self.packed_ref[basis, at] = value
+        for before in range(basis + 1):
+            other = value if before == basis else self.packed_ref[before, at]
+            key, term = (before, basis), other * value
+            self.sums[key] = self.sums[key] + term if key in self.sums else term
 
     def write(self, out_ref):
         lane = lanes_of((1, LANES))
-        own = (lanes_of() >= 32) & (lanes_of() < 80)
         total = jnp.zeros((1, LANES), f32)
         for at, key in enumerate(PAIRS):
-            value = jnp.where(own, jnp.sum(self.sums[key], axis=0), 0.0)
+            value = jnp.where(self.both, jnp.sum(self.sums[key], axis=0), 0.0)
             value = jnp.sum(jnp.sum(value, axis=0, keepdims=True), axis=1, keepdims=True)
             total = jnp.where(lane == at, value, total)
         out_ref[...] = total
 
 
-PAIRS = [(i, j) for j in range(4) for i in range(j + 1)]
+PACKED = (3, (OWN_HI - OWN_LO) // 2, 3, 8, LANES)
 
 
 def krylov(refs, diag_ref, tables, diff, dots, reach, last_ref):
@@ -224,33 +348,37 @@
             new = diag_ref[row] * source[row] - rest
             if target is not None:
                 target[row] = new
-            if OWN_LO <= row < OWN_HI:
-                for i in range(k + 1):
-                    dots.add((i, k + 1), refs[i][row] * new)
-                dots.add((k + 1, k + 1), new * new)
+            dots.add(k + 1, row, new)
 
         apply_rows(source, lo, hi, *tables, diff, emit)
 
 
+def row_base(face_ref, rate, diff):
+    cache = {}
+
+    def base(row):
+        kind = ((row + 8) // 16, {7: 1, 8: 2}.get(row % 16, 0))
+        if kind not in cache:
+            beside, south, north = row_faces(face_ref, row)
+            cache[kind] = rate + diff * (beside + (south + north))
+        return cache[kind]
+
+    return base
+
+
 def first_kernel(
-    pred_ref, prev_ref, row1_ref, row2_ref, col1_ref, col2_ref, where_ref, face_ref, stencil_ref,
-    param_ref, block_ref, state_ref, p0_ref, p1_ref, p2_ref, p3_ref, gram_ref, own_ref, old_ref,
-    diag_ref,
+    own_ref, col1_ref, col2_ref, face_ref, stencil_ref, param_ref, block_ref,
+    state_ref, p0_ref, p1_ref, p2_ref, p3_ref, gram_ref, old_ref, diag_ref, packed_ref,
 ):
-    owner = where_ref[1]
+    _, owner = position()
     even_owner, has_left, has_right = owner % 2 == 0, owner > 0, owner < OWNERS - 1
-    rows_ref = (row1_ref, row2_ref)
-    own_ref[:, SPECIES:24, :] = jnp.zeros((2 * TILES * COLS_DEV, 24 - SPECIES, LANES), f32)
-    for which, patch_ref in enumerate((pred_ref, prev_ref)):
-        for k in range(TILES):
-            for c in range(COLS_DEV):
-                own_ref[(which * TILES + k) * COLS_DEV + c, 0:SPECIES, :] = tile_of(
-                    patch_ref, rows_ref, where_ref, which, k, c
-                )
+    blank = jnp.zeros((3, 8, LANES), f32)
     for which, target in enumerate((state_ref, old_ref)):
 
         def beside(at, which=which):
-            first, second = (ref[which, at].reshape(3, 8, LANES) for ref in (col1_ref, col2_ref))
+            first, second = (
+                get_tile(ref, which * MSG + at).reshape(3, 8, LANES) for ref in (col1_ref, col2_ref)
+            )
             left, right = jnp.where(even_owner, second, first), jnp.where(even_owner, first, second)
             return jnp.where(has_left, left, 0.0), jnp.where(has_right, right, 0.0)
 
@@ -258,35 +386,34 @@
             if k % 2 == 0:
                 far_left, far_right = beside(TILES + k // 2)
             left, right = beside(k)
-            own = [
-                own_ref[(which * TILES + k) * COLS_DEV + c].reshape(3, 8, LANES)
-                for c in range(COLS_DEV)
-            ]
-            tiles = [
-                far_left if k % 2 else roll(far_left, 8),
-                roll(left, 16),
-                roll(own[0], 32),
-                roll(own[1], 48),
-                roll(own[2], 64),
-                roll(right, 80),
-                roll(far_right, 88 if k % 2 else 96),
-                jnp.zeros((3, 8, LANES), f32),
-            ]
-            for a, row in swap_blocks(tiles, range(8)).items():
-                target[k * 8 + a] = row
+            tiles = mix_blocks(
+                [
+                    far_left if k % 2 else roll(far_left, 8),
+                    roll(left, 16),
+                    blank,
+                    blank,
+                    blank,
+                    roll(right, 80),
+                    roll(far_right, 88 if k % 2 else 96),
+                    blank,
+                ]
+            )
+            for a in range(8):
+                tile = tiles[-a % 8] + own_ref[which, k * 8 + (-a % 8)]
+                target[k * 8 + a] = roll(tile, -16 * a) if a else tile
     rate, diff, decay = param_ref[0], param_ref[1], param_ref[2]
     tables = (block_ref[...], stencil_ref, face_ref)
-    dots = Dots()
+    dots = Dots(packed_ref)
+    base_of = row_base(face_ref, rate, diff)
 
     def emit(row, faces, rest):
         u = state_ref[row]
-        base = rate + diff * (faces[0] + (faces[1] + faces[2]))
+        base = base_of(row)
         cubic = decay * (u * u)
         new = (base + cubic) * u - rate * old_ref[row] - rest
         diag_ref[row] = (base - THETA / SIGMA) + 3.0 * cubic
         p0_ref[row] = new
-        if OWN_LO <= row < OWN_HI:
-            dots.add((0, 0), new * new)
+        dots.add(0, row, new)
 
     apply_rows(state_ref, 2, 78, *tables, diff, emit)
     krylov((p0_ref, p1_ref, p2_ref), diag_ref, tables, diff, dots, 6, p3_ref)
@@ -359,13 +486,14 @@
 
 def second_kernel(
     parts_ref, state_ref, p0_ref, p1_ref, p2_ref, p3_ref, face_ref, stencil_ref, param_ref,
-    block_ref, next_ref, q0_ref, q1_ref, q2_ref, gram_ref, diag_ref,
+    block_ref, next_ref, q0_ref, q1_ref, q2_ref, gram_ref, diag_ref, packed_ref,
 ):
     c0, c1, c2 = combine(parts_ref)
     shift = THETA / SIGMA
     rate, diff, decay = param_ref[0], param_ref[1], param_ref[2]
     tables = (block_ref[...], stencil_ref, face_ref)
-    dots = Dots()
+    dots = Dots(packed_ref)
+    base_of = row_base(face_ref, rate - shift, diff)
     a0, a1, a2 = 1.0 + shift * c0, c0 + shift * c1, c1 + shift * c2
     triple = 3.0 * decay
     for row in range(5, 75):
@@ -373,14 +501,11 @@
         d = c0 * p0 + c1 * p1 + c2 * p2
         linear = (a0 * p0 + a1 * p1) + (a2 * p2 + c2 * p3_ref[row])
         new = linear + (decay * (d * d)) * (3.0 * u + d)
-        beside, south, north = row_faces(face_ref, row)
         u = u + d
-        base = rate + diff * (beside + (south + north)) - shift
-        diag_ref[row] = base + triple * (u * u)
+        diag_ref[row] = base_of(row) + triple * (u * u)
         next_ref[row] = u
         q0_ref[row] = new
-        if OWN_LO <= row < OWN_HI:
-            dots.add((0, 0), new * new)
+        dots.add(0, row, new)
     krylov((q0_ref, q1_ref, q2_ref), diag_ref, tables, diff, dots, 3, None)
     dots.write(gram_ref)
 
@@ -388,53 +513,34 @@
 SLOTS = PATCH_DEV + 2 * MOVE_CAP
 
 
-def last_kernel(
-    parts_ref, next_ref, q0_ref, q1_ref, q2_ref, owner_ref, where_ref, out_ref, low_ref, high_ref
-):
-    band, owner = where_ref[0], where_ref[1]
+def last_kernel(parts_ref, next_ref, q0_ref, q1_ref, q2_ref, flag_ref, out_ref, low_ref, high_ref):
     c0, c1, c2 = combine(parts_ref)
     slots_ref = (low_ref, high_ref)
-    for ref in slots_ref:
-        ref[PATCH_DEV * 24 : SLOTS * 24, :] = jnp.zeros((2 * MOVE_CAP * 24, LANES), f32)
-    base = (band * OWNERS + owner) * PATCH_DEV
-    stays = [owner_ref[base + s] == owner for s in range(PATCH_DEV)]
-    left_base = jnp.maximum(base - PATCH_DEV, 0)
-    right_base = jnp.minimum(base + PATCH_DEV, BANDS * OWNERS * PATCH_DEV - PATCH_DEV)
-    left_in = [
-        (owner > 0) & (owner_ref[left_base + r * COLS_DEV + COLS_DEV - 1] == owner)
-        for r in range(ROWS_DEV)
-    ]
-    right_in = [
-        (owner < OWNERS - 1) & (owner_ref[right_base + r * COLS_DEV] == owner)
-        for r in range(ROWS_DEV)
-    ]
+    blank = jnp.zeros((3, 8, LANES), f32)
+
+    def put(half, slot, tile):
+        slots_ref[half][slot * 24 : slot * 24 + 24, :] = tile.reshape(24, LANES)
+
+    arrived = {}
     for r in range(ROWS_DEV):
-        halves = []
         for half in range(2):
             rows = []
             for a in range(8):
                 row = OWN_LO + r * 16 + half * 8 + a
                 value = next_ref[row] + (c0 * q0_ref[row] + c1 * q1_ref[row] + c2 * q2_ref[row])
                 rows.append(roll(value, 16 * a) if a else value)
-            halves.append(
-                {g: t.reshape(24, LANES) for g, t in swap_blocks(rows, range(1, 6)).items()}
-            )
-        for c in range(COLS_DEV):
-            slot = r * COLS_DEV + c
-            for half in range(2):
-                slots_ref[half][slot * 24 : slot * 24 + 24, :] = jnp.where(
-                    stays[slot], halves[half][2 + c], 0.0
-                )
-        for moving, g, first in ((left_in, 1, PATCH_DEV), (right_in, 5, PATCH_DEV + MOVE_CAP)):
-            rank = jnp.int32(0)
-            for before in range(r):
-                rank = rank + moving[before].astype(jnp.int32)
-            for place in range(min(r + 1, MOVE_CAP)):
-
-                @pl.when(moving[r] & (rank == place))
-                def _(slot=first + place, g=g):
-                    for half in range(2):
-                        slots_ref[half][slot * 24 : slot * 24 + 24, :] = halves[half][g]
+            tiles = swap_blocks(rows, range(1, 6))
+            for c in range(COLS_DEV):
+                slot = r * COLS_DEV + c
+                put(half, slot, jnp.where(flag_ref[slot] == 1, tiles[2 + c], 0.0))
+            for side, g in enumerate((1, 5)):
+                for at, (row_of, m) in enumerate(ARRIVALS):
+                    if row_of == r:
+                        flag = flag_ref[STAYS + side * len(ARRIVALS) + at] == 1
+                        key = (half, PATCH_DEV + side * MOVE_CAP + m)
+                        arrived[key] = jnp.where(flag, tiles[g], arrived.get(key, blank))
+    for (half, slot), tile in arrived.items():
+        put(half, slot, tile)
 
     for s in range(SPECIES):
         for part in range(SLOTS // 8):
@@ -475,11 +581,17 @@
 
 
 def per_device(previous, predicted, new_owner, levels, diffusion, decay, reaction):
-    where = jnp.stack([lax.axis_index("grp"), lax.axis_index(PATCH)]).astype(jnp.int32)
     prev, pred = (x.reshape(PATCH_DEV * SPECIES * 2, LANES) for x in (previous, predicted))
     shape = jax.ShapeDtypeStruct
-    strip = shape((2, COLS_DEV, 24, LANES), f32)
-    strips = call(row_strip_kernel, (strip, strip), [vm(), vm(), sm()])(pred, prev, where)
+    strip = shape((dense(ROW_TILES), LANES), f32)
+    local = shape((INPUT_ROWS + 8, LANES), f32)
+    far = pl.BlockSpec(memory_space=pltpu.HBM)
+    pred, prev, *strips = call(
+        row_strip_kernel,
+        (local, local, strip, strip),
+        [far, far],
+        [pltpu.SemaphoreType.DMA((6,))],
+    )(pred, prev)
     row1, row2 = (exchanged(x, "grp", odd) for odd, x in enumerate(strips))
 
     rate = jnp.where(jnp.arange(24) < SPECIES - 1, 4.0, 0.0)
@@ -499,35 +611,44 @@
 
     blocks = jnp.concatenate([two(high), two(high), two(low)], axis=1)
 
-    faces, stencil = call(
-        face_kernel, (shape((6, 4, 8, LANES), f32), shape((6, 2 * LANES, LANES), bf16)), [sm(), sm()]
-    )(levels.reshape(-1), where)
-    message = shape((2, MSG, 24, LANES), f32)
-    messages = call(pack_kernel, (message, message), [vm()] * 4 + [sm()])(
-        pred, prev, row1, row2, where
-    )
+    faces, stencil, flags = call(
+        face_kernel,
+        (
+            shape((6, 4, 8, LANES), f32),
+            shape((6, 2 * LANES, LANES), bf16),
+            shape((FLAGS, 8, LANES), jnp.int32),
+        ),
+        [sm(), sm()],
+    )(levels.reshape(-1), new_owner.reshape(-1))
+    message = shape((dense(COL_TILES), LANES), f32)
+    messages = call(pack_kernel, (message, message), [vm()] * 4)(pred, prev, row1, row2)
     col1, col2 = (exchanged(x, PATCH, odd) for odd, x in enumerate(messages))
     state = shape(STATE, f32)
     gram = shape((1, LANES), f32)
+    own = call(
+        own_kernel,
+        shape((2,) + STATE, f32),
+        [vm()] * 4,
+        [pltpu.VMEM((2 * TILES * COLS_DEV, 24, LANES), f32)],
+    )(pred, prev, row1, row2)
     u0, p0, p1, p2, p3, gram1 = call(
         first_kernel,
         (state,) * 5 + (gram,),
-        [vm()] * 6 + [sm()] + [vm()] * 4,
-        [
-            pltpu.VMEM((2 * TILES * COLS_DEV, 24, LANES), f32),
-            pltpu.VMEM(STATE, f32),
-            pltpu.VMEM(STATE, f32),
-        ],
-    )(pred, prev, row1, row2, col1, col2, where, faces, stencil, params, blocks)
+        [vm()] * 7,
+        [pltpu.VMEM(STATE, f32), pltpu.VMEM(STATE, f32), pltpu.VMEM(PACKED, f32)],
+    )(own, col1, col2, faces, stencil, params, blocks)
     u1, q0, q1, q2, gram2 = call(
-        second_kernel, (state,) * 4 + (gram,), [vm()] * 10, [pltpu.VMEM(STATE, f32)]
+        second_kernel,
+        (state,) * 4 + (gram,),
+        [vm()] * 10,
+        [pltpu.VMEM(STATE, f32), pltpu.VMEM(PACKED, f32)],
     )(summed(gram1), u0, p0, p1, p2, p3, faces, stencil, params, blocks)
     out = call(
         last_kernel,
         shape((SPECIES, SLOTS, 2 * LANES), f32),
-        [vm()] * 5 + [sm(), sm()],
+        [vm()] * 6,
         [pltpu.VMEM((SLOTS * 24, LANES), f32)] * 2,
-    )(summed(gram2), u1, q0, q1, q2, new_owner.reshape(-1), where)
+    )(summed(gram2), u1, q0, q1, q2, flags)
     return jnp.transpose(out, (1, 0, 2))[None, None]
 
 

time: 67.3 us -> 62.2 us (0.924)
  blocking collectives: 21.6 us -> 34.4 us
  waiting for transfers between devices: 15.7 us -> 4.41 us
  starting transfers between devices: 11.9 us -> 7.02 us
  Pallas kernels: 11.5 us -> 9.56 us
    all_to_all x1 -> x2, blocking collectives: 21.6 us -> 34.4 us  [summed(): return lax.all_to_all(spread_out, EVERY, 0, 0).reshape(DEVICES, LANES)]
    all_to_all x1 -> x0, waiting for transfers between devices: 9.7 us -> none  [summed(): return lax.all_to_all(spread_out, EVERY, 0, 0).reshape(DEVICES, LANES)]
    all_to_all x1 -> x0, starting transfers between devices: 3.96 us -> none  [summed(): return lax.all_to_all(spread_out, EVERY, 0, 0).reshape(DEVICES, LANES)]
    pallas_call x4 -> x5, Pallas kernels: 7.91 us -> 5.78 us  [the longest x1 3.26 us: per_device(): call(first_kernel, (state,) * 5 + (gram,), [vm()] * 7, [pltpu.VMEM(STATE,...]
    ppermute x4, waiting for transfers between devices: 6.01 us -> 4.41 us  [exchanged(): lax.ppermute(x, axis, [((i + odd) % count, m % count) for i, m in enumera...]
    unnamed x24 -> x6, local copies, waits for them, and re-layouts: 4.86 us -> 3.57 us
    ppermute x4, starting transfers between devices: 7.89 us -> 7.02 us  [exchanged(): lax.ppermute(x, axis, [((i + odd) % count, m % count) for i, m in enumera...]
    div x1, other arithmetic: 0.01 us -> 0.71 us  [per_device(): matrix = jnp.pad(reaction / SIGMA, (pad, pad))]
  transfers between devices with their start and end apart: 5 -> 4, of which waited for: 3 -> 1; matrix products, arithmetic and copies ran while one was open for 1% -> 7% of each run, Pallas kernels for 1% -> 2%
where the time goes in v3:
time: 62.2 us; the launch traced here: 61.8 us
  blocking collectives  34.4 us (55%)
  Pallas kernels  9.56 us (15%)
  starting transfers between devices  7.02 us (11%)
  local copies, waits for them, and re-layouts  5.48 us (9%)
  waiting for transfers between devices  4.41 us (7%)
  other arithmetic  0.83 us (1%)
    all_to_all x2, blocking collectives, summed(): return lax.all_to_all(spread_out, EVERY, 0, 0).reshape(DEVICES, LANES)  34.4 us
    ppermute x4, starting transfers between devices, exchanged(): lax.ppermute(x, axis, [((i + odd) % count, m % count) for i, m in enumera...  7.02 us
    ppermute x4, waiting for transfers between devices, exchanged(): lax.ppermute(x, axis, [((i + odd) % count, m % count) for i, m in enumera...  4.41 us
    unnamed x6, local copies, waits for them, and re-layouts  3.57 us
    pallas_call x1, Pallas kernels, per_device(): call(first_kernel, (state,) * 5 + (gram,), [vm()] * 7, [pltpu.VMEM(STATE,...  3.26 us
    pallas_call x1, Pallas kernels, per_device(): call(second_kernel, (state,) * 4 + (gram,), [vm()] * 10, [pltpu.VMEM(STAT...  2.74 us
    pallas_call x1, Pallas kernels, per_device(): call(last_kernel, shape((SPECIES, SLOTS, 2 * LANES), f32), [vm()] * 6, [p...  1.37 us
  transfers between devices with their start and end apart: 4, of which 1 were waited for; matrix products, arithmetic and copies ran while one was open for 7% of the time, Pallas kernels for 2%

profile of v3, /device:TPU:1, one launch (start us, length us, event | category | flops | bytes accessed | tf_op | source)
XLA Modules:
  0.0 61.8 jit_solution(11622460828591570319)
XLA Ops:
  0.0 0.9 %copy-done = f32[1,1,12,21,256]{4,1,3,2,0:T(1,128)S(1)} copy-done((f32[1,1,12,21,256]{4,1,3,2,0:T(1,128)S(1)}, f32[1,1,12,21,256]{4,1,3,2,0:T(1,128)}, u32[]{:S(2)}) %copy-start) | copy-done | bytes 258072
  0.9 0.0 copy-start.1
  1.0 0.9 %copy-done.1 = f32[1,1,12,21,256]{4,1,3,2,0:T(1,128)S(1)} copy-done((f32[1,1,12,21,256]{4,1,3,2,0:T(1,128)S(1)}, f32[1,1,12,21,256]{4,1,3,2,0:T(1,128)}, u32[]{:S(2)}) %copy-start.1) | copy-done | bytes 258072
  1.9 0.7 %shard_map.73 = (f32[512,128]{1,0:T(8,128)S(1)}, f32[512,128]{1,0:T(8,128)S(1)}, f32[136,128]{1,0:T(8,128)S(1)}, f32[136,128]{1,0:T(8,128)S(1)}) custom-call(f32[504,128]{1,0:T(8,128)S(1)} %bitcast.11, f32[504,128]{1,0:T(8,128)S(1)} %bitcast.12), custom_call_target="tpu_custom_call" | custom-call | tf_op jit(solution)/shard_map/pallas_call | solution.py:589
  2.6 2.2 %collective-permute-start = (f32[136,128]{1,0:T(8,128)S(1)}, f32[136,128]{1,0:T(8,128)S(1)}, u32[]{:S(2)}, u32[]{:S(2)}) collective-permute-start(f32[136,128]{1,0:T(8,128)S(1)} %get-tuple-element.27), channel_id=1, source_target_pairs={{0,1},{1,0},{2,3},{3,2},{4,5},{5,4},{6,7},{7,6},{8,9},{9,8},{10,11... | collective-permute-start | bytes 208904 | tf_op jit(solution)/shard_map/ppermute | solution.py:575
  4.8 1.9 %collective-permute-start.1 = (f32[136,128]{1,0:T(8,128)S(1)}, f32[136,128]{1,0:T(8,128)S(1)}, u32[]{:S(2)}, u32[]{:S(2)}) collective-permute-start(f32[136,128]{1,0:T(8,128)S(1)} %get-tuple-element.28), channel_id=1, source_target_pairs={{1,2},{2,1},{3,0},{0,3},{5,6},{6,5},{7,4},{4,7},{9,10},{10,9},{11,... | collective-permute-start | bytes 208904 | tf_op jit(solution)/shard_map/ppermute | solution.py:575
  6.7 0.7 %pad.15 = f32[24]{0:T(128)S(1)} pad(f32[21]{0:T(128)} %param.11, f32[]{:T(128)} %constant.14.clone.1), padding=0_3 | pad | bytes 184 | tf_op jit(solution)/shard_map/jit(_pad)/pad | solution.py:599
  7.4 0.7 %pad.16 = f32[24]{0:T(128)S(1)} pad(f32[21]{0:T(128)} %param.12, f32[]{:T(128)} %constant.14.clone.1), padding=0_3 | pad | bytes 184 | tf_op jit(solution)/shard_map/jit(_pad)/pad | solution.py:599
  8.0 0.1 stack.11
  8.1 0.1 stack.10
  8.2 0.7 %broadcast_multiply_fusion = f32[21,21]{1,0:T(8,128)S(1)} fusion(f32[21,21]{1,0:T(8,128)} %param.13), kind=kLoop, calls=%fused_computation.15 | loop fusion | flops 441 | bytes 3528 | tf_op jit(solution)/shard_map/div | solution.py:601
  8.9 0.8 %copy.11 = s32[4,32,12]{2,1,0:T(8,128)S(1)} copy(s32[4,32,12]{1,0,2:T(4,128)} %param.9) | data formatting | bytes 12288 | tf_op args[2]
  9.8 0.1 reshape.67.owners_ref
  9.9 0.8 %copy.10 = s32[4,32,12]{2,1,0:T(8,128)S(1)} copy(s32[4,32,12]{1,0,2:T(4,128)} %param.10) | data formatting | bytes 12288 | tf_op args[3]
  10.7 0.1 reshape.66.levels_ref
  10.8 1.0 %shard_map.76 = (f32[6,4,8,128]{3,2,1,0:T(8,128)S(1)}, bf16[6,256,128]{2,1,0:T(8,128)(2,1)S(1)}, s32[26,8,128]{2,1,0:T(8,128)S(1)}) custom-call(s32[1536]{0:T(1024)S(1)} %reshape.66.levels_ref, s32[1536]{0:T(1024)S(1)} %reshape.67.owners_ref), custom_call_target="tpu_custom_call" | custom-call | tf_op jit(solution)/shard_map/pallas_call | solution.py:614
  11.9 0.0 collective-permute-done.row1_ref
  11.9 0.0 collective-permute-done.1.row2_ref
  11.9 0.2 shard_map.75
  12.0 1.3 %collective-permute-start.2 = (f32[640,128]{1,0:T(8,128)S(1)}, f32[640,128]{1,0:T(8,128)S(1)}, u32[]{:S(2)}, u32[]{:S(2)}) collective-permute-start(f32[640,128]{1,0:T(8,128)S(1)} %get-tuple-element.29), channel_id=1, source_target_pairs={{0,4},{4,0},{8,12},{12,8},{16,20},{20,16},{24,28},{28,24},{32,36},... | collective-permute-start | bytes 983048 | tf_op jit(solution)/shard_map/ppermute | solution.py:575
  13.4 1.6 %collective-permute-start.3 = (f32[640,128]{1,0:T(8,128)S(1)}, f32[640,128]{1,0:T(8,128)S(1)}, u32[]{:S(2)}, u32[]{:S(2)}) collective-permute-start(f32[640,128]{1,0:T(8,128)S(1)} %get-tuple-element.30), channel_id=1, source_target_pairs={{4,8},{8,4},{12,16},{16,12},{20,24},{24,20},{28,32},{32,28},{36,40... | collective-permute-start | bytes 983048 | tf_op jit(solution)/shard_map/ppermute | solution.py:575
  15.0 0.1 fusion.10
  15.1 0.1 fusion.7.block_ref
  15.2 0.3 shard_map.74.own_ref
  15.4 0.0 collective-permute-done.2.col1_ref
  15.5 4.4 %collective-permute-done.3.col2_ref = f32[640,128]{1,0:T(8,128)S(1)} collective-permute-done((f32[640,128]{1,0:T(8,128)S(1)}, f32[640,128]{1,0:T(8,128)S(1)}, u32[]{:S(2)}, u32[]{:S(2)}) %collective-permute-start.3) | collective-permute-done | bytes 327712 | tf_op jit(solution)/shard_map/ppermute | solution.py:575
  19.9 0.1 broadcast_in_dim.36.param_ref
  19.9 3.3 %shard_map.77 = (f32[80,3,8,128]{3,2,1,0:T(8,128)S(1)}, f32[80,3,8,128]{3,2,1,0:T(8,128)S(1)}, f32[80,3,8,128]{3,2,1,0:T(8,128)S(1)}, f32[80,3,8,128]{3,2,1,0:T(...) custom-call(f32[2,80,3,8,128]{4,3,2,1,0:T(8,128)S(1)} %shard_map.74.own_ref, ...), custom_call_target="tpu_custom_call" | custom-call | tf_op jit(solution)/shard_map/pallas_call | solution.py:634
  23.2 20.7 %all_to_all.10 = f32[128,1,128]{2,1,0:T(1,128)S(1)} all-to-all(f32[128,1,128]{2,1,0:T(1,128)S(1)} %broadcast_in_dim.38), channel_id=1, replica_groups=mesh['patch_0'=4,'patch_1'=4,'patch_2'=2,'grp'=4] {'patch_0','patch_1','..., dimensions={0} | all-to-all | bytes 131072 | tf_op jit(solution)/shard_map/all_to_all | solution.py:580
  44.0 2.7 %shard_map.78 = (f32[80,3,8,128]{3,2,1,0:T(8,128)S(1)}, f32[80,3,8,128]{3,2,1,0:T(8,128)S(1)}, f32[80,3,8,128]{3,2,1,0:T(8,128)S(1)}, f32[80,3,8,128]{3,2,1,0:T(8,128)S(1)}, f32[1,128]{1,0:T(1,128)S(1)}) custom-call(f32[128,128]{1,0:T(8,128)S(1)} %bitcast.9, f32[80,3,8,128]{3,2,1,0:T(8,128)S(1)} %get-tuple-element.34.state_ref, ...), custom_call_target="tpu_custom_call" | custom-call | tf_op jit(solution)/shard_map/pallas_call | solution.py:640
  46.8 13.7 %all_to_all.11 = f32[128,1,128]{2,1,0:T(1,128)S(1)} all-to-all(f32[128,1,128]{2,1,0:T(1,128)S(1)} %broadcast_in_dim.40), channel_id=1, replica_groups=mesh['patch_0'=4,'patch_1'=4,'patch_2'=2,'grp'=4] {'patch_0','patch_1','..., dimensions={0} | all-to-all | bytes 131072 | tf_op jit(solution)/shard_map/all_to_all | solution.py:580
  60.5 1.4 %shard_map.79 = f32[21,16,256]{2,1,0:T(8,128)} custom-call(f32[128,128]{1,0:T(8,128)S(1)} %bitcast.10, f32[80,3,8,128]{3,2,1,0:T(8,128)S(1)} %get-tuple-element.40.next_ref, f32[80,3,8,128]{3,2,1,0:T(8,128)S(1)} %get-tuple-element.41.q0_ref, f32[80,3,8,128]{3,2,1,0:T(8,128)S(1)} %get-tuple-element.42.q1_ref, f32[80,3,8,128]{3,2,1,0:T(8,128)S(1)} %get-tuple-element.43.q2_ref, ...), custom_call_target="tpu_custom_call" | custom-call | tf_op jit(solution)/shard_map/pallas_call | solution.py:646
  (6 shorter events, 0.1 us)
Async XLA Ops:
  0.0 0.9 %copy-start = (f32[1,1,12,21,256]{4,1,3,2,0:T(1,128)S(1)}, f32[1,1,12,21,256]{4,1,3,2,0:T(1,128)}, u32[]{:S(2)}) copy-start(f32[1,1,12,21,256]{4,1,3,2,0:T(1,128)} %param.8) | copy-start | bytes 774148
  0.9 0.9 %copy-start.1 = (f32[1,1,12,21,256]{4,1,3,2,0:T(1,128)S(1)}, f32[1,1,12,21,256]{4,1,3,2,0:T(1,128)}, u32[]{:S(2)}) copy-start(f32[1,1,12,21,256]{4,1,3,2,0:T(1,128)} %param.7) | copy-start | bytes 774148
  2.6 9.3 %collective-permute-start = (f32[136,128]{1,0:T(8,128)S(1)}, f32[136,128]{1,0:T(8,128)S(1)}, u32[]{:S(2)}, u32[]{:S(2)}) collective-permute-start(f32[136,128]{1,0:T(8,128)S(1)} %get-tuple-element.27), channel_id=1, source_target_pairs={{0,1},{1,0},{2,3},{3,2},{4,5},{5,4},{6,7},{7,6},{8,9},{9,8},{10,11... | collective-permute-start | bytes 208904 | tf_op jit(solution)/shard_map/ppermute | solution.py:575
  4.8 7.1 %collective-permute-start.1 = (f32[136,128]{1,0:T(8,128)S(1)}, f32[136,128]{1,0:T(8,128)S(1)}, u32[]{:S(2)}, u32[]{:S(2)}) collective-permute-start(f32[136,128]{1,0:T(8,128)S(1)} %get-tuple-element.28), channel_id=1, source_target_pairs={{1,2},{2,1},{3,0},{0,3},{5,6},{6,5},{7,4},{4,7},{9,10},{10,9},{11,... | collective-permute-start | bytes 208904 | tf_op jit(solution)/shard_map/ppermute | solution.py:575
  12.0 3.4 %collective-permute-start.2 = (f32[640,128]{1,0:T(8,128)S(1)}, f32[640,128]{1,0:T(8,128)S(1)}, u32[]{:S(2)}, u32[]{:S(2)}) collective-permute-start(f32[640,128]{1,0:T(8,128)S(1)} %get-tuple-element.29), channel_id=1, source_target_pairs={{0,4},{4,0},{8,12},{12,8},{16,20},{20,16},{24,28},{28,24},{32,36},... | collective-permute-start | bytes 983048 | tf_op jit(solution)/shard_map/ppermute | solution.py:575
  13.4 6.5 %collective-permute-start.3 = (f32[640,128]{1,0:T(8,128)S(1)}, f32[640,128]{1,0:T(8,128)S(1)}, u32[]{:S(2)}, u32[]{:S(2)}) collective-permute-start(f32[640,128]{1,0:T(8,128)S(1)} %get-tuple-element.30), channel_id=1, source_target_pairs={{4,8},{8,4},{12,16},{16,12},{20,24},{24,20},{28,32},{32,28},{36,40... | collective-permute-start | bytes 983048 | tf_op jit(solution)/shard_map/ppermute | solution.py:575

commit v4 on v3

--- a/solution.py
+++ b/solution.py
@@ -65,19 +65,18 @@
 
 
 def write_flags(owners_ref, flag_ref, band, owner):
-    base = (band * OWNERS + owner) * PATCH_DEV
-
     def put(at, condition):
         flag_ref[at] = jnp.full((8, LANES), jnp.where(condition, 1, 0), jnp.int32)
 
     for slot in range(PATCH_DEV):
-        put(slot, owners_ref[base + slot] == owner)
-    left_base = jnp.maximum(base - PATCH_DEV, 0)
-    right_base = jnp.minimum(base + PATCH_DEV, (BANDS * OWNERS - 1) * PATCH_DEV)
-    sides = ((owner > 0, left_base + COLS_DEV - 1), (owner < OWNERS - 1, right_base))
-    for side, (exists, first) in enumerate(sides):
+        put(slot, owners_ref[slot, band, owner] == owner)
+    sides = (
+        (owner > 0, jnp.maximum(owner - 1, 0), COLS_DEV - 1),
+        (owner < OWNERS - 1, jnp.minimum(owner + 1, OWNERS - 1), 0),
+    )
+    for side, (exists, beside, column) in enumerate(sides):
         moving = [
-            jnp.where(exists & (owners_ref[first + r * COLS_DEV] == owner), 1, 0)
+            jnp.where(exists & (owners_ref[r * COLS_DEV + column, band, beside] == owner), 1, 0)
             for r in range(ROWS_DEV)
         ]
         for at, (r, m) in enumerate(ARRIVALS):
@@ -87,22 +86,57 @@
             put(STAYS + side * len(ARRIVALS) + at, (moving[r] == 1) & (rank == m))
 
 
-def face_kernel(levels_ref, owners_ref, face_ref, stencil_ref, flag_ref):
+def write_params(diffusion_ref, decay_ref, param_ref):
+    row = lax.broadcasted_iota(jnp.int32, (8, LANES), 0)
+    for part in range(3):
+        rate = jnp.where(row + 8 * part < SPECIES - 1, 4.0, 0.0)
+        diff = decay = jnp.zeros((8, LANES), f32)
+        for i in range(min(8, SPECIES - 8 * part)):
+            diff = jnp.where(row == i, diffusion_ref[8 * part + i], diff)
+            decay = jnp.where(row == i, decay_ref[8 * part + i], decay)
+        for at, value in enumerate((rate, diff, decay)):
+            param_ref[at, part] = value * (1.0 / SIGMA)
+
+
+def write_blocks(reaction_ref, block_ref, wide_ref):
+    wide_ref[...] = jnp.zeros((24, LANES), f32)
+    wide_ref[0:SPECIES, 0:SPECIES] = reaction_ref[...] * (1.0 / SIGMA)
+    matrix = wide_ref[...]
+    high = matrix.astype(bf16).astype(f32)
+    low = matrix - high
+    tail = lax.broadcasted_iota(jnp.int32, (24, LANES), 1) < 16
+    upper = (high + roll(high, 48)) + roll(low, 96)
+    lower = roll(high + roll(high, 48), 24)
+    turned = roll(low, 120)
+    block_ref[:, 0:LANES] = jnp.concatenate(
+        [upper, lower + jnp.where(tail, 0.0, turned)], axis=0
+    ).astype(bf16)
+    block_ref[:, LANES : 2 * LANES] = jnp.concatenate(
+        [jnp.zeros((24, LANES), f32), jnp.where(tail, turned, 0.0)], axis=0
+    ).astype(bf16)
+
+
+def table_kernel(
+    levels_ref, owners_ref, diffusion_ref, decay_ref, reaction_ref,
+    face_ref, stencil_ref, flag_ref, param_ref, block_ref, wide_ref,
+):
     band, owner = position()
     write_flags(owners_ref, flag_ref, band, owner)
+    write_params(diffusion_ref, decay_ref, param_ref)
+    write_blocks(reaction_ref, block_ref, wide_ref)
     lane_group = lanes_of() // 16
     kappas = []
     for idx in range(6):
         patch_row = band * ROWS_DEV + idx - 1
         row_in = (patch_row >= 0) & (patch_row < BANDS * ROWS_DEV)
         row_safe = jnp.clip(patch_row, 0, BANDS * ROWS_DEV - 1)
-        row_base = (row_safe // ROWS_DEV) * (OWNERS * PATCH_DEV) + (row_safe % ROWS_DEV) * COLS_DEV
+        near_band, near_row = row_safe // ROWS_DEV, row_safe % ROWS_DEV
         kap = jnp.zeros((8, LANES), f32)
         for g in range(8):
             near_owner = owner + (g - 2 - (g - 2) % COLS_DEV) // COLS_DEV
             inside = row_in & (near_owner >= 0) & (near_owner < OWNERS)
             safe = jnp.clip(near_owner, 0, OWNERS - 1)
-            level = levels_ref[row_base + safe * PATCH_DEV + (g - 2) % COLS_DEV]
+            level = levels_ref[near_row * COLS_DEV + (g - 2) % COLS_DEV, near_band, safe]
             value = jnp.where(level == 0, 1.0, jnp.where(level == 1, 4.0, 16.0))
             value = jnp.where(inside, value, 0.0).astype(f32)
             kap = jnp.where(lane_group == g, value, kap)
@@ -402,7 +436,7 @@
                 tile = tiles[-a % 8] + own_ref[which, k * 8 + (-a % 8)]
                 target[k * 8 + a] = roll(tile, -16 * a) if a else tile
     rate, diff, decay = param_ref[0], param_ref[1], param_ref[2]
-    tables = (block_ref[...], stencil_ref, face_ref)
+    tables = (block_ref[:, 0:144], stencil_ref, face_ref)
     dots = Dots(packed_ref)
     base_of = row_base(face_ref, rate, diff)
 
@@ -491,7 +525,7 @@
     c0, c1, c2 = combine(parts_ref)
     shift = THETA / SIGMA
     rate, diff, decay = param_ref[0], param_ref[1], param_ref[2]
-    tables = (block_ref[...], stencil_ref, face_ref)
+    tables = (block_ref[:, 0:144], stencil_ref, face_ref)
     dots = Dots(packed_ref)
     base_of = row_base(face_ref, rate - shift, diff)
     a0, a1, a2 = 1.0 + shift * c0, c0 + shift * c1, c1 + shift * c2
@@ -569,10 +603,15 @@
     return pl.BlockSpec(memory_space=pltpu.SMEM)
 
 
+def in_hbm(x):
+    return pltpu.with_memory_space_constraint(x, pltpu.HBM)
+
+
 def exchanged(x, axis, odd):
     count = lax.axis_size(axis)
-    mates = [((i - odd) ^ 1) + odd for i in range(odd, count + odd)]
-    return lax.ppermute(x, axis, [((i + odd) % count, m % count) for i, m in enumerate(mates)])
+    mates = [((i - odd) ^ 1) + odd for i in range(count)]
+    pairs = [(i, m if 0 <= m < count else i) for i, m in enumerate(mates)]
+    return lax.ppermute(x, axis, pairs)
 
 
 def summed(gram):
@@ -591,38 +630,38 @@
         (local, local, strip, strip),
         [far, far],
         [pltpu.SemaphoreType.DMA((6,))],
-    )(pred, prev)
+    )(in_hbm(pred), in_hbm(prev))
     row1, row2 = (exchanged(x, "grp", odd) for odd, x in enumerate(strips))
 
-    rate = jnp.where(jnp.arange(24) < SPECIES - 1, 4.0, 0.0)
-    pad = (0, 24 - SPECIES)
-    params = jnp.stack([rate, jnp.pad(diffusion, pad), jnp.pad(decay, pad)]) / SIGMA
-    params = jnp.broadcast_to(params.astype(f32)[:, :, None], (3, 24, LANES)).reshape(3, 3, 8, LANES)
-    matrix = jnp.pad(reaction / SIGMA, (pad, pad))
-    rounded = lax.reduce_precision(matrix, 8, 7)
-    high = rounded.astype(bf16)
-    low = (matrix - rounded).astype(bf16)
-    none = jnp.zeros_like(high)
-
-    def two(x):
-        return jnp.concatenate(
-            [jnp.concatenate([x, none], axis=1), jnp.concatenate([none, x], axis=1)], axis=0
-        )
-
-    blocks = jnp.concatenate([two(high), two(high), two(low)], axis=1)
-
-    faces, stencil, flags = call(
-        face_kernel,
+    message = shape((dense(COL_TILES), LANES), f32)
+    messages = call(pack_kernel, (message, message), [vm()] * 4)(pred, prev, row1, row2)
+    inputs = (new_owner, levels, diffusion, decay, reaction)
+    messages, inputs = lax.optimization_barrier((tuple(messages), inputs))
+    new_owner, levels, diffusion, decay, reaction = inputs
+    col1, col2 = (exchanged(x, PATCH, odd) for odd, x in enumerate(messages))
+    faces, stencil, flags, params, blocks = call(
+        table_kernel,
         (
             shape((6, 4, 8, LANES), f32),
             shape((6, 2 * LANES, LANES), bf16),
             shape((FLAGS, 8, LANES), jnp.int32),
+            shape((3, 3, 8, LANES), f32),
+            shape((48, 2 * LANES), bf16),
         ),
-        [sm(), sm()],
-    )(levels.reshape(-1), new_owner.reshape(-1))
-    message = shape((dense(COL_TILES), LANES), f32)
-    messages = call(pack_kernel, (message, message), [vm()] * 4)(pred, prev, row1, row2)
-    col1, col2 = (exchanged(x, PATCH, odd) for odd, x in enumerate(messages))
+        [sm()] * 4 + [vm()],
+        [pltpu.VMEM((24, LANES), f32)],
+    )(
+        *(
+            in_hbm(x)
+            for x in (
+                levels.transpose(2, 0, 1),
+                new_owner.transpose(2, 0, 1),
+                diffusion,
+                decay,
+                reaction,
+            )
+        )
+    )
     state = shape(STATE, f32)
     gram = shape((1, LANES), f32)
     own = call(

time: 62.2 us -> 62.2 us (level)
  local copies, waits for them, and re-layouts: 5.48 us -> 0.09 us
  blocking collectives: 34.4 us -> 38.9 us
  Pallas kernels: 9.56 us -> 10.9 us
  starting transfers between devices: 7.02 us -> 8.36 us
  other arithmetic: 0.83 us -> 0 us
  waiting for transfers between devices: 4.41 us -> 3.66 us
    all_to_all x2, blocking collectives: 34.4 us -> 38.9 us  [summed(): return lax.all_to_all(spread_out, EVERY, 0, 0).reshape(DEVICES, LANES)]
    unnamed x6 -> x0, local copies, waits for them, and re-layouts: 3.57 us -> none
    ppermute x4, starting transfers between devices: 7.02 us -> 8.36 us  [exchanged(): return lax.ppermute(x, axis, pairs)]
    pad x2 -> x0, local copies, waits for them, and re-layouts: 1.32 us -> none  [the longest x1 0.66 us: per_device(): jnp.pad(diffusion, pad)]
    pallas_call x1, Pallas kernels: 1.05 us -> 1.88 us  [per_device(): call(table_kernel, (shape((6, 4, 8, LANES), f32), shape((6, 2 * LANES, LA...]
    ppermute x4, waiting for transfers between devices: 4.41 us -> 3.66 us  [exchanged(): return lax.ppermute(x, axis, pairs)]
    div x2 -> x0, other arithmetic: 0.72 us -> none  [the longest x1 0.71 us: per_device(): matrix = jnp.pad(reaction / SIGMA, (pad, pad))]
  transfers between devices with their start and end apart: 4 -> 4, of which waited for: 1 -> 2; matrix products, arithmetic and copies ran while one was open for 7% -> 0% of each run, Pallas kernels for 2% -> 4%
where the time goes in v4:
time: 62.2 us; the launch traced here: 61.9 us
  blocking collectives  38.9 us (63%)
  Pallas kernels  10.9 us (18%)
  starting transfers between devices  8.36 us (13%)
  waiting for transfers between devices  3.66 us (6%)
    all_to_all x2, blocking collectives, summed(): return lax.all_to_all(spread_out, EVERY, 0, 0).reshape(DEVICES, LANES)  38.9 us
    ppermute x4, starting transfers between devices, exchanged(): return lax.ppermute(x, axis, pairs)  8.36 us
    ppermute x4, waiting for transfers between devices, exchanged(): return lax.ppermute(x, axis, pairs)  3.66 us
    pallas_call x1, Pallas kernels, per_device(): call(first_kernel, (state,) * 5 + (gram,), [vm()] * 7, [pltpu.VMEM(STATE,...  3.27 us
    pallas_call x1, Pallas kernels, per_device(): call(second_kernel, (state,) * 4 + (gram,), [vm()] * 10, [pltpu.VMEM(STAT...  2.74 us
    pallas_call x1, Pallas kernels, per_device(): call(table_kernel, (shape((6, 4, 8, LANES), f32), shape((6, 2 * LANES, LA...  1.88 us
    pallas_call x1, Pallas kernels, per_device(): call(last_kernel, shape((SPECIES, SLOTS, 2 * LANES), f32), [vm()] * 6, [p...  1.37 us
  transfers between devices with their start and end apart: 4, of which 2 were waited for; matrix products, arithmetic and copies ran while one was open for 0% of the time, Pallas kernels for 4%

profile of v4, /device:TPU:1, one launch (start us, length us, event | category | flops | bytes accessed | tf_op | source)
XLA Modules:
  0.0 61.9 jit_solution(14897679913118436426)
XLA Ops:
  0.0 1.1 %shard_map.73 = (f32[512,128]{1,0:T(8,128)S(1)}, f32[512,128]{1,0:T(8,128)S(1)}, f32[136,128]{1,0:T(8,128)S(1)}, f32[136,128]{1,0:T(8,128)S(1)}) custom-call(f32[504,128]{1,0:T(8,128)} %bitcast.15, f32[504,128]{1,0:T(8,128)} %bitcast.16), custom_call_target="tpu_custom_call" | custom-call | tf_op jit(solution)/shard_map/pallas_call | solution.py:628
  1.2 2.2 %collective-permute-start = (f32[136,128]{1,0:T(8,128)S(1)}, f32[136,128]{1,0:T(8,128)S(1)}, u32[]{:S(2)}, u32[]{:S(2)}) collective-permute-start(f32[136,128]{1,0:T(8,128)S(1)} %get-tuple-element.36), channel_id=1, source_target_pairs={{0,1},{1,0},{2,3},{3,2},{4,5},{5,4},{6,7},{7,6},{8,9},{9,8},{10,11... | collective-permute-start | bytes 208904 | tf_op jit(solution)/shard_map/ppermute | solution.py:614
  3.4 0.7 %collective-permute-start.1 = (f32[136,128]{1,0:T(8,128)S(1)}, f32[136,128]{1,0:T(8,128)S(1)}, u32[]{:S(2)}, u32[]{:S(2)}) collective-permute-start(f32[136,128]{1,0:T(8,128)S(1)} %get-tuple-element.37), channel_id=1, source_target_pairs={{0,0},{1,2},{2,1},{3,3},{4,4},{5,6},{6,5},{7,7},{8,8},{9,10},{10,9... | collective-permute-start | bytes 208904 | tf_op jit(solution)/shard_map/ppermute | solution.py:614
  4.0 1.0 %collective-permute-done.row1_ref = f32[136,128]{1,0:T(8,128)S(1)} collective-permute-done((f32[136,128]{1,0:T(8,128)S(1)}, f32[136,128]{1,0:T(8,128)S(1)}, u32[]{:S(2)}, u32[]{:S(2)}) %collective-permute-start) | collective-permute-done | bytes 69664 | tf_op jit(solution)/shard_map/ppermute | solution.py:614
  5.1 0.0 collective-permute-done.1.row2_ref
  5.1 0.2 shard_map.75
  5.2 2.0 %collective-permute-start.2 = (f32[640,128]{1,0:T(8,128)S(1)}, f32[640,128]{1,0:T(8,128)S(1)}, u32[]{:S(2)}, u32[]{:S(2)}) collective-permute-start(f32[640,128]{1,0:T(8,128)S(1)} %get-tuple-element.40), channel_id=1, source_target_pairs={{0,4},{4,0},{8,12},{12,8},{16,20},{20,16},{24,28},{28,24},{32,36},... | collective-permute-start | bytes 983048 | tf_op jit(solution)/shard_map/ppermute | solution.py:614
  7.2 3.6 %collective-permute-start.3 = (f32[640,128]{1,0:T(8,128)S(1)}, f32[640,128]{1,0:T(8,128)S(1)}, u32[]{:S(2)}, u32[]{:S(2)}) collective-permute-start(f32[640,128]{1,0:T(8,128)S(1)} %get-tuple-element.41), channel_id=1, source_target_pairs={{0,0},{4,8},{8,4},{12,16},{16,12},{20,24},{24,20},{28,32},{32,28},... | collective-permute-start | bytes 983048 | tf_op jit(solution)/shard_map/ppermute | solution.py:614
  10.7 1.9 %shard_map.76 = (f32[6,4,8,128]{3,2,1,0:T(8,128)S(1)}, bf16[6,256,128]{2,1,0:T(8,128)(2,1)S(1)}, s32[26,8,128]{2,1,0:T(8,128)S(1)}, f32[3,3,8,128]{3,2,1,0:T(8,128)S(1)}, bf16[48,256]{1,0:T(8,128)(2,1)S(1)}) custom-call(s32[12,4,32]{2,1,0:T(4,128)} %bitcast.17, s32[12,4,32]{2,1,0:T(4,128)} %bitcast.18, f32[21]{0:T(128)} %diffusion_ref, f32[21]{0:T(128)} %decay_ref, ...), custom_call_target="tpu_custom_call" | custom-call | tf_op jit(solution)/shard_map/pallas_call | solution.py:642
  12.6 0.3 shard_map.74.own_ref
  12.9 0.0 collective-permute-done.2.col1_ref
  12.9 2.6 %collective-permute-done.3.col2_ref = f32[640,128]{1,0:T(8,128)S(1)} collective-permute-done((f32[640,128]{1,0:T(8,128)S(1)}, f32[640,128]{1,0:T(8,128)S(1)}, u32[]{:S(2)}, u32[]{:S(2)}) %collective-permute-start.3) | collective-permute-done | bytes 327712 | tf_op jit(solution)/shard_map/ppermute | solution.py:614
  15.6 3.3 %shard_map.77 = (f32[80,3,8,128]{3,2,1,0:T(8,128)S(1)}, f32[80,3,8,128]{3,2,1,0:T(8,128)S(1)}, f32[80,3,8,128]{3,2,1,0:T(8,128)S(1)}, f32[80,3,8,128]{3,2,1,0:T(...) custom-call(f32[2,80,3,8,128]{4,3,2,1,0:T(8,128)S(1)} %shard_map.74.own_ref, ...), custom_call_target="tpu_custom_call" | custom-call | tf_op jit(solution)/shard_map/pallas_call | solution.py:673
  18.9 25.2 %all_to_all.10 = f32[128,1,128]{2,1,0:T(1,128)S(1)} all-to-all(f32[128,1,128]{2,1,0:T(1,128)S(1)} %broadcast_in_dim.20), channel_id=1, replica_groups=mesh['patch_0'=4,'patch_1'=4,'patch_2'=2,'grp'=4] {'patch_0','patch_1','..., dimensions={0} | all-to-all | bytes 131072 | tf_op jit(solution)/shard_map/all_to_all | solution.py:619
  44.1 2.7 %shard_map.78 = (f32[80,3,8,128]{3,2,1,0:T(8,128)S(1)}, f32[80,3,8,128]{3,2,1,0:T(8,128)S(1)}, f32[80,3,8,128]{3,2,1,0:T(8,128)S(1)}, f32[80,3,8,128]{3,2,1,0:T(8,128)S(1)}, f32[1,128]{1,0:T(1,128)S(1)}) custom-call(f32[128,128]{1,0:T(8,128)S(1)} %bitcast.11, f32[80,3,8,128]{3,2,1,0:T(8,128)S(1)} %get-tuple-element.52.state_ref, ...), custom_call_target="tpu_custom_call" | custom-call | tf_op jit(solution)/shard_map/pallas_call | solution.py:679
  46.9 13.7 %all_to_all.11 = f32[128,1,128]{2,1,0:T(1,128)S(1)} all-to-all(f32[128,1,128]{2,1,0:T(1,128)S(1)} %broadcast_in_dim.22), channel_id=1, replica_groups=mesh['patch_0'=4,'patch_1'=4,'patch_2'=2,'grp'=4] {'patch_0','patch_1','..., dimensions={0} | all-to-all | bytes 131072 | tf_op jit(solution)/shard_map/all_to_all | solution.py:619
  60.6 1.4 %shard_map.79 = f32[21,16,256]{2,1,0:T(8,128)} custom-call(f32[128,128]{1,0:T(8,128)S(1)} %bitcast.12, f32[80,3,8,128]{3,2,1,0:T(8,128)S(1)} %get-tuple-element.58.next_ref, f32[80,3,8,128]{3,2,1,0:T(8,128)S(1)} %get-tuple-element.59.q0_ref, f32[80,3,8,128]{3,2,1,0:T(8,128)S(1)} %get-tuple-element.60.q1_ref, f32[80,3,8,128]{3,2,1,0:T(8,128)S(1)} %get-tuple-element.61.q2_ref, ...), custom_call_target="tpu_custom_call" | custom-call | tf_op jit(solution)/shard_map/pallas_call | solution.py:685
  (2 shorter events, 0.1 us)
Async XLA Ops:
  1.2 3.9 %collective-permute-start = (f32[136,128]{1,0:T(8,128)S(1)}, f32[136,128]{1,0:T(8,128)S(1)}, u32[]{:S(2)}, u32[]{:S(2)}) collective-permute-start(f32[136,128]{1,0:T(8,128)S(1)} %get-tuple-element.36), channel_id=1, source_target_pairs={{0,1},{1,0},{2,3},{3,2},{4,5},{5,4},{6,7},{7,6},{8,9},{9,8},{10,11... | collective-permute-start | bytes 208904 | tf_op jit(solution)/shard_map/ppermute | solution.py:614
  3.4 1.7 %collective-permute-start.1 = (f32[136,128]{1,0:T(8,128)S(1)}, f32[136,128]{1,0:T(8,128)S(1)}, u32[]{:S(2)}, u32[]{:S(2)}) collective-permute-start(f32[136,128]{1,0:T(8,128)S(1)} %get-tuple-element.37), channel_id=1, source_target_pairs={{0,0},{1,2},{2,1},{3,3},{4,4},{5,6},{6,5},{7,7},{8,8},{9,10},{10,9... | collective-permute-start | bytes 208904 | tf_op jit(solution)/shard_map/ppermute | solution.py:614
  5.2 7.7 %collective-permute-start.2 = (f32[640,128]{1,0:T(8,128)S(1)}, f32[640,128]{1,0:T(8,128)S(1)}, u32[]{:S(2)}, u32[]{:S(2)}) collective-permute-start(f32[640,128]{1,0:T(8,128)S(1)} %get-tuple-element.40), channel_id=1, source_target_pairs={{0,4},{4,0},{8,12},{12,8},{16,20},{20,16},{24,28},{28,24},{32,36},... | collective-permute-start | bytes 983048 | tf_op jit(solution)/shard_map/ppermute | solution.py:614
  7.2 8.4 %collective-permute-start.3 = (f32[640,128]{1,0:T(8,128)S(1)}, f32[640,128]{1,0:T(8,128)S(1)}, u32[]{:S(2)}, u32[]{:S(2)}) collective-permute-start(f32[640,128]{1,0:T(8,128)S(1)} %get-tuple-element.41), channel_id=1, source_target_pairs={{0,0},{4,8},{8,4},{12,16},{16,12},{20,24},{24,20},{28,32},{32,28},... | collective-permute-start | bytes 983048 | tf_op jit(solution)/shard_map/ppermute | solution.py:614

commit v5 on v4

--- a/solution.py
+++ b/solution.py
@@ -607,11 +607,21 @@
     return pltpu.with_memory_space_constraint(x, pltpu.HBM)
 
 
-def exchanged(x, axis, odd):
-    count = lax.axis_size(axis)
-    mates = [((i - odd) ^ 1) + odd for i in range(count)]
-    pairs = [(i, m if 0 <= m < count else i) for i, m in enumerate(mates)]
-    return lax.ppermute(x, axis, pairs)
+def exchanged(x, along_bands, odd):
+
+    def mate(owner, band):
+        at, count = (band, BANDS) if along_bands else (owner, OWNERS)
+        near = ((at - odd) ^ 1) + odd
+        if not 0 <= near < count:
+            return (owner ^ 1, band) if along_bands else (owner, band ^ 1)
+        return (owner, near) if along_bands else (near, band)
+
+    pairs = []
+    for owner in range(OWNERS):
+        for band in range(BANDS):
+            to_owner, to_band = mate(owner, band)
+            pairs.append((owner * BANDS + band, to_owner * BANDS + to_band))
+    return lax.ppermute(x, EVERY, pairs)
 
 
 def summed(gram):
@@ -631,14 +641,14 @@
         [far, far],
         [pltpu.SemaphoreType.DMA((6,))],
     )(in_hbm(pred), in_hbm(prev))
-    row1, row2 = (exchanged(x, "grp", odd) for odd, x in enumerate(strips))
+    row1, row2 = (exchanged(x, True, odd) for odd, x in enumerate(strips))
 
     message = shape((dense(COL_TILES), LANES), f32)
     messages = call(pack_kernel, (message, message), [vm()] * 4)(pred, prev, row1, row2)
     inputs = (new_owner, levels, diffusion, decay, reaction)
     messages, inputs = lax.optimization_barrier((tuple(messages), inputs))
     new_owner, levels, diffusion, decay, reaction = inputs
-    col1, col2 = (exchanged(x, PATCH, odd) for odd, x in enumerate(messages))
+    col1, col2 = (exchanged(x, False, odd) for odd, x in enumerate(messages))
     faces, stencil, flags, params, blocks = call(
         table_kernel,
         (

time: 62.2 us -> 58.5 us (0.941)
  blocking collectives: 38.9 us -> 36.7 us
  starting transfers between devices: 8.36 us -> 6.67 us
    all_to_all x2, blocking collectives: 38.9 us -> 36.7 us  [summed(): return lax.all_to_all(spread_out, EVERY, 0, 0).reshape(DEVICES, LANES)]
    ppermute x4, starting transfers between devices: 8.36 us -> 6.67 us  [exchanged(): return lax.ppermute(x, EVERY, pairs)]
  transfers between devices with their start and end apart: 4 -> 4, of which waited for: 2 -> 3; matrix products, arithmetic and copies ran while one was open for 0% -> 0% of each run, Pallas kernels for 4% -> 4%
where the time goes in v5:
time: 58.5 us; the launch traced here: 58.2 us
  blocking collectives  36.7 us (63%)
  Pallas kernels  10.8 us (18%)
  starting transfers between devices  6.67 us (11%)
  waiting for transfers between devices  3.78 us (6%)
    all_to_all x2, blocking collectives, summed(): return lax.all_to_all(spread_out, EVERY, 0, 0).reshape(DEVICES, LANES)  36.7 us
    ppermute x4, starting transfers between devices, exchanged(): return lax.ppermute(x, EVERY, pairs)  6.67 us
    ppermute x4, waiting for transfers between devices, exchanged(): return lax.ppermute(x, EVERY, pairs)  3.78 us
    pallas_call x1, Pallas kernels, per_device(): call(first_kernel, (state,) * 5 + (gram,), [vm()] * 7, [pltpu.VMEM(STATE,...  3.27 us
    pallas_call x1, Pallas kernels, per_device(): call(second_kernel, (state,) * 4 + (gram,), [vm()] * 10, [pltpu.VMEM(STAT...  2.74 us
    pallas_call x1, Pallas kernels, per_device(): call(table_kernel, (shape((6, 4, 8, LANES), f32), shape((6, 2 * LANES, LA...  1.88 us
    pallas_call x1, Pallas kernels, per_device(): call(last_kernel, shape((SPECIES, SLOTS, 2 * LANES), f32), [vm()] * 6, [p...  1.37 us
  transfers between devices with their start and end apart: 4, of which 3 were waited for; matrix products, arithmetic and copies ran while one was open for 0% of the time, Pallas kernels for 4%

profile of v5, /device:TPU:1, one launch (start us, length us, event | category | flops | bytes accessed | tf_op | source)
XLA Modules:
  0.0 58.2 jit_solution(10511690243216275807)
XLA Ops:
  0.0 1.1 %shard_map.73 = (f32[512,128]{1,0:T(8,128)S(1)}, f32[512,128]{1,0:T(8,128)S(1)}, f32[136,128]{1,0:T(8,128)S(1)}, f32[136,128]{1,0:T(8,128)S(1)}) custom-call(f32[504,128]{1,0:T(8,128)} %bitcast.15, f32[504,128]{1,0:T(8,128)} %bitcast.16), custom_call_target="tpu_custom_call" | custom-call | tf_op jit(solution)/shard_map/pallas_call | solution.py:638
  1.2 2.2 %collective-permute-start = (f32[136,128]{1,0:T(8,128)S(1)}, f32[136,128]{1,0:T(8,128)S(1)}, u32[]{:S(2)}, u32[]{:S(2)}) collective-permute-start(f32[136,128]{1,0:T(8,128)S(1)} %get-tuple-element.36), channel_id=1, source_target_pairs={{0,1},{1,0},{2,3},{3,2},{4,5},{5,4},{6,7},{7,6},{8,9},{9,8},{10,11... | collective-permute-start | bytes 208904 | tf_op jit(solution)/shard_map/ppermute | solution.py:624
  3.4 1.0 %collective-permute-start.1 = (f32[136,128]{1,0:T(8,128)S(1)}, f32[136,128]{1,0:T(8,128)S(1)}, u32[]{:S(2)}, u32[]{:S(2)}) collective-permute-start(f32[136,128]{1,0:T(8,128)S(1)} %get-tuple-element.37), channel_id=1, source_target_pairs={{0,4},{1,2},{2,1},{3,7},{4,0},{5,6},{6,5},{7,3},{8,12},{9,10},{10,... | collective-permute-start | bytes 208904 | tf_op jit(solution)/shard_map/ppermute | solution.py:624
  4.3 0.7 %collective-permute-done.row1_ref = f32[136,128]{1,0:T(8,128)S(1)} collective-permute-done((f32[136,128]{1,0:T(8,128)S(1)}, f32[136,128]{1,0:T(8,128)S(1)}, u32[]{:S(2)}, u32[]{:S(2)}) %collective-permute-start) | collective-permute-done | bytes 69664 | tf_op jit(solution)/shard_map/ppermute | solution.py:624
  5.1 0.2 collective-permute-done.1.row2_ref
  5.2 0.2 shard_map.75
  5.4 1.8 %collective-permute-start.2 = (f32[640,128]{1,0:T(8,128)S(1)}, f32[640,128]{1,0:T(8,128)S(1)}, u32[]{:S(2)}, u32[]{:S(2)}) collective-permute-start(f32[640,128]{1,0:T(8,128)S(1)} %get-tuple-element.40), channel_id=1, source_target_pairs={{0,4},{1,5},{2,6},{3,7},{4,0},{5,1},{6,2},{7,3},{8,12},{9,13},{10,... | collective-permute-start | bytes 983048 | tf_op jit(solution)/shard_map/ppermute | solution.py:624
  7.2 1.7 %collective-permute-start.3 = (f32[640,128]{1,0:T(8,128)S(1)}, f32[640,128]{1,0:T(8,128)S(1)}, u32[]{:S(2)}, u32[]{:S(2)}) collective-permute-start(f32[640,128]{1,0:T(8,128)S(1)} %get-tuple-element.41), channel_id=1, source_target_pairs={{0,1},{1,0},{2,3},{3,2},{4,8},{5,9},{6,10},{7,11},{8,4},{9,5},{10,... | collective-permute-start | bytes 983048 | tf_op jit(solution)/shard_map/ppermute | solution.py:624
  8.9 1.9 %shard_map.76 = (f32[6,4,8,128]{3,2,1,0:T(8,128)S(1)}, bf16[6,256,128]{2,1,0:T(8,128)(2,1)S(1)}, s32[26,8,128]{2,1,0:T(8,128)S(1)}, f32[3,3,8,128]{3,2,1,0:T(8,128)S(1)}, bf16[48,256]{1,0:T(8,128)(2,1)S(1)}) custom-call(s32[12,4,32]{2,1,0:T(4,128)} %bitcast.17, s32[12,4,32]{2,1,0:T(4,128)} %bitcast.18, f32[21]{0:T(128)} %diffusion_ref, f32[21]{0:T(128)} %decay_ref, ...), custom_call_target="tpu_custom_call" | custom-call | tf_op jit(solution)/shard_map/pallas_call | solution.py:652
  10.8 0.3 shard_map.74.own_ref
  11.1 0.0 collective-permute-done.2.col1_ref
  11.1 2.9 %collective-permute-done.3.col2_ref = f32[640,128]{1,0:T(8,128)S(1)} collective-permute-done((f32[640,128]{1,0:T(8,128)S(1)}, f32[640,128]{1,0:T(8,128)S(1)}, u32[]{:S(2)}, u32[]{:S(2)}) %collective-permute-start.3) | collective-permute-done | bytes 327712 | tf_op jit(solution)/shard_map/ppermute | solution.py:624
  14.0 3.3 %shard_map.77 = (f32[80,3,8,128]{3,2,1,0:T(8,128)S(1)}, f32[80,3,8,128]{3,2,1,0:T(8,128)S(1)}, f32[80,3,8,128]{3,2,1,0:T(8,128)S(1)}, f32[80,3,8,128]{3,2,1,0:T(...) custom-call(f32[2,80,3,8,128]{4,3,2,1,0:T(8,128)S(1)} %shard_map.74.own_ref, ...), custom_call_target="tpu_custom_call" | custom-call | tf_op jit(solution)/shard_map/pallas_call | solution.py:683
  17.3 23.0 %all_to_all.10 = f32[128,1,128]{2,1,0:T(1,128)S(1)} all-to-all(f32[128,1,128]{2,1,0:T(1,128)S(1)} %broadcast_in_dim.20), channel_id=1, replica_groups=mesh['patch_0'=4,'patch_1'=4,'patch_2'=2,'grp'=4] {'patch_0','patch_1','..., dimensions={0} | all-to-all | bytes 131072 | tf_op jit(solution)/shard_map/all_to_all | solution.py:629
  40.3 2.7 %shard_map.78 = (f32[80,3,8,128]{3,2,1,0:T(8,128)S(1)}, f32[80,3,8,128]{3,2,1,0:T(8,128)S(1)}, f32[80,3,8,128]{3,2,1,0:T(8,128)S(1)}, f32[80,3,8,128]{3,2,1,0:T(8,128)S(1)}, f32[1,128]{1,0:T(1,128)S(1)}) custom-call(f32[128,128]{1,0:T(8,128)S(1)} %bitcast.11, f32[80,3,8,128]{3,2,1,0:T(8,128)S(1)} %get-tuple-element.52.state_ref, ...), custom_call_target="tpu_custom_call" | custom-call | tf_op jit(solution)/shard_map/pallas_call | solution.py:689
  43.1 13.7 %all_to_all.11 = f32[128,1,128]{2,1,0:T(1,128)S(1)} all-to-all(f32[128,1,128]{2,1,0:T(1,128)S(1)} %broadcast_in_dim.22), channel_id=1, replica_groups=mesh['patch_0'=4,'patch_1'=4,'patch_2'=2,'grp'=4] {'patch_0','patch_1','..., dimensions={0} | all-to-all | bytes 131072 | tf_op jit(solution)/shard_map/all_to_all | solution.py:629
  56.8 1.4 %shard_map.79 = f32[21,16,256]{2,1,0:T(8,128)} custom-call(f32[128,128]{1,0:T(8,128)S(1)} %bitcast.12, f32[80,3,8,128]{3,2,1,0:T(8,128)S(1)} %get-tuple-element.58.next_ref, f32[80,3,8,128]{3,2,1,0:T(8,128)S(1)} %get-tuple-element.59.q0_ref, f32[80,3,8,128]{3,2,1,0:T(8,128)S(1)} %get-tuple-element.60.q1_ref, f32[80,3,8,128]{3,2,1,0:T(8,128)S(1)} %get-tuple-element.61.q2_ref, ...), custom_call_target="tpu_custom_call" | custom-call | tf_op jit(solution)/shard_map/pallas_call | solution.py:695
  (2 shorter events, 0.1 us)
Async XLA Ops:
  1.2 3.9 %collective-permute-start = (f32[136,128]{1,0:T(8,128)S(1)}, f32[136,128]{1,0:T(8,128)S(1)}, u32[]{:S(2)}, u32[]{:S(2)}) collective-permute-start(f32[136,128]{1,0:T(8,128)S(1)} %get-tuple-element.36), channel_id=1, source_target_pairs={{0,1},{1,0},{2,3},{3,2},{4,5},{5,4},{6,7},{7,6},{8,9},{9,8},{10,11... | collective-permute-start | bytes 208904 | tf_op jit(solution)/shard_map/ppermute | solution.py:624
  3.4 1.9 %collective-permute-start.1 = (f32[136,128]{1,0:T(8,128)S(1)}, f32[136,128]{1,0:T(8,128)S(1)}, u32[]{:S(2)}, u32[]{:S(2)}) collective-permute-start(f32[136,128]{1,0:T(8,128)S(1)} %get-tuple-element.37), channel_id=1, source_target_pairs={{0,4},{1,2},{2,1},{3,7},{4,0},{5,6},{6,5},{7,3},{8,12},{9,10},{10,... | collective-permute-start | bytes 208904 | tf_op jit(solution)/shard_map/ppermute | solution.py:624
  5.4 5.7 %collective-permute-start.2 = (f32[640,128]{1,0:T(8,128)S(1)}, f32[640,128]{1,0:T(8,128)S(1)}, u32[]{:S(2)}, u32[]{:S(2)}) collective-permute-start(f32[640,128]{1,0:T(8,128)S(1)} %get-tuple-element.40), channel_id=1, source_target_pairs={{0,4},{1,5},{2,6},{3,7},{4,0},{5,1},{6,2},{7,3},{8,12},{9,13},{10,... | collective-permute-start | bytes 983048 | tf_op jit(solution)/shard_map/ppermute | solution.py:624
  7.2 6.8 %collective-permute-start.3 = (f32[640,128]{1,0:T(8,128)S(1)}, f32[640,128]{1,0:T(8,128)S(1)}, u32[]{:S(2)}, u32[]{:S(2)}) collective-permute-start(f32[640,128]{1,0:T(8,128)S(1)} %get-tuple-element.41), channel_id=1, source_target_pairs={{0,1},{1,0},{2,3},{3,2},{4,8},{5,9},{6,10},{7,11},{8,4},{9,5},{10,... | collective-permute-start | bytes 983048 | tf_op jit(solution)/shard_map/ppermute | solution.py:624

commit v6 on v5

--- a/solution.py
+++ b/solution.py
@@ -21,7 +21,7 @@
 OWN_LO, OWN_HI = 8, 72
 LANES = 128
 TILES = 10
-MSG = TILES + TILES // 2
+INNER, CORNER = 12, 3
 
 SIGMA = 32.0
 THETA = 14.0
@@ -168,7 +168,6 @@
 
 
 ROW_TILES = 2 * COLS_DEV
-COL_TILES = 2 * MSG
 
 
 def dense(tiles):
@@ -193,7 +192,20 @@
 EDGE = 128
 
 
-def row_strip_kernel(pred_hbm, prev_hbm, pred_ref, prev_ref, first_ref, second_ref, sems):
+def packed_pair(low, high):
+    odd = (lax.broadcasted_iota(jnp.int32, (SPECIES, LANES), 1) // 8) % 2 == 1
+    return lambda: jnp.where(odd, high, roll(low, -8)), lambda: jnp.where(odd, roll(high, 8), low)
+
+
+def put_columns(first_ref, second_ref, at, right, left):
+    _, owner = position()
+    put_tile(first_ref, at, jnp.where(owner % 2 == 0, right, left))
+    put_tile(second_ref, at, jnp.where(owner % 2 == 0, left, right))
+
+
+def strip_kernel(
+    pred_hbm, prev_hbm, pred_ref, prev_ref, first_ref, second_ref, inner1_ref, inner2_ref, sems
+):
     band, _ = position()
     even = band % 2 == 0
     top = INPUT_ROWS - EDGE
@@ -223,8 +235,24 @@
             put_tile(second_ref, which * COLS_DEV + c, jnp.where(even, down, up))
     finish(first_ref, ROW_TILES)
     finish(second_ref, ROW_TILES)
-    copies[0][2].wait()
-    copies[1][2].wait()
+    for which, (_, patch_ref) in enumerate(pairs):
+        copies[which][2].wait()
+        for half in range(2 * ROWS_DEV):
+            slot = half // 2 * COLS_DEV
+            put_columns(
+                inner1_ref,
+                inner2_ref,
+                which * INNER + half,
+                half_tile(patch_ref, slot + 2, half % 2),
+                half_tile(patch_ref, slot, half % 2),
+            )
+        for r in range(ROWS_DEV):
+            slot = r * COLS_DEV + 1
+            east, west = packed_pair(half_tile(patch_ref, slot, 0), half_tile(patch_ref, slot, 1))
+            at = which * INNER + 2 * ROWS_DEV + r
+            put_columns(inner1_ref, inner2_ref, at, east(), west())
+    finish(inner1_ref, 2 * INNER)
+    finish(inner2_ref, 2 * INNER)
 
 
 def tile_of(patch_ref, rows_ref, which, k, c):
@@ -239,30 +267,18 @@
     return half_tile(patch_ref, ((k - 1) // 2) * COLS_DEV + c, (k - 1) % 2)
 
 
-def pack_kernel(pred_ref, prev_ref, row1_ref, row2_ref, first_ref, second_ref):
-    odd = (lax.broadcasted_iota(jnp.int32, (SPECIES, LANES), 1) // 8) % 2 == 1
-    _, owner = position()
-    even_owner = owner % 2 == 0
-    for which, patch_ref in enumerate((pred_ref, prev_ref)):
-
-        def put(at, right, left, which=which):
-            put_tile(first_ref, which * MSG + at, jnp.where(even_owner, right, left))
-            put_tile(second_ref, which * MSG + at, jnp.where(even_owner, left, right))
-
-        def tile(k, c, which=which, patch_ref=patch_ref):
-            return tile_of(patch_ref, (row1_ref, row2_ref), which, k, c)
-
-        for k in range(TILES):
-            put(k, tile(k, 2), tile(k, 0))
-        for pair in range(TILES // 2):
-            low, high = tile(2 * pair, 1), tile(2 * pair + 1, 1)
-            put(
-                TILES + pair,
-                jnp.where(odd, high, roll(low, -8)),
-                jnp.where(odd, roll(high, 8), low),
-            )
-    finish(first_ref, COL_TILES)
-    finish(second_ref, COL_TILES)
+def corner_kernel(row1_ref, row2_ref, first_ref, second_ref):
+    for which in range(2):
+
+        def tile(k, c, which=which):
+            return tile_of(None, (row1_ref, row2_ref), which, k, c)
+
+        for at, k in enumerate((0, TILES - 1)):
+            put_columns(first_ref, second_ref, which * CORNER + at, tile(k, 2), tile(k, 0))
+        east, west = packed_pair(tile(0, 1), tile(TILES - 1, 1))
+        put_columns(first_ref, second_ref, which * CORNER + 2, east(), west())
+    finish(first_ref, 2 * CORNER)
+    finish(second_ref, 2 * CORNER)
 
 
 def own_kernel(pred_ref, prev_ref, row1_ref, row2_ref, own_ref, tile_ref):
@@ -401,7 +417,7 @@
 
 
 def first_kernel(
-    own_ref, col1_ref, col2_ref, face_ref, stencil_ref, param_ref, block_ref,
+    own_ref, inner1_ref, inner2_ref, corner1_ref, corner2_ref, face_ref, stencil_ref, param_ref, block_ref,
     state_ref, p0_ref, p1_ref, p2_ref, p3_ref, gram_ref, old_ref, diag_ref, packed_ref,
 ):
     _, owner = position()
@@ -409,26 +425,29 @@
     blank = jnp.zeros((3, 8, LANES), f32)
     for which, target in enumerate((state_ref, old_ref)):
 
-        def beside(at, which=which):
-            first, second = (
-                get_tile(ref, which * MSG + at).reshape(3, 8, LANES) for ref in (col1_ref, col2_ref)
-            )
+        def beside(refs, at):
+            first, second = (get_tile(ref, at).reshape(3, 8, LANES) for ref in refs)
             left, right = jnp.where(even_owner, second, first), jnp.where(even_owner, first, second)
             return jnp.where(has_left, left, 0.0), jnp.where(has_right, right, 0.0)
 
         for k in range(TILES):
-            if k % 2 == 0:
-                far_left, far_right = beside(TILES + k // 2)
-            left, right = beside(k)
+            if k in (0, TILES - 1):
+                refs, at = (corner1_ref, corner2_ref), which * CORNER + (k > 0)
+                pair, high = which * CORNER + 2, k > 0
+            else:
+                refs, at = (inner1_ref, inner2_ref), which * INNER + k - 1
+                pair, high = which * INNER + 2 * ROWS_DEV + (k - 1) // 2, k % 2 == 0
+            left, right = beside(refs, at)
+            far_left, far_right = beside(refs, pair)
             tiles = mix_blocks(
                 [
-                    far_left if k % 2 else roll(far_left, 8),
+                    far_left if high else roll(far_left, 8),
                     roll(left, 16),
                     blank,
                     blank,
                     blank,
                     roll(right, 80),
-                    roll(far_right, 88 if k % 2 else 96),
+                    roll(far_right, 88 if high else 96),
                     blank,
                 ]
             )
@@ -624,6 +643,13 @@
     return lax.ppermute(x, EVERY, pairs)
 
 
+def swapped(pair, along_bands):
+    out = []
+    for odd, x in enumerate(pair):
+        out.append(exchanged(x, along_bands, odd))
+    return out
+
+
 def summed(gram):
     spread_out = jnp.broadcast_to(gram[None], (DEVICES, 1, LANES))
     return lax.all_to_all(spread_out, EVERY, 0, 0).reshape(DEVICES, LANES)
@@ -635,20 +661,21 @@
     strip = shape((dense(ROW_TILES), LANES), f32)
     local = shape((INPUT_ROWS + 8, LANES), f32)
     far = pl.BlockSpec(memory_space=pltpu.HBM)
+    inner, corner = (shape((dense(2 * count), LANES), f32) for count in (INNER, CORNER))
     pred, prev, *strips = call(
-        row_strip_kernel,
-        (local, local, strip, strip),
+        strip_kernel,
+        (local, local, strip, strip, inner, inner),
         [far, far],
         [pltpu.SemaphoreType.DMA((6,))],
     )(in_hbm(pred), in_hbm(prev))
-    row1, row2 = (exchanged(x, True, odd) for odd, x in enumerate(strips))
-
-    message = shape((dense(COL_TILES), LANES), f32)
-    messages = call(pack_kernel, (message, message), [vm()] * 4)(pred, prev, row1, row2)
+    row1, row2 = swapped(strips[:2], True)
+    inner_cols = swapped(strips[2:], False)
+    corners = call(corner_kernel, (corner, corner), [vm()] * 2)(row1, row2)
+
     inputs = (new_owner, levels, diffusion, decay, reaction)
-    messages, inputs = lax.optimization_barrier((tuple(messages), inputs))
+    corners, inputs = lax.optimization_barrier((tuple(corners), inputs))
     new_owner, levels, diffusion, decay, reaction = inputs
-    col1, col2 = (exchanged(x, False, odd) for odd, x in enumerate(messages))
+    corner_cols = swapped(corners, False)
     faces, stencil, flags, params, blocks = call(
         table_kernel,
         (
@@ -683,9 +710,9 @@
     u0, p0, p1, p2, p3, gram1 = call(
         first_kernel,
         (state,) * 5 + (gram,),
-        [vm()] * 7,
+        [vm()] * 9,
         [pltpu.VMEM(STATE, f32), pltpu.VMEM(STATE, f32), pltpu.VMEM(PACKED, f32)],
-    )(own, col1, col2, faces, stencil, params, blocks)
+    )(own, *inner_cols, *corner_cols, faces, stencil, params, blocks)
     u1, q0, q1, q2, gram2 = call(
         second_kernel,
         (state,) * 4 + (gram,),

time: 58.5 us -> 56.6 us (0.968)
  blocking collectives: 36.7 us -> 33.8 us
  waiting for transfers between devices: 3.78 us -> 4.72 us
    all_to_all x2, blocking collectives: 36.7 us -> 33.8 us  [summed(): return lax.all_to_all(spread_out, EVERY, 0, 0).reshape(DEVICES, LANES)]
    ppermute x4 -> x6, waiting for transfers between devices: 3.78 us -> 4.72 us  [exchanged(): return lax.ppermute(x, EVERY, pairs)]
    ppermute x4 -> x6, starting transfers between devices: 6.67 us -> 6.6 us  [exchanged(): return lax.ppermute(x, EVERY, pairs)]
  transfers between devices with their start and end apart: 4 -> 6, of which waited for: 3 -> 2; matrix products, arithmetic and copies ran while one was open for 0% -> 0% of each run, Pallas kernels for 4% -> 4%
where the time goes in v6:
time: 56.6 us; the launch traced here: 56.3 us
  blocking collectives  33.8 us (60%)
  Pallas kernels  11.1 us (20%)
  starting transfers between devices  6.6 us (12%)
  waiting for transfers between devices  4.72 us (8%)
    all_to_all x2, blocking collectives, summed(): return lax.all_to_all(spread_out, EVERY, 0, 0).reshape(DEVICES, LANES)  33.8 us
    ppermute x6, starting transfers between devices, exchanged(): return lax.ppermute(x, EVERY, pairs)  6.6 us
    ppermute x6, waiting for transfers between devices, exchanged(): return lax.ppermute(x, EVERY, pairs)  4.72 us
    pallas_call x1, Pallas kernels, per_device(): call(first_kernel, (state,) * 5 + (gram,), [vm()] * 9, [pltpu.VMEM(STATE,...  3.44 us
    pallas_call x1, Pallas kernels, per_device(): call(second_kernel, (state,) * 4 + (gram,), [vm()] * 10, [pltpu.VMEM(STAT...  2.75 us
    pallas_call x1, Pallas kernels, per_device(): call(table_kernel, (shape((6, 4, 8, LANES), f32), shape((6, 2 * LANES, LA...  1.88 us
    pallas_call x1, Pallas kernels, per_device(): call(last_kernel, shape((SPECIES, SLOTS, 2 * LANES), f32), [vm()] * 6, [p...  1.37 us
    pallas_call x1, Pallas kernels, per_device(): call(strip_kernel, (local, local, strip, strip, inner, inner), [far, far]...  1.29 us
  transfers between devices with their start and end apart: 6, of which 2 were waited for; matrix products, arithmetic and copies ran while one was open for 0% of the time, Pallas kernels for 4%

profile of v6, /device:TPU:1, one launch (start us, length us, event | category | flops | bytes accessed | tf_op | source)
XLA Modules:
  0.0 56.3 jit_solution(13905784768566345870)
XLA Ops:
  0.0 1.3 %shard_map.73 = (f32[512,128]{1,0:T(8,128)S(1)}, f32[512,128]{1,0:T(8,128)S(1)}, f32[136,128]{1,0:T(8,128)S(1)}, f32[136,128]{1,0:T(8,128)S(1)}, f32[512,128]{1,0:T(8,128)S(1)}, /*index=5*/f32[512,128]{1,0:T(8,128)S(1)}) custom-call(f32[504,128]{1,0:T(8,128)} %bitcast.15, f32[504,128]{1,0:T(8,128)} %bitcast.16), custom_call_target="tpu_custom_call" | custom-call | tf_op jit(solution)/shard_map/pallas_call | solution.py:665
  1.3 1.5 %collective-permute-start.2 = (f32[512,128]{1,0:T(8,128)S(1)}, f32[512,128]{1,0:T(8,128)S(1)}, u32[]{:S(2)}, u32[]{:S(2)}) collective-permute-start(f32[512,128]{1,0:T(8,128)S(1)} %get-tuple-element.40), channel_id=1, source_target_pairs={{0,4},{1,5},{2,6},{3,7},{4,0},{5,1},{6,2},{7,3},{8,12},{9,13},{10,... | collective-permute-start | bytes 786440 | tf_op jit(solution)/shard_map/ppermute | solution.py:643
  2.8 1.7 %collective-permute-start.3 = (f32[512,128]{1,0:T(8,128)S(1)}, f32[512,128]{1,0:T(8,128)S(1)}, u32[]{:S(2)}, u32[]{:S(2)}) collective-permute-start(f32[512,128]{1,0:T(8,128)S(1)} %get-tuple-element.41), channel_id=1, source_target_pairs={{0,1},{1,0},{2,3},{3,2},{4,8},{5,9},{6,10},{7,11},{8,4},{9,5},{10,... | collective-permute-start | bytes 786440 | tf_op jit(solution)/shard_map/ppermute | solution.py:643
  4.5 1.3 %collective-permute-start = (f32[136,128]{1,0:T(8,128)S(1)}, f32[136,128]{1,0:T(8,128)S(1)}, u32[]{:S(2)}, u32[]{:S(2)}) collective-permute-start(f32[136,128]{1,0:T(8,128)S(1)} %get-tuple-element.38), channel_id=1, source_target_pairs={{0,1},{1,0},{2,3},{3,2},{4,5},{5,4},{6,7},{7,6},{8,9},{9,8},{10,11... | collective-permute-start | bytes 208904 | tf_op jit(solution)/shard_map/ppermute | solution.py:643
  5.8 0.0 collective-permute-start.1
  5.8 2.9 %collective-permute-done.row1_ref = f32[136,128]{1,0:T(8,128)S(1)} collective-permute-done((f32[136,128]{1,0:T(8,128)S(1)}, f32[136,128]{1,0:T(8,128)S(1)}, u32[]{:S(2)}, u32[]{:S(2)}) %collective-permute-start) | collective-permute-done | bytes 69664 | tf_op jit(solution)/shard_map/ppermute | solution.py:643
  8.7 0.0 collective-permute-done.1.row2_ref
  8.7 0.1 shard_map.75
  8.8 2.1 %collective-permute-start.4 = (f32[136,128]{1,0:T(8,128)S(1)}, f32[136,128]{1,0:T(8,128)S(1)}, u32[]{:S(2)}, u32[]{:S(2)}) collective-permute-start(f32[136,128]{1,0:T(8,128)S(1)} %get-tuple-element.44), channel_id=1, source_target_pairs={{0,4},{1,5},{2,6},{3,7},{4,0},{5,1},{6,2},{7,3},{8,12},{9,13},{10,... | collective-permute-start | bytes 208904 | tf_op jit(solution)/shard_map/ppermute | solution.py:643
  10.9 0.0 collective-permute-start.5
  10.9 1.9 %shard_map.76 = (f32[6,4,8,128]{3,2,1,0:T(8,128)S(1)}, bf16[6,256,128]{2,1,0:T(8,128)(2,1)S(1)}, s32[26,8,128]{2,1,0:T(8,128)S(1)}, f32[3,3,8,128]{3,2,1,0:T(8,128)S(1)}, bf16[48,256]{1,0:T(8,128)(2,1)S(1)}) custom-call(s32[12,4,32]{2,1,0:T(4,128)} %bitcast.17, s32[12,4,32]{2,1,0:T(4,128)} %bitcast.18, f32[21]{0:T(128)} %diffusion_ref, f32[21]{0:T(128)} %decay_ref, ...), custom_call_target="tpu_custom_call" | custom-call | tf_op jit(solution)/shard_map/pallas_call | solution.py:679
  12.8 0.3 shard_map.74.own_ref
  13.1 0.0 collective-permute-done.4.corner1_ref
  13.1 1.8 %collective-permute-done.5.corner2_ref = f32[136,128]{1,0:T(8,128)S(1)} collective-permute-done((f32[136,128]{1,0:T(8,128)S(1)}, f32[136,128]{1,0:T(8,128)S(1)}, u32[]{:S(2)}, u32[]{:S(2)}) %collective-permute-start.5) | collective-permute-done | bytes 69664 | tf_op jit(solution)/shard_map/ppermute | solution.py:643
  14.9 0.0 collective-permute-done.2.inner1_ref
  14.9 0.0 collective-permute-done.3.inner2_ref
  14.9 3.4 %shard_map.77 = (f32[80,3,8,128]{3,2,1,0:T(8,128)S(1)}, f32[80,3,8,128]{3,2,1,0:T(8,128)S(1)}, f32[80,3,8,128]{3,2,1,0:T(8,128)S(1)}, f32[80,3,8,128]{3,2,1,0:T(...) custom-call(f32[2,80,3,8,128]{4,3,2,1,0:T(8,128)S(1)} %shard_map.74.own_ref, ...), custom_call_target="tpu_custom_call" | custom-call | tf_op jit(solution)/shard_map/pallas_call | solution.py:710
  18.4 20.1 %all_to_all.10 = f32[128,1,128]{2,1,0:T(1,128)S(1)} all-to-all(f32[128,1,128]{2,1,0:T(1,128)S(1)} %broadcast_in_dim.20), channel_id=1, replica_groups=mesh['patch_0'=4,'patch_1'=4,'patch_2'=2,'grp'=4] {'patch_0','patch_1','..., dimensions={0} | all-to-all | bytes 131072 | tf_op jit(solution)/shard_map/all_to_all | solution.py:655
  38.5 2.8 %shard_map.78 = (f32[80,3,8,128]{3,2,1,0:T(8,128)S(1)}, f32[80,3,8,128]{3,2,1,0:T(8,128)S(1)}, f32[80,3,8,128]{3,2,1,0:T(8,128)S(1)}, f32[80,3,8,128]{3,2,1,0:T(8,128)S(1)}, f32[1,128]{1,0:T(1,128)S(1)}) custom-call(f32[128,128]{1,0:T(8,128)S(1)} %bitcast.11, f32[80,3,8,128]{3,2,1,0:T(8,128)S(1)} %get-tuple-element.56.state_ref, ...), custom_call_target="tpu_custom_call" | custom-call | tf_op jit(solution)/shard_map/pallas_call | solution.py:716
  41.3 13.7 %all_to_all.11 = f32[128,1,128]{2,1,0:T(1,128)S(1)} all-to-all(f32[128,1,128]{2,1,0:T(1,128)S(1)} %broadcast_in_dim.22), channel_id=1, replica_groups=mesh['patch_0'=4,'patch_1'=4,'patch_2'=2,'grp'=4] {'patch_0','patch_1','..., dimensions={0} | all-to-all | bytes 131072 | tf_op jit(solution)/shard_map/all_to_all | solution.py:655
  55.0 1.4 %shard_map.79 = f32[21,16,256]{2,1,0:T(8,128)} custom-call(f32[128,128]{1,0:T(8,128)S(1)} %bitcast.12, f32[80,3,8,128]{3,2,1,0:T(8,128)S(1)} %get-tuple-element.62.next_ref, f32[80,3,8,128]{3,2,1,0:T(8,128)S(1)} %get-tuple-element.63.q0_ref, f32[80,3,8,128]{3,2,1,0:T(8,128)S(1)} %get-tuple-element.64.q1_ref, f32[80,3,8,128]{3,2,1,0:T(8,128)S(1)} %get-tuple-element.65.q2_ref, ...), custom_call_target="tpu_custom_call" | custom-call | tf_op jit(solution)/shard_map/pallas_call | solution.py:722
  (2 shorter events, 0.1 us)
Async XLA Ops:
  1.3 13.6 %collective-permute-start.2 = (f32[512,128]{1,0:T(8,128)S(1)}, f32[512,128]{1,0:T(8,128)S(1)}, u32[]{:S(2)}, u32[]{:S(2)}) collective-permute-start(f32[512,128]{1,0:T(8,128)S(1)} %get-tuple-element.40), channel_id=1, source_target_pairs={{0,4},{1,5},{2,6},{3,7},{4,0},{5,1},{6,2},{7,3},{8,12},{9,13},{10,... | collective-permute-start | bytes 786440 | tf_op jit(solution)/shard_map/ppermute | solution.py:643
  2.8 12.2 %collective-permute-start.3 = (f32[512,128]{1,0:T(8,128)S(1)}, f32[512,128]{1,0:T(8,128)S(1)}, u32[]{:S(2)}, u32[]{:S(2)}) collective-permute-start(f32[512,128]{1,0:T(8,128)S(1)} %get-tuple-element.41), channel_id=1, source_target_pairs={{0,1},{1,0},{2,3},{3,2},{4,8},{5,9},{6,10},{7,11},{8,4},{9,5},{10,... | collective-permute-start | bytes 786440 | tf_op jit(solution)/shard_map/ppermute | solution.py:643
  4.5 4.2 %collective-permute-start = (f32[136,128]{1,0:T(8,128)S(1)}, f32[136,128]{1,0:T(8,128)S(1)}, u32[]{:S(2)}, u32[]{:S(2)}) collective-permute-start(f32[136,128]{1,0:T(8,128)S(1)} %get-tuple-element.38), channel_id=1, source_target_pairs={{0,1},{1,0},{2,3},{3,2},{4,5},{5,4},{6,7},{7,6},{8,9},{9,8},{10,11... | collective-permute-start | bytes 208904 | tf_op jit(solution)/shard_map/ppermute | solution.py:643
  5.8 2.9 %collective-permute-start.1 = (f32[136,128]{1,0:T(8,128)S(1)}, f32[136,128]{1,0:T(8,128)S(1)}, u32[]{:S(2)}, u32[]{:S(2)}) collective-permute-start(f32[136,128]{1,0:T(8,128)S(1)} %get-tuple-element.39), channel_id=1, source_target_pairs={{0,4},{1,2},{2,1},{3,7},{4,0},{5,6},{6,5},{7,3},{8,12},{9,10},{10,... | collective-permute-start | bytes 208904 | tf_op jit(solution)/shard_map/ppermute | solution.py:643
  8.8 4.3 %collective-permute-start.4 = (f32[136,128]{1,0:T(8,128)S(1)}, f32[136,128]{1,0:T(8,128)S(1)}, u32[]{:S(2)}, u32[]{:S(2)}) collective-permute-start(f32[136,128]{1,0:T(8,128)S(1)} %get-tuple-element.44), channel_id=1, source_target_pairs={{0,4},{1,5},{2,6},{3,7},{4,0},{5,1},{6,2},{7,3},{8,12},{9,13},{10,... | collective-permute-start | bytes 208904 | tf_op jit(solution)/shard_map/ppermute | solution.py:643
  10.9 4.0 %collective-permute-start.5 = (f32[136,128]{1,0:T(8,128)S(1)}, f32[136,128]{1,0:T(8,128)S(1)}, u32[]{:S(2)}, u32[]{:S(2)}) collective-permute-start(f32[136,128]{1,0:T(8,128)S(1)} %get-tuple-element.45), channel_id=1, source_target_pairs={{0,1},{1,0},{2,3},{3,2},{4,8},{5,9},{6,10},{7,11},{8,4},{9,5},{10,... | collective-permute-start | bytes 208904 | tf_op jit(solution)/shard_map/ppermute | solution.py:643
